TPU v7x, 32 devices: a whole 2x2x4 slice. The times are simulated.
32 devices in a mesh: fsdp: 8 (over z, x), tp: 4 (over y, core).
Axes of the slice: x: 2, y: 2, z: 4, core: 2. Of those that a mesh axis runs over, the one named last changes fastest.
Arguments:
- block_input: bfloat16 [2, 2048, 2048], P(None, 'fsdp'), may hold values from -6 to 6
- doc_lengths: int32 [2, 6], replicated, may hold values from 1 to 1536, 2048 in all within a row
- ln1_gain: float32 [2048], replicated, may hold values from 0.5 to 1.5
- ln1_bias: float32 [2048], replicated, may hold values from -2 to 2
- w_qkv: bfloat16 [2048, 3, 2048], P('fsdp', None, 'tp'), may hold values from -0.125 to 0.125
- qkv_bias: float32 [3, 2048], P(None, 'tp'), may hold values from -2 to 2
- w_out: bfloat16 [2048, 2048], P('fsdp', 'tp'), may hold values from -2 to 2
- ln2_gain: float32 [2048], replicated, may hold values from 0.5 to 1.5
- ln2_bias: float32 [2048], replicated, may hold values from -2 to 2
- w_gate_up: bfloat16 [2048, 2, 5632], P('fsdp', None, 'tp'), may hold values from -0.125 to 0.125
- w_down: bfloat16 [2048, 5632], P('fsdp', 'tp'), may hold values from -0.078125 to 0.078125
- grad_y: bfloat16 [2, 2048, 2048], P(None, 'fsdp'), may hold values from -6 to 6
Outputs:
- block_output: bfloat16 [2, 2048, 2048], P(None, 'fsdp')
- grad_input: bfloat16 [2, 2048, 2048], P(None, 'fsdp')
- grad_ln1_gain: float32 [2048], replicated
- grad_ln1_bias: float32 [2048], replicated
- grad_w_qkv: float32 [2048, 3, 2048], P('fsdp', None, 'tp')
- grad_qkv_bias: float32 [3, 2048], P(None, 'tp')
- grad_w_out: float32 [2048, 2048], P('fsdp', 'tp')
- grad_ln2_gain: float32 [2048], replicated
- grad_ln2_bias: float32 [2048], replicated
- grad_w_gate_up: float32 [2048, 2, 5632], P('fsdp', None, 'tp')
- grad_w_down: float32 [2048, 5632], P('fsdp', 'tp')
Inputs may be any that keep to these rules, and one draw needn't show every extreme that they name: `doc_lengths`: each row sums to 2048, and in each row the longest document has exactly 1536 tokens.
All inputs are finite; a program needn't handle non-finite values.
Results may differ from a plain program's by a relative error of at most 0.025.
Values may be sent and summed in bfloat16 or wider, within the bound.
A program may use at most 256 MiB of HBM per device.

v0:
```python
import math

import jax
import jax.numpy as jnp
from jax import lax
from jax.sharding import PartitionSpec as P

HD = 64
ROT = 16
LEN = 2048
SEQ_MB = 1
MICRO = 2


epsilon = 1e-05
negative = -1e30


def layer_norm(matrix_in, norm_gain, norm_shift):
    center = jnp.mean(matrix_in, axis=-1, keepdims=True)
    centered = matrix_in - center
    spread = jnp.mean(centered * centered, axis=-1, keepdims=True)
    inverse = lax.rsqrt(spread + epsilon)
    normed = centered * inverse
    return (normed * norm_gain + norm_shift, normed, inverse)


def norm_back(incoming, normed, inverse, norm_gain):
    scaled = incoming * norm_gain
    first_mean = jnp.mean(scaled, axis=-1, keepdims=True)
    cross_mean = jnp.mean(scaled * normed, axis=-1, keepdims=True)
    return inverse * (scaled - first_mean - normed * cross_mean)


def doc_layout(lengths, places):
    doc_ends = jnp.cumsum(lengths, axis=-1)
    passed = (places[:, :, None] >= doc_ends[:, None, :]).astype(jnp.int32)
    segment = jnp.sum(passed, axis=-1)
    begins = jnp.sum(passed * lengths[:, None, :], axis=-1)
    return (segment, places - begins)


def rotary_tables(offset):
    halfway = ROT // 2
    exponent = jnp.arange(halfway, dtype=jnp.float32) * (2.0 / ROT)
    frequency = jnp.exp(-math.log(10000.0) * exponent)
    angles = offset.astype(jnp.float32)[..., None] * frequency
    return (jnp.cos(angles), jnp.sin(angles))


def rotate(head_rows, cosine_table, sine_table, direction):
    halfway = ROT // 2
    leading = head_rows[..., :halfway]
    behind = head_rows[..., halfway:ROT]
    cosine_part = cosine_table[..., None, :]
    sine_part = sine_table[..., None, :] * direction
    return jnp.concatenate(
        [
            leading * cosine_part - behind * sine_part,
            behind * cosine_part + leading * sine_part,
            head_rows[..., ROT:],
        ],
        axis=-1,
    )


def pair_mask(query_seg, query_place, key_seg, key_place):
    same_doc = query_seg[:, :, None] == key_seg[:, None, :]
    causal = key_place[:, None, :] <= query_place[:, :, None]
    return (same_doc & causal)[:, :, None, :]


def fold_blocks(update, folded, part_arrays, block_len):
    extent = part_arrays[0].shape[1]
    number = extent // block_len
    blocks = tuple(
        (
            jnp.swapaxes(
                part_array.reshape((part_array.shape[0], number, block_len) + part_array.shape[2:]),
                0,
                1,
            )
            for part_array in part_arrays
        )
    )

    def advance(running, element):
        block_index, block_parts = element
        return (update(running, block_parts, block_index * block_len), None)

    folded, unused = lax.scan(advance, folded, (jnp.arange(number, dtype=jnp.int32), blocks))
    return folded


def fetch_weights(w_qkv, w_out, w_gate_up, w_down):
    return (
        lax.all_gather(w_qkv, "fsdp", axis=0, tiled=True),
        lax.all_gather(w_out, "fsdp", axis=0, tiled=True),
        lax.all_gather(w_gate_up, "fsdp", axis=0, tiled=True),
        lax.all_gather(w_down, "fsdp", axis=0, tiled=True),
    )


def on_device(
    block_input,
    doc_lengths,
    ln1_gain,
    ln1_bias,
    w_qkv,
    qkv_bias,
    w_out,
    ln2_gain,
    ln2_bias,
    w_gate_up,
    w_down,
    grad_y,
):
    floats = jnp.float32
    halves = jnp.bfloat16
    factor = 1.0 / math.sqrt(HD)
    per_batch = SEQ_MB
    shard_len = block_input.shape[1]
    model_width = block_input.shape[2]
    head_cols = qkv_bias.shape[1]
    heads_local = head_cols // HD
    hidden_cols = w_down.shape[1]
    row_count = per_batch * shard_len
    rows_owned = model_width // lax.axis_size("fsdp")
    first_row = lax.axis_index("fsdp") * shard_len
    query_place = jnp.broadcast_to(
        first_row + jnp.arange(shard_len, dtype=jnp.int32), (per_batch, shard_len)
    )
    key_block = min(LEN, 512)
    block_count = LEN // key_block
    g_ln1_gain = jnp.zeros((model_width,), floats)
    g_ln1_bias = jnp.zeros((model_width,), floats)
    g_ln2_gain = jnp.zeros((model_width,), floats)
    g_ln2_bias = jnp.zeros((model_width,), floats)
    g_bias = jnp.zeros((3, head_cols), floats)
    stored = []
    output_parts = []
    input_grads = []
    for batch in range(MICRO):
        lower = batch * per_batch
        seq_rows = block_input[lower : lower + per_batch]
        lengths = doc_lengths[lower : lower + per_batch]
        seq_grad = grad_y[lower : lower + per_batch]
        query_seg, offset = doc_layout(lengths, query_place)
        cosine_table, sine_table = rotary_tables(offset)
        gathered = fetch_weights(w_qkv, w_out, w_gate_up, w_down)
        full_qkv, full_out, full_gate_up, full_down = gathered
        input_wide = seq_rows.reshape(row_count, model_width).astype(floats)
        first_norm, normed1, inverse1 = layer_norm(input_wide, ln1_gain, ln1_bias)
        first_low = first_norm.astype(halves)
        projected = (
            jnp.dot(
                first_low,
                full_qkv.reshape(model_width, 3 * head_cols),
                preferred_element_type=floats,
            ).reshape(row_count, 3, head_cols)
            + qkv_bias
        )
        projected = projected.reshape(per_batch, shard_len, 3, heads_local, HD)
        query_heads = rotate(projected[:, :, 0], cosine_table, sine_table, 1.0).astype(halves)
        key_heads = rotate(projected[:, :, 1], cosine_table, sine_table, 1.0).astype(halves)
        value_heads = projected[:, :, 2].astype(halves)
        key_flat = key_heads.reshape(per_batch, shard_len, head_cols)
        value_flat = value_heads.reshape(per_batch, shard_len, head_cols)

        def attend(running, block_parts, offset_at):
            key_part, value_part = block_parts
            extent = key_part.shape[1]
            key_place = jnp.broadcast_to(
                offset_at + jnp.arange(extent, dtype=jnp.int32), (per_batch, extent)
            )
            key_seg = doc_layout(lengths, key_place)[0]
            allowed = pair_mask(query_seg, query_place, key_seg, key_place)
            scores = (
                jnp.einsum(
                    "sqhd,skhd->sqhk",
                    query_heads,
                    key_part.reshape(per_batch, extent, heads_local, HD),
                    preferred_element_type=floats,
                )
                * factor
            )
            scores = jnp.where(allowed, scores, negative)
            highest, denominator, summed = running
            new_high = jnp.maximum(highest, jnp.max(scores, axis=-1))
            shrink = jnp.exp(highest - new_high)
            weights = jnp.where(allowed, jnp.exp(scores - new_high[..., None]), 0.0)
            denominator = denominator * shrink + jnp.sum(weights, axis=-1)
            summed = summed * shrink[..., None] + jnp.einsum(
                "sqhk,skhd->sqhd",
                weights.astype(halves),
                value_part.reshape(per_batch, extent, heads_local, HD),
                preferred_element_type=floats,
            )
            return (new_high, denominator, summed)

        start_state = (
            jnp.full((per_batch, shard_len, heads_local), negative, floats),
            jnp.zeros((per_batch, shard_len, heads_local), floats),
            jnp.zeros((per_batch, shard_len, heads_local, HD), floats),
        )
        highest, denominator, summed = fold_blocks(
            attend,
            start_state,
            (
                lax.all_gather(key_flat, "fsdp", axis=1, tiled=True),
                lax.all_gather(value_flat, "fsdp", axis=1, tiled=True),
            ),
            key_block,
        )
        lse_rows = highest + jnp.log(denominator)
        attended = (summed / denominator[..., None]).astype(halves).reshape(row_count, head_cols)
        attn_part = jnp.einsum("rc,oc->ro", attended, full_out, preferred_element_type=floats)
        residual = input_wide + lax.psum(attn_part.astype(jnp.bfloat16), "tp").astype(jnp.float32)
        second_norm, normed2, inverse2 = layer_norm(residual, ln2_gain, ln2_bias)
        second_low = second_norm.astype(halves)
        gate_up = jnp.dot(
            second_low,
            full_gate_up.reshape(model_width, 2 * hidden_cols),
            preferred_element_type=floats,
        ).reshape(row_count, 2, hidden_cols)
        gate = gate_up[:, 0]
        up_part = gate_up[:, 1]
        sigmoid_gate = jax.nn.sigmoid(gate)
        hidden = (gate * sigmoid_gate * up_part).astype(halves)
        ffn_part = jnp.einsum("rf,of->ro", hidden, full_down, preferred_element_type=floats)
        residual_out = residual + lax.psum(ffn_part.astype(jnp.bfloat16), "tp").astype(jnp.float32)
        output_parts.append(residual_out.astype(halves).reshape(per_batch, shard_len, model_width))
        full_qkv, full_out, full_gate_up, full_down = (
            lax.all_gather(w_qkv, "fsdp", axis=0, tiled=True),
            lax.all_gather(w_out, "fsdp", axis=0, tiled=True),
            lax.all_gather(w_gate_up, "fsdp", axis=0, tiled=True),
            lax.all_gather(w_down, "fsdp", axis=0, tiled=True),
        )
        grad_rows = seq_grad.reshape(row_count, model_width)
        grad_hidden = jnp.dot(grad_rows, full_down, preferred_element_type=floats)
        grad_gate = grad_hidden * up_part * sigmoid_gate * (1.0 + gate * (1.0 - sigmoid_gate))
        grad_upper = grad_hidden * gate * sigmoid_gate
        grad_gate_up = (
            jnp.stack([grad_gate, grad_upper], axis=1)
            .astype(halves)
            .reshape(row_count, 2 * hidden_cols)
        )
        second_part = jnp.einsum(
            "rg,dg->rd",
            grad_gate_up,
            full_gate_up.reshape(model_width, 2 * hidden_cols),
            preferred_element_type=floats,
        )
        grad_second = lax.psum(second_part.astype(jnp.bfloat16), "tp").astype(jnp.float32)
        grad_residual = grad_rows.astype(floats) + norm_back(
            grad_second, normed2, inverse2, ln2_gain
        )
        g_ln2_gain = g_ln2_gain + jnp.sum(grad_second * normed2, axis=0)
        g_ln2_bias = g_ln2_bias + jnp.sum(grad_second, axis=0)
        residual_low = grad_residual.astype(halves)
        grad_attended = jnp.dot(residual_low, full_out, preferred_element_type=floats).astype(
            halves
        )
        delta_rows = jnp.sum(
            (grad_attended.astype(floats) * attended.astype(floats)).reshape(
                per_batch, shard_len, heads_local, HD
            ),
            axis=-1,
        )
        grad_heads = grad_attended.reshape(per_batch, shard_len, heads_local, HD)
        all_keys, all_values = (
            lax.all_gather(key_flat, "fsdp", axis=1, tiled=True),
            lax.all_gather(value_flat, "fsdp", axis=1, tiled=True),
        )

        def backward_block(running, block_index):
            offset_at = block_index * key_block
            key_part = lax.dynamic_slice_in_dim(all_keys, offset_at, key_block, 1).reshape(
                per_batch, key_block, heads_local, HD
            )
            value_part = lax.dynamic_slice_in_dim(all_values, offset_at, key_block, 1).reshape(
                per_batch, key_block, heads_local, HD
            )
            key_place = jnp.broadcast_to(
                offset_at + jnp.arange(key_block, dtype=jnp.int32), (per_batch, key_block)
            )
            key_seg = doc_layout(lengths, key_place)[0]
            allowed = pair_mask(query_seg, query_place, key_seg, key_place)
            scores = (
                jnp.einsum("sqhd,skhd->sqhk", query_heads, key_part, preferred_element_type=floats)
                * factor
            )
            softmax_out = jnp.where(allowed, jnp.exp(scores - lse_rows[..., None]), 0.0)
            grad_probs = jnp.einsum(
                "sqhd,skhd->sqhk", grad_heads, value_part, preferred_element_type=floats
            )
            grad_scores = (softmax_out * (grad_probs - delta_rows[..., None]) * factor).astype(
                halves
            )
            running = running + jnp.einsum(
                "sqhk,skhd->sqhd", grad_scores, key_part, preferred_element_type=floats
            )
            key_term = jnp.einsum(
                "sqhk,sqhd->skhd", grad_scores, query_heads, preferred_element_type=floats
            )
            value_term = jnp.einsum(
                "sqhk,sqhd->skhd",
                softmax_out.astype(halves),
                grad_heads,
                preferred_element_type=floats,
            )
            return (running, (key_term, value_term))

        zero_heads = jnp.zeros((per_batch, shard_len, heads_local, HD), floats)
        grad_query, block_terms = lax.scan(
            backward_block, zero_heads, jnp.arange(block_count, dtype=jnp.int32)
        )
        key_terms = jnp.swapaxes(block_terms[0], 0, 1).reshape(per_batch, LEN, head_cols)
        value_terms = jnp.swapaxes(block_terms[1], 0, 1).reshape(per_batch, LEN, head_cols)
        grad_key, grad_value = (
            lax.psum_scatter(
                key_terms.astype(jnp.bfloat16), "fsdp", scatter_dimension=1, tiled=True
            ).astype(jnp.float32),
            lax.psum_scatter(
                value_terms.astype(jnp.bfloat16), "fsdp", scatter_dimension=1, tiled=True
            ).astype(jnp.float32),
        )
        grad_key = grad_key.reshape(per_batch, shard_len, heads_local, HD)
        grad_value = grad_value.reshape(per_batch, shard_len, heads_local, HD)
        grad_query = rotate(grad_query, cosine_table, sine_table, -1.0)
        grad_key = rotate(grad_key, cosine_table, sine_table, -1.0)
        grad_projected = jnp.stack([grad_query, grad_key, grad_value], axis=2).reshape(
            row_count, 3, head_cols
        )
        g_bias = g_bias + jnp.sum(grad_projected, axis=0)
        grad_qkv = grad_projected.astype(halves).reshape(row_count, 3 * head_cols)
        first_part = jnp.einsum(
            "rc,dc->rd",
            grad_qkv,
            full_qkv.reshape(model_width, 3 * head_cols),
            preferred_element_type=floats,
        )
        grad_first = lax.psum(first_part.astype(jnp.bfloat16), "tp").astype(jnp.float32)
        g_ln1_gain = g_ln1_gain + jnp.sum(grad_first * normed1, axis=0)
        g_ln1_bias = g_ln1_bias + jnp.sum(grad_first, axis=0)
        grad_input = (grad_residual + norm_back(grad_first, normed1, inverse1, ln1_gain)).astype(
            halves
        )
        input_grads.append(grad_input.reshape(per_batch, shard_len, model_width))
        kept_rows = (
            first_low,
            grad_qkv,
            residual_low,
            attended,
            second_low,
            grad_gate_up,
            grad_rows,
            hidden,
        )
        stored.append(kept_rows)
    joined = tuple(
        (jnp.concatenate([entry[column] for entry in stored], axis=0) for column in range(8))
    )
    first_low, grad_qkv, residual_low, attended, second_low, grad_gate_up, grad_rows, hidden = (
        joined
    )

    def product(left_rows, right_rows):
        return lax.dot_general(
            left_rows, right_rows, (((0,), (0,)), ((), ())), preferred_element_type=floats
        )

    weight_grads = lax.psum_scatter(
        jnp.concatenate(
            [
                product(first_low, grad_qkv),
                product(residual_low, attended),
                product(second_low, grad_gate_up),
                product(grad_rows, hidden),
            ],
            axis=1,
        ).astype(jnp.bfloat16),
        "fsdp",
        scatter_dimension=0,
        tiled=True,
    ).astype(jnp.float32)
    g_ln1_gain, g_ln1_bias, g_bias, g_ln2_gain, g_ln2_bias = (
        lax.psum(g_ln1_gain.astype(jnp.bfloat16), "fsdp").astype(jnp.float32),
        lax.psum(g_ln1_bias.astype(jnp.bfloat16), "fsdp").astype(jnp.float32),
        lax.psum(g_bias.astype(jnp.bfloat16), "fsdp").astype(jnp.float32),
        lax.psum(g_ln2_gain.astype(jnp.bfloat16), "fsdp").astype(jnp.float32),
        lax.psum(g_ln2_bias.astype(jnp.bfloat16), "fsdp").astype(jnp.float32),
    )
    grad_w_qkv = weight_grads[:, : 3 * head_cols].reshape(rows_owned, 3, head_cols)
    grad_w_out = weight_grads[:, 3 * head_cols : 4 * head_cols]
    grad_w_gate_up = weight_grads[:, 4 * head_cols : 4 * head_cols + 2 * hidden_cols].reshape(
        rows_owned, 2, hidden_cols
    )
    grad_w_down = weight_grads[:, 4 * head_cols + 2 * hidden_cols :]
    block_output = jnp.concatenate(output_parts, axis=0)
    grad_block = jnp.concatenate(input_grads, axis=0)
    return (
        block_output,
        grad_block,
        g_ln1_gain,
        g_ln1_bias,
        grad_w_qkv,
        g_bias,
        grad_w_out,
        g_ln2_gain,
        g_ln2_bias,
        grad_w_gate_up,
        grad_w_down,
    )


def solution(mesh):
    placed = (
        P(None, "fsdp", None),
        P(),
        P(),
        P(),
        P("fsdp", None, "tp"),
        P(None, "tp"),
        P("fsdp", "tp"),
        P(),
        P(),
        P("fsdp", None, "tp"),
        P("fsdp", "tp"),
        P(None, "fsdp", None),
    )
    return jax.shard_map(
        on_device,
        mesh=mesh,
        in_specs=placed,
        out_specs=(
            P(None, "fsdp", None),
            P(None, "fsdp", None),
            P(),
            P(),
            P("fsdp", None, "tp"),
            P(None, "tp"),
            P("fsdp", "tp"),
            P(),
            P(),
            P("fsdp", None, "tp"),
            P("fsdp", "tp"),
        ),
        check_vma=False,
    )
```

profile of v0, /device:TPU:24, one launch (start us, length us, event | category | flops | bytes accessed | tf_op | source)
XLA Modules:
  0.0 1805.6 jit_solution(16882995159830599643)
XLA Ops:
  15.2 92.8 %all-gather.9.cloned.1.call-done = bf16[2048,3,512]{2,0,1:T(8,128)(2,1)} async-done(((bf16[256,3,512]{2,0,1:T(8,128)(2,1)}), bf16[2048,3,512]{2,0,1:T(8,128)(2,1)}) %all-gather.9.cloned.1.call-update) | async-done | bytes 6291472 | tf_op jit(solution)/shard_map/all_gather | solution.py:97
  108.0 8.8 copy.106
  116.9 5.8 fusion.229
  130.4 46.1 %all-gather.11.cloned.1.call-done = bf16[1,2048,512]{1,2,0:T(8,128)(2,1)} async-done(((bf16[1,256,512]{1,2,0:T(8,128)(2,1)}), bf16[1,2048,512]{1,2,0:T(8,128)(2,1)}) %all-gather.11.cloned.1.call-update) | async-done | bytes 2097168 | tf_op jit(solution)/shard_map/all_gather | solution.py:210
  179.6 48.1 %all-gather.13.cloned.1.call-done = bf16[1,2048,512]{1,2,0:T(8,128)(2,1)} async-done(((bf16[1,256,512]{1,2,0:T(8,128)(2,1)}), bf16[1,2048,512]{1,2,0:T(8,128)(2,1)}) %all-gather.13.cloned.1.call-update) | async-done | bytes 2097168 | tf_op jit(solution)/shard_map/all_gather | solution.py:211
  231.3 55.9 %while.68 = (s32[]{:T(128)}, f32[1,256,8]{1,2,0:T(8,128)S(1)}, f32[1,256,8]{1,2,0:T(8,128)}, f32[1,256,8,64]{1,3,2,0:T(8,128)}, s32[1,256]{1,0:T(1,128)}, /*inde...) while((s32[]{:T(128)}, f32[1,256,8]{1,2,0:T(8,128)S(1)}, ...), condition=%wide.region_9.10_spmd.clone, body=%wide.region_5.9_spmd.clone.sunk | while | flops 282875136 | bytes 34551080 | solution.py:91
  239.0 3.3 fusion.358
  252.2 3.3 fusion.358
  266.4 3.3 fusion.358
  280.7 3.3 fusion.358
  288.3 3.4 convolution_convert_fusion.5
  291.8 36.8 %all-reduce.8.cloned.1.call-done = bf16[256,2048]{1,0:T(8,128)(2,1)} async-done(((bf16[256,2048]{1,0:T(8,128)(2,1)}), bf16[256,2048]{1,0:T(8,128)(2,1)}) %all-reduce.8.cloned.1.call-update) | async-done | bytes 1048592 | tf_op jit(solution)/shard_map/psum | solution.py:218
  331.0 5.8 fusion.232
  344.4 46.6 %all-gather.21.cloned.1.call-done = bf16[1,2048,512]{1,2,0:T(8,128)(2,1)} async-done(((bf16[1,256,512]{1,2,0:T(8,128)(2,1)}), bf16[1,2048,512]{1,2,0:T(8,128)(2,1)}) %all-gather.21.cloned.1.call-update) | async-done | bytes 2097168 | tf_op jit(solution)/shard_map/all_gather | solution.py:210
  394.2 48.1 %all-gather.23.cloned.1.call-done = bf16[1,2048,512]{1,2,0:T(8,128)(2,1)} async-done(((bf16[1,256,512]{1,2,0:T(8,128)(2,1)}), bf16[1,2048,512]{1,2,0:T(8,128)(2,1)}) %all-gather.23.cloned.1.call-update) | async-done | bytes 2097168 | tf_op jit(solution)/shard_map/all_gather | solution.py:211
  445.9 62.6 %while.69 = (s32[]{:T(128)}, f32[1,256,8]{1,2,0:T(8,128)S(1)}, f32[1,256,8]{1,2,0:T(8,128)}, f32[1,256,8,64]{1,3,2,0:T(8,128)}, s32[1,256]{1,0:T(1,128)S(1)}, /*...) while((s32[]{:T(128)}, f32[1,256,8]{1,2,0:T(8,128)S(1)}, ...), condition=%wide.region_23.24_spmd.clone, body=%wide.region_19.23_spmd.clone.sunk | while | flops 282875136 | bytes 34555212 | solution.py:91
  450.8 3.4 fusion.364
  454.9 3.3 fusion.366
  466.3 3.4 fusion.364
  470.5 3.3 fusion.366
  482.0 3.4 fusion.364
  486.2 3.3 fusion.366
  489.6 3.2 fusion.367
  497.7 3.4 fusion.364
  501.8 3.3 fusion.366
  509.6 3.4 convolution_convert_fusion.4
  516.4 33.1 %all-reduce.10.cloned.1.call-done = bf16[256,2048]{1,0:T(8,128)(2,1)} async-done(((bf16[256,2048]{1,0:T(8,128)(2,1)}), bf16[256,2048]{1,0:T(8,128)(2,1)}) %all-reduce.10.cloned.1.call-update) | async-done | bytes 1048592 | tf_op jit(solution)/shard_map/psum | solution.py:218
  555.6 158.6 %all-gather.17.cloned.1.call-done = bf16[2048,2,1408]{2,0,1:T(8,128)(2,1)} async-done(((bf16[256,2,1408]{2,0,1:T(8,128)(2,1)}), bf16[2048,2,1408]{2,0,1:T(8,128)(2,1)}) %all-gather.17.cloned.1.call-update) | async-done | bytes 11534352 | tf_op jit(solution)/shard_map/all_gather | solution.py:99
  714.2 15.5 copy.111
  729.7 9.6 fusion.134
  739.3 4.8 fusion.136
  744.0 62.8 %all-gather.19.cloned.1.call-done = bf16[2048,1408]{1,0:T(8,128)(2,1)} async-done(((bf16[256,1408]{1,0:T(8,128)(2,1)}), bf16[2048,1408]{1,0:T(8,128)(2,1)}) %all-gather.19.cloned.1.call-update) | async-done | bytes 5767184 | tf_op jit(solution)/shard_map/all_gather | solution.py:100
  806.8 6.8 multiply_bitcast_fusion.3
  813.7 6.3 multiply_bitcast_fusion.1
  820.0 5.3 fusion.161
  825.2 5.7 fusion.162
  833.3 49.3 %all-reduce.14.cloned.1.call-done = (bf16[256,2048]{1,0:T(8,128)(2,1)}, bf16[256,2048]{1,0:T(8,128)(2,1)}) async-done(((bf16[256,2048]{1,0:T(8,128)(2,1)}, bf16[256,2048]{1,0:T(8,128)(2,1)}), (bf16[256,2048]{1,0:T(8,128)(2,1)}, bf16[256,2048]{1,0:T(8,128)(2,1)})) %all-reduce.14.cloned.1.call-update) | async-done | bytes 2097168 | tf_op jit(solution)/shard_map/psum | solution.py:254
  882.6 4.9 fusion.205
  887.7 3.3 fusion.272
  895.5 53.9 %while.71 = (s32[]{:T(128)}, f32[1,256,8,64]{1,3,2,0:T(8,128)}, bf16[4,1,512,8,64]{2,4,3,1,0:T(8,128)(2,1)}, bf16[4,1,512,8,64]{2,4,3,1,0:T(8,128)(2,1)}, s32[4]...) while((s32[]{:T(128)}, f32[1,256,8,64]{1,3,2,0:T(8,128)}, ...), condition=%wide.region_46.47_spmd.clone, body=%wide.region_44.46_spmd.clone.sunk | while | flops 683287808 | bytes 77501840 | solution.py:315
  949.4 3.2 copy.126
  963.7 51.4 %while.70 = (s32[]{:T(128)}, f32[1,256,8,64]{1,3,2,0:T(8,128)S(1)}, bf16[4,1,512,8,64]{2,4,3,1,0:T(8,128)(2,1)}, bf16[4,1,512,8,64]{2,4,3,1,0:T(8,128)(2,1)}, s3...) while((s32[]{:T(128)}, f32[1,256,8,64]{1,3,2,0:T(8,128)S(1)}, ...), condition=%wide.region_34.35_spmd.clone, body=%wide.region_32.34_spmd.clone.sunk | while | flops 683287808 | bytes 79599040 | solution.py:315
  1015.1 3.2 copy.118
  1022.8 4.3 copy.150
  1027.1 6.4 reshape.1855
  1035.3 4.3 copy.149
  1039.5 6.6 reshape.1854
  1046.9 5.9 convolution_convert_fusion.6
  1053.2 5.7 convolution_convert_fusion.7
  1061.0 34.1 %reduce-scatter.6.cloned.1.call-done = bf16[1,256,512]{1,2,0:T(8,128)(2,1)} async-done(((bf16[1,2048,512]{1,2,0:T(8,128)(2,1)}), bf16[1,256,512]{1,2,0:T(8,128)(2,1)}) %reduce-scatter.6.cloned.1.call-update) | async-done | bytes 262160 | tf_op jit(solution)/shard_map/reduce_scatter | solution.py:321
  1102.2 64.3 %reduce-scatter.12.cloned.1.call-done = bf16[1,256,512]{2,1,0:T(8,128)(2,1)} async-done(((bf16[1,2048,512]{2,1,0:T(8,128)(2,1)}), bf16[1,256,512]{2,1,0:T(8,128)(2,1)}) %reduce-scatter.12.cloned.1.call-update) | async-done | bytes 262160 | tf_op jit(solution)/shard_map/reduce_scatter | solution.py:324
  1169.3 68.5 %reduce-scatter.8.cloned.1.call-done = bf16[1,256,512]{2,1,0:T(8,128)(2,1)} async-done(((bf16[1,2048,512]{2,1,0:T(8,128)(2,1)}), bf16[1,256,512]{2,1,0:T(8,128)(2,1)}) %reduce-scatter.8.cloned.1.call-update) | async-done | bytes 262160 | tf_op jit(solution)/shard_map/reduce_scatter | solution.py:324
  1241.0 5.9 fusion.164
  1258.5 8.0 convolution_convert_fusion.2
  1266.5 9.0 convolution_convert_fusion
  1282.0 53.9 %all-reduce.12.cloned.1.call-done = (bf16[256,2048]{1,0:T(8,128)(2,1)}, bf16[256,2048]{1,0:T(8,128)(2,1)}, bf16[256,2048]{1,0:T(8,128)(2,1)}, bf16[256,2048]{1,0:T(8,128)(2,1)}) async-done(((bf16[256,2048]{1,0:T(8,128)(2,1)}, bf16[256,2048]{1,0:T(8,128)(2,1)}, bf16[256,2048]{1,0:T(8,128)(2,1)}, bf16[256,2048]{1,0:T(8,128)(2,1)}), (bf16[256,2048]{1,0:T(8,128)(2,1)}, bf16[256,2048]{1,0:T(8,128)(2,1)}, ...) | async-done | bytes 4194320 | tf_op jit(solution)/shard_map/psum | solution.py:231
  1335.9 3.7 fusion.178
  1339.7 5.6 convolution_convert_fusion.1
  1345.3 8.7 copy.136
  1354.0 17.8 pad_maximum_fusion
  1375.6 34.6 %all-reduce = (bf16[2048]{0:T(1024)(128)(2,1)S(1)}, bf16[2048]{0:T(1024)(128)(2,1)S(1)}, bf16[3,512]{1,0:T(4,128)(2,1)S(1)}, bf16[2048]{0:T(1024)(128)(2,1)S(1)}, bf16[2048]{0:T(1024)(128)(2,1)S(1)}) all-reduce(bf16[2048]{0:T(1024)(128)(2,1)S(1)} %add_convert_fusion.12, ...), channel_id=1, replica_groups=mesh['fsdp'=8,'tp'=4] {'fsdp'}, use_global_device_ids=true, to_apply=%region_54.55 | all-reduce | flops 9728 | bytes 38912 | tf_op jit(solution)/shard_map/psum | solution.py:388
  1413.4 4.0 fusion.245
  1422.9 358.6 %reduce-scatter.14.cloned.1.call-done = bf16[256,6272]{1,0:T(8,128)(2,1)} async-done(((bf16[2048,6272]{1,0:T(8,128)(2,1)}), bf16[256,6272]{1,0:T(8,128)(2,1)}) %reduce-scatter.14.cloned.1.call-update) | async-done | bytes 3211280 | tf_op jit(solution)/shard_map/reduce_scatter | solution.py:373
  1791.9 4.7 reshape.1819
  (700 shorter events, 301.1 us)
Async XLA Ops:
  7.2 100.8 %all-gather.9.cloned.1.call-start = ((), (), s32[]{:S(2)}) async-start(), calls=%async_computation.5 | async-start | bytes 7077888 | tf_op jit(solution)/shard_map/all_gather | solution.py:97
  7.9 168.6 %all-gather.11.cloned.1.call-start = ((), (), s32[]{:S(2)}) async-start(), calls=%async_computation.6 | async-start | bytes 2359296 | tf_op jit(solution)/shard_map/all_gather | solution.py:210
  14.0 102.9 %copy-start.100 = (f32[256]{0:T(256)}, f32[256]{0:T(256)S(1)}, u32[]{:S(2)}) copy-start(f32[256]{0:T(256)S(1)} %get-tuple-element.1137) | copy-start | bytes 3076
  14.4 102.4 %copy-start.102 = (f32[256]{0:T(256)}, f32[256]{0:T(256)S(1)}, u32[]{:S(2)}) copy-start(f32[256]{0:T(256)S(1)} %add_rsqrt_fusion.3) | copy-start | bytes 3076
  15.2 111.8 %copy-start.79 = (f32[256,8]{0,1:T(8,128)}, f32[256,8]{0,1:T(8,128)S(1)}, u32[]{:S(2)}) copy-start(f32[256,8]{0,1:T(8,128)S(1)} %get-tuple-element.1119) | copy-start | bytes 24580
  15.2 101.7 %copy-start.76 = (f32[2048]{0:T(1024)S(1)}, f32[2048]{0:T(1024)}, u32[]{:S(2)}) copy-start(f32[2048]{0:T(1024)} %param.22) | copy-start | bytes 24580
  15.2 101.7 %copy-start.115 = (f32[2048]{0:T(1024)S(1)}, f32[2048]{0:T(1024)}, u32[]{:S(2)}) copy-start(f32[2048]{0:T(1024)} %param.23) | copy-start | bytes 24580
  15.2 101.7 %copy-start.120 = (f32[3,512]{1,0:T(4,128)S(1)}, f32[3,512]{1,0:T(4,128)}, u32[]{:S(2)}) copy-start(f32[3,512]{1,0:T(4,128)} %param.25) | copy-start | bytes 18436
  127.8 99.9 %all-gather.13.cloned.1.call-start = ((), (), s32[]{:S(2)}) async-start(), calls=%async_computation.7 | async-start | bytes 2359296 | tf_op jit(solution)/shard_map/all_gather | solution.py:211
  129.7 158.6 %all-gather.15.cloned.1.call-start = ((), (), s32[]{:S(2)}) async-start(), calls=%async_computation.8 | async-start | bytes 2359296 | tf_op jit(solution)/shard_map/all_gather | solution.py:98
  130.2 198.3 %all-reduce.8.cloned.1.call-start = ((), (), s32[]{:S(2)}) async-start(), calls=%async_computation.9 | async-start | bytes 2097152 | tf_op jit(solution)/shard_map/psum | solution.py:218
  288.3 542.8 %copy-start.46 = (bf16[1,256,8,64]{1,3,2,0:T(8,128)(2,1)}, bf16[1,256,8,64]{1,3,2,0:T(8,128)(2,1)S(1)}, u32[]{:S(2)}) copy-start(bf16[1,256,8,64]{1,3,2,0:T(8,128)(2,1)S(1)} %divide_convert_fusion.1) | copy-start | bytes 786436
  288.3 40.3 %copy-start.98 = (f32[256]{0:T(256)S(1)}, f32[256]{0:T(256)}, u32[]{:S(2)}) copy-start(f32[256]{0:T(256)} %get-tuple-element.1136) | copy-start | bytes 3076
  291.7 39.3 %copy-start.77 = (f32[2048]{0:T(1024)S(1)}, f32[2048]{0:T(1024)}, u32[]{:S(2)}) copy-start(f32[2048]{0:T(1024)} %param.22) | copy-start | bytes 24580
  291.7 39.3 %copy-start.116 = (f32[2048]{0:T(1024)S(1)}, f32[2048]{0:T(1024)}, u32[]{:S(2)}) copy-start(f32[2048]{0:T(1024)} %param.23) | copy-start | bytes 24580
  291.7 39.3 %copy-start.121 = (f32[3,512]{1,0:T(4,128)S(1)}, f32[3,512]{1,0:T(4,128)}, u32[]{:S(2)}) copy-start(f32[3,512]{1,0:T(4,128)} %param.25) | copy-start | bytes 18436
  291.7 99.3 %all-gather.21.cloned.1.call-start = ((), (), s32[]{:S(2)}) async-start(), calls=%async_computation.12 | async-start | bytes 2359296 | tf_op jit(solution)/shard_map/all_gather | solution.py:210
  342.0 100.3 %all-gather.23.cloned.1.call-start = ((), (), s32[]{:S(2)}) async-start(), calls=%async_computation.13 | async-start | bytes 2359296 | tf_op jit(solution)/shard_map/all_gather | solution.py:211
  343.8 205.7 %all-reduce.10.cloned.1.call-start = ((), (), s32[]{:S(2)}) async-start(), calls=%async_computation.14 | async-start | bytes 2097152 | tf_op jit(solution)/shard_map/psum | solution.py:218
  509.6 322.9 %copy-start.48 = (bf16[1,256,8,64]{1,3,2,0:T(8,128)(2,1)}, bf16[1,256,8,64]{1,3,2,0:T(8,128)(2,1)S(1)}, u32[]{:S(2)}) copy-start(bf16[1,256,8,64]{1,3,2,0:T(8,128)(2,1)S(1)} %divide_convert_fusion) | copy-start | bytes 786436
  513.1 201.1 %all-gather.17.cloned.1.call-start = ((), (), s32[]{:S(2)}) async-start(), calls=%async_computation.10 | async-start | bytes 12976128 | tf_op jit(solution)/shard_map/all_gather | solution.py:99
  515.8 291.1 %all-gather.19.cloned.1.call-start = ((), (), s32[]{:S(2)}) async-start(), calls=%async_computation.11 | async-start | bytes 6488064 | tf_op jit(solution)/shard_map/all_gather | solution.py:100
  516.3 366.3 %all-reduce.14.cloned.1.call-start = ((), (), s32[]{:S(2)}) async-start(), calls=%async_computation.21 | async-start | bytes 4194304 | tf_op jit(solution)/shard_map/psum | solution.py:254
  516.4 371.1 %copy-start.85 = (f32[256]{0:T(256)}, f32[256]{0:T(256)S(1)}, u32[]{:S(2)}) copy-start(f32[256]{0:T(256)S(1)} %broadcast_multiply_fusion.12) | copy-start | bytes 3076
  552.0 335.6 %copy-start.94 = (f32[256]{0:T(256)}, f32[256]{0:T(256)S(1)}, u32[]{:S(2)}) copy-start(f32[256]{0:T(256)S(1)} %add_rsqrt_fusion.2) | copy-start | bytes 3076
  552.0 335.5 %copy-start.83 = (f32[256]{0:T(256)}, f32[256]{0:T(256)S(1)}, u32[]{:S(2)}) copy-start(f32[256]{0:T(256)S(1)} %broadcast_multiply_fusion.10) | copy-start | bytes 3076
  553.2 334.4 %copy-start.96 = (f32[256]{0:T(256)}, f32[256]{0:T(256)S(1)}, u32[]{:S(2)}) copy-start(f32[256]{0:T(256)S(1)} %add_rsqrt_fusion) | copy-start | bytes 3076
  729.7 9.6 copy-start.23
  729.7 9.6 copy-start.54
  806.8 13.1 slice-start
  806.8 13.1 slice-start.1
  831.0 228.1 %reduce-scatter.10.cloned.1.call-start = ((), (), s32[]{:S(2)}) async-start(), calls=%async_computation.17 | async-start | bytes 2359296 | tf_op jit(solution)/shard_map/reduce_scatter | solution.py:321
  955.5 139.6 %reduce-scatter.6.cloned.1.call-start = ((), (), s32[]{:S(2)}) async-start(), calls=%async_computation.15 | async-start | bytes 2359296 | tf_op jit(solution)/shard_map/reduce_scatter | solution.py:321
  1021.2 145.3 %reduce-scatter.12.cloned.1.call-start = ((), (), s32[]{:S(2)}) async-start(), calls=%async_computation.18 | async-start | bytes 2359296 | tf_op jit(solution)/shard_map/reduce_scatter | solution.py:324
  1033.6 204.3 %reduce-scatter.8.cloned.1.call-start = ((), (), s32[]{:S(2)}) async-start(), calls=%async_computation.16 | async-start | bytes 2359296 | tf_op jit(solution)/shard_map/reduce_scatter | solution.py:324
  1046.2 289.6 %all-reduce.12.cloned.1.call-start = ((), (), s32[]{:S(2)}) async-start(), calls=%async_computation.20 | async-start | bytes 8388608 | tf_op jit(solution)/shard_map/psum | solution.py:231
  1059.0 38.9 %copy-start.82 = (f32[256,8]{0,1:T(8,128)S(1)}, f32[256,8]{0,1:T(8,128)}, u32[]{:S(2)}) copy-start(f32[256,8]{0,1:T(8,128)} %get-tuple-element.1128) | copy-start | bytes 24580
  1059.0 38.8 %copy-start.88 = (f32[256,8]{0,1:T(8,128)S(1)}, f32[256,8]{0,1:T(8,128)}, u32[]{:S(2)}) copy-start(f32[256,8]{0,1:T(8,128)} %get-tuple-element.1129) | copy-start | bytes 24580
  1098.1 69.4 %copy-start.33 = (f32[256,1,512]{2,0,1:T(8,128)}, f32[256,1,512]{2,0,1:T(8,128)S(1)}, u32[]{:S(2)}) copy-start(f32[256,1,512]{2,0,1:T(8,128)S(1)} %copy.130) | copy-start | bytes 1572868
  1100.1 68.2 %copy-start.34 = (f32[256,1,512]{2,0,1:T(8,128)S(1)}, f32[256,1,512]{2,0,1:T(8,128)}, u32[]{:S(2)}) copy-start(f32[256,1,512]{2,0,1:T(8,128)} %copy.129) | copy-start | bytes 1572868
  1168.3 78.6 %slice-start.3 = ((s8[6291456]{0:T(1024)(128)(4,1)}), s8[2097152]{0:T(1024)(128)(4,1)S(1)}, s32[]{:S(2)}) async-start(s8[6291456]{0:T(1024)(128)(4,1)} %bitcast.809), calls=%async_computation.25 | async-start | bytes 4194304
  1169.3 71.7 %copy-start.41 = (bf16[256,3,512]{2,0,1:T(8,128)(2,1)S(1)}, bf16[256,3,512]{2,0,1:T(8,128)(2,1)}, u32[]{:S(2)}) copy-start(bf16[256,3,512]{2,0,1:T(8,128)(2,1)} %fusion.236) | copy-start | bytes 2359300
  1249.8 531.7 %reduce-scatter.14.cloned.1.call-start = ((), (), s32[]{:S(2)}) async-start(), calls=%async_computation.19 | async-start | bytes 28901376 | tf_op jit(solution)/shard_map/reduce_scatter | solution.py:373
  1258.5 8.0 copy-start.50
  1258.5 8.0 copy-start.51
  1258.5 8.0 copy-start.55
  1258.5 8.0 copy-start.56
  1266.5 9.1 copy-start.38
  1266.5 9.1 copy-start.40
  1266.5 9.1 copy-start.47
  1266.5 9.1 copy-start.49
  1279.4 56.5 %copy-start.3 = (bf16[2,256,2048]{2,1,0:T(8,128)(2,1)S(1)}, bf16[2,256,2048]{2,1,0:T(8,128)(2,1)}, u32[]{:S(2)}) copy-start(bf16[2,256,2048]{2,1,0:T(8,128)(2,1)} %param.20) | copy-start | bytes 6291460
  1279.4 56.5 %copy-start.78 = (f32[2048]{0:T(1024)S(1)}, f32[2048]{0:T(1024)}, u32[]{:S(2)}) copy-start(f32[2048]{0:T(1024)} %param.22) | copy-start | bytes 24580
  1279.4 56.5 %copy-start.99 = (f32[256]{0:T(256)S(1)}, f32[256]{0:T(256)}, u32[]{:S(2)}) copy-start(f32[256]{0:T(256)} %get-tuple-element.1136) | copy-start | bytes 3076
  1279.4 56.5 %copy-start.101 = (f32[256]{0:T(256)S(1)}, f32[256]{0:T(256)}, u32[]{:S(2)}) copy-start(f32[256]{0:T(256)} %copy-done.100) | copy-start | bytes 3076
  1279.4 56.5 %copy-start.103 = (f32[256]{0:T(256)S(1)}, f32[256]{0:T(256)}, u32[]{:S(2)}) copy-start(f32[256]{0:T(256)} %copy-done.102) | copy-start | bytes 3076
  1279.4 56.5 %copy-start.105 = (f32[256]{0:T(256)S(1)}, f32[256]{0:T(256)}, u32[]{:S(2)}) copy-start(f32[256]{0:T(256)} %copy-done.104) | copy-start | bytes 3076
  1279.4 56.5 %copy-start.117 = (f32[2048]{0:T(1024)S(1)}, f32[2048]{0:T(1024)}, u32[]{:S(2)}) copy-start(f32[2048]{0:T(1024)} %param.23) | copy-start | bytes 24580
  1371.9 41.4 %copy-start.13 = (bf16[256,2048]{1,0:T(8,128)(2,1)S(1)}, bf16[256,2048]{1,0:T(8,128)(2,1)}, u32[]{:S(2)}) copy-start(bf16[256,2048]{1,0:T(8,128)(2,1)} %all-reduce.10.cloned.1.call-done) | copy-start | bytes 3145732
  1371.9 41.4 %copy-start.72 = (f32[2048]{0:T(1024)S(1)}, f32[2048]{0:T(1024)}, u32[]{:S(2)}) copy-start(f32[2048]{0:T(1024)} %param.27) | copy-start | bytes 24580
  1371.9 41.3 %copy-start.84 = (f32[256]{0:T(256)S(1)}, f32[256]{0:T(256)}, u32[]{:S(2)}) copy-start(f32[256]{0:T(256)} %copy-done.83) | copy-start | bytes 3076
  1371.9 41.3 %copy-start.97 = (f32[256]{0:T(256)S(1)}, f32[256]{0:T(256)}, u32[]{:S(2)}) copy-start(f32[256]{0:T(256)} %copy-done.96) | copy-start | bytes 3076
  1371.9 41.3 %copy-start.111 = (f32[256]{0:T(256)S(1)}, f32[256]{0:T(256)}, u32[]{:S(2)}) copy-start(f32[256]{0:T(256)} %copy-done.110) | copy-start | bytes 3076
  1371.9 41.3 %copy-start.113 = (f32[256]{0:T(256)S(1)}, f32[256]{0:T(256)}, u32[]{:S(2)}) copy-start(f32[256]{0:T(256)} %copy-done.112) | copy-start | bytes 3076
  (131 other events, 415.8 us)
Sparse Core Ops, SparseCore 0:
  10.2 97.7 all-gather.8
  127.9 48.5 all-gather.10
  179.1 48.5 all-gather.12
  229.6 47.7 all-gather.14
  291.8 36.6 all-reduce.7
  342.1 48.9 all-gather.20
  393.7 48.5 all-gather.22
  513.2 36.3 all-reduce.9
  552.3 161.8 all-gather.16
  716.2 90.5 all-gather.18
  831.1 51.4 all-reduce.13
  955.6 67.6 reduce-scatter.9
  1026.9 68.1 reduce-scatter.5
  1099.0 67.4 reduce-scatter.11
  1170.5 67.3 reduce-scatter.7
  1249.9 85.8 all-reduce.11
  1372.0 409.4 reduce-scatter.13
where the time goes:
time: 1820 us; the launch traced here: 1810 us
  waiting for transfers between devices  1200 us (66%)
  matrix products  208 us (11%)
  local copies, waits for them, and re-layouts  204 us (11%)
  other arithmetic  126 us (7%)
  blocking collectives  34.6 us (2%)
    reduce_scatter x1, waiting for transfers between devices, on_device(): lax.psum_scatter(jnp.concatenate([product(first_low, grad_qkv), product(r...  359 us
    all_gather x1, waiting for transfers between devices, fetch_weights(): lax.all_gather(w_gate_up, 'fsdp', axis=0, tiled=True)  159 us
    reduce_scatter x2, waiting for transfers between devices, on_device(): lax.psum_scatter(value_terms.astype(jnp.bfloat16), 'fsdp', scatter_dimens...  133 us
    all_gather x2, waiting for transfers between devices, on_device(): lax.all_gather(value_flat, 'fsdp', axis=1, tiled=True)  96.2 us
    all_gather x1, waiting for transfers between devices, fetch_weights(): lax.all_gather(w_qkv, 'fsdp', axis=0, tiled=True)  92.8 us
    all_gather x2, waiting for transfers between devices, on_device(): lax.all_gather(key_flat, 'fsdp', axis=1, tiled=True)  92.8 us
    psum x2, waiting for transfers between devices, on_device(): lax.psum(attn_part.astype(jnp.bfloat16), 'tp').astype(jnp.float32)  69.9 us
    all_gather x1, waiting for transfers between devices, fetch_weights(): lax.all_gather(w_down, 'fsdp', axis=0, tiled=True)  62.8 us
  transfers between devices with their start and end apart: 17, of which 15 were waited for; matrix products, arithmetic and copies ran while one was open for 14% of the time, Pallas kernels for 0%

commit v1 on v0

--- a/solution.py
+++ b/solution.py
@@ -1,8 +1,12 @@
+import functools
 import math
 
 import jax
 import jax.numpy as jnp
 from jax import lax
+from jax.experimental import pallas as pl
+from jax.experimental.pallas import tpu as pltpu
+from jax.sharding import Mesh
 from jax.sharding import PartitionSpec as P
 
 HD = 64
@@ -414,37 +418,650 @@
     )
 
 
+FLIP = ((0, 1), (1, 0))
+LINE = 4
+QUARTER = 128
+
+
+def flip(block, axis):
+    return lax.ppermute(block, axis, FLIP)
+
+
+def head_rows(lanes_of, head):
+    return (lanes_of >= head * HD) & (lanes_of < (head + 1) * HD)
+
+
+def place_rows(place_ref, own_ref, other_ref, target, column):
+    at_z, at_x, at_c = place_ref[0], place_ref[1], place_ref[2]
+    for rel_c in range(2):
+        for rel_z in range(LINE):
+            source = pl.ds((rel_c * LINE + rel_z) * QUARTER, QUARTER)
+            base = lax.rem(at_z + rel_z, LINE) * (4 * QUARTER) + jnp.abs(at_c - rel_c) * QUARTER
+            mine = pl.multiple_of(base + at_x * (2 * QUARTER), QUARTER)
+            theirs = pl.multiple_of(base + (1 - at_x) * (2 * QUARTER), QUARTER)
+            target[pl.ds(mine, QUARTER), :] = column(own_ref, source)
+            target[pl.ds(theirs, QUARTER), :] = column(other_ref, source)
+
+
+def fetch_rows(place_ref, own_ref, other_ref, origin, write):
+    at_z, at_x, at_c = place_ref[0], place_ref[1], place_ref[2]
+    for rel_c in range(2):
+        for rel_z in range(LINE):
+            goal = pl.ds((rel_c * LINE + rel_z) * QUARTER, QUARTER)
+            base = lax.rem(at_z + rel_z, LINE) * (4 * QUARTER) + jnp.abs(at_c - rel_c) * QUARTER
+            mine = pl.multiple_of(base + at_x * (2 * QUARTER), QUARTER)
+            theirs = pl.multiple_of(base + (1 - at_x) * (2 * QUARTER), QUARTER)
+            write(own_ref, goal, origin(pl.ds(mine, QUARTER)))
+            write(other_ref, goal, origin(pl.ds(theirs, QUARTER)))
+
+
+def allowed_block(begin_row, key_at, query_at, key_len, query_len):
+    keys = key_at + lax.broadcasted_iota(jnp.int32, (key_len, query_len), 0)
+    queries = query_at + lax.broadcasted_iota(jnp.int32, (key_len, query_len), 1)
+    return (keys <= queries) & (keys >= begin_row)
+
+
+def attend_kernel(
+    block, place_ref, first_ref, begin_ref, own_ref, other_ref, out_own, out_other, lse_ref, qs, ks, vs, vt, ot
+):
+    floats, halves = jnp.float32, jnp.bfloat16
+    length = qs.shape[0]
+    scale = jnp.asarray(1.0 / math.sqrt(HD), halves)
+    place_rows(place_ref, own_ref, other_ref, qs, lambda ref, rows: ref[0, rows, :] * scale)
+    place_rows(place_ref, own_ref, other_ref, ks, lambda ref, rows: ref[1, rows, :])
+    place_rows(place_ref, own_ref, other_ref, vs, lambda ref, rows: ref[2, rows, :])
+    vt[...] = vs[...].astype(floats).T.astype(halves)
+    lanes_of = lax.broadcasted_iota(jnp.int32, (block, 2 * HD), 1)
+
+    def one_query(index, carry):
+        query_at = pl.multiple_of(index * block, block)
+        query_both = qs[pl.ds(query_at, block), :]
+        begin_row = begin_ref[:, pl.ds(query_at, block)]
+        start = first_ref[index]
+        for head in range(2):
+            query_head = jnp.where(head_rows(lanes_of, head), query_both, jnp.zeros_like(query_both))
+
+            def one_key(step, running):
+                highest, total, summed = running
+                key_at = pl.multiple_of(step * block, block)
+                scores = lax.dot_general(
+                    ks[pl.ds(key_at, block), :],
+                    query_head,
+                    (((1,), (1,)), ((), ())),
+                    preferred_element_type=floats,
+                )
+                allowed = allowed_block(begin_row, key_at, query_at, block, block)
+                scores = jnp.where(allowed, scores, negative)
+                new_high = jnp.maximum(highest, jnp.max(scores, axis=0, keepdims=True))
+                shrink = jnp.exp(highest - new_high)
+                weights = jnp.exp(scores - new_high)
+                total = total * shrink + jnp.sum(weights, axis=0, keepdims=True)
+                summed = summed * shrink + jnp.dot(
+                    vt[head * HD : (head + 1) * HD, pl.ds(key_at, block)],
+                    weights.astype(halves),
+                    preferred_element_type=floats,
+                )
+                return (new_high, total, summed)
+
+            highest, total, summed = lax.fori_loop(
+                start,
+                index + 1,
+                one_key,
+                (
+                    jnp.full((1, block), negative, floats),
+                    jnp.zeros((1, block), floats),
+                    jnp.zeros((HD, block), floats),
+                ),
+            )
+            ot[head * HD : (head + 1) * HD, pl.ds(query_at, block)] = summed / total
+            lse_ref[head : head + 1, pl.ds(query_at, block)] = highest + jnp.log(total)
+        return carry
+
+    lax.fori_loop(0, length // block, one_query, 0)
+    qs[...] = ot[...].T.astype(halves)
+
+    def write(ref, rows, content):
+        ref[rows, :] = content
+
+    fetch_rows(place_ref, out_own, out_other, lambda rows: qs[rows, :], write)
+
+
+def attend_back_kernel(
+    block,
+    place_ref,
+    last_ref,
+    begin_ref,
+    own_ref,
+    other_ref,
+    att_own,
+    att_other,
+    grad_own,
+    grad_other,
+    lse_ref,
+    cos_ref,
+    up_ref,
+    down_ref,
+    out_own,
+    out_other,
+    bias_ref,
+    qs,
+    ks,
+    kt,
+    vs,
+    gs,
+    at,
+    dq,
+    dk,
+    dv,
+    delta,
+):
+    floats, halves = jnp.float32, jnp.bfloat16
+    length = qs.shape[0]
+    scale = jnp.asarray(1.0 / math.sqrt(HD), halves)
+    place_rows(place_ref, own_ref, other_ref, qs, lambda ref, rows: ref[0, rows, :] * scale)
+    place_rows(place_ref, own_ref, other_ref, ks, lambda ref, rows: ref[1, rows, :])
+    place_rows(place_ref, own_ref, other_ref, vs, lambda ref, rows: ref[2, rows, :])
+    place_rows(place_ref, grad_own, grad_other, gs, lambda ref, rows: ref[rows, :])
+    place_rows(place_ref, att_own, att_other, at, lambda ref, rows: ref[rows, :])
+    kt[...] = (ks[...] * scale).astype(floats).T.astype(halves)
+    pairs = gs[...].astype(floats) * at[...].astype(floats)
+    whole_lanes = lax.broadcasted_iota(jnp.int32, (8, 2 * HD), 1)
+    for head in range(2):
+        chosen = jnp.where(head_rows(whole_lanes, head), 1.0, 0.0)
+        delta[8 * head : 8 * head + 8, :] = lax.dot_general(
+            chosen,
+            pairs,
+            (((1,), (1,)), ((), ())),
+            precision=lax.Precision.HIGHEST,
+            preferred_element_type=floats,
+        )
+    dq[...] = jnp.zeros_like(dq)
+    lanes_of = lax.broadcasted_iota(jnp.int32, (block, 2 * HD), 1)
+
+    def one_key(index, carry):
+        key_at = pl.multiple_of(index * block, block)
+        key_both = ks[pl.ds(key_at, block), :]
+        value_both = vs[pl.ds(key_at, block), :]
+        finish = last_ref[index]
+
+        def one_query(step, running):
+            grad_key, grad_value = running
+            query_at = pl.multiple_of(step * block, block)
+            query_both = qs[pl.ds(query_at, block), :]
+            grad_both = gs[pl.ds(query_at, block), :]
+            begin_row = begin_ref[:, pl.ds(query_at, block)]
+            allowed = allowed_block(begin_row, key_at, query_at, block, block)
+            for head in range(2):
+                chosen = head_rows(lanes_of, head)
+                query_head = jnp.where(chosen, query_both, jnp.zeros_like(query_both))
+                grad_head = jnp.where(chosen, grad_both, jnp.zeros_like(grad_both))
+                scores = lax.dot_general(
+                    key_both, query_head, (((1,), (1,)), ((), ())), preferred_element_type=floats
+                )
+                lse_row = lse_ref[head : head + 1, pl.ds(query_at, block)]
+                probs = jnp.where(allowed, jnp.exp(scores - lse_row), 0.0)
+                grad_probs = lax.dot_general(
+                    value_both, grad_head, (((1,), (1,)), ((), ())), preferred_element_type=floats
+                )
+                delta_row = delta[8 * head : 8 * head + 1, pl.ds(query_at, block)]
+                grad_scores = (probs * (grad_probs - delta_row)).astype(halves)
+                grad_value = grad_value + jnp.dot(
+                    probs.astype(halves), grad_head, preferred_element_type=floats
+                )
+                grad_key = grad_key + jnp.dot(
+                    grad_scores, query_head, preferred_element_type=floats
+                )
+                rows = pl.ds(head * HD, HD)
+                dq[rows, pl.ds(query_at, block)] += jnp.dot(
+                    kt[rows, pl.ds(key_at, block)], grad_scores, preferred_element_type=floats
+                )
+            return (grad_key, grad_value)
+
+        zero = jnp.zeros((block, 2 * HD), floats)
+        grad_key, grad_value = lax.fori_loop(index, finish, one_query, (zero, zero))
+        dk[pl.ds(key_at, block), :] = grad_key
+        dv[pl.ds(key_at, block), :] = grad_value
+        return carry
+
+    lax.fori_loop(0, length // block, one_key, 0)
+
+    def turn_back(rows, content):
+        return (
+            content * cos_ref[rows, :]
+            - pltpu.roll(content, 8, 1) * up_ref[rows, :]
+            - pltpu.roll(content, 2 * HD - 8, 1) * down_ref[rows, :]
+        )
+
+    sums = [jnp.zeros((1, 2 * HD), floats)] * 3
+    for part in range(length // block):
+        rows = pl.ds(part * block, block)
+        parts = (
+            turn_back(rows, dq[:, rows].T),
+            turn_back(rows, dk[rows, :]),
+            dv[rows, :],
+        )
+        for kind in range(3):
+            sums[kind] = sums[kind] + jnp.sum(parts[kind], axis=0, keepdims=True)
+        qs[rows, :] = parts[0].astype(halves)
+        ks[rows, :] = parts[1].astype(halves)
+        vs[rows, :] = parts[2].astype(halves)
+    for kind in range(3):
+        bias_ref[kind : kind + 1, :] = sums[kind]
+
+        def write(ref, rows, content, kind=kind):
+            ref[kind, rows, :] = content
+
+        held = (qs, ks, vs)[kind]
+        fetch_rows(place_ref, out_own, out_other, lambda rows, held=held: held[rows, :], write)
+
+
+def qkv_kernel(rows_ref, weight_ref, bias_ref, cos_ref, up_ref, down_ref, out_ref):
+    floats = jnp.float32
+    width = 2 * HD
+    for part in range(2):
+        product = jnp.dot(
+            rows_ref[...],
+            weight_ref[:, part * 3 * width : (part + 1) * 3 * width],
+            preferred_element_type=floats,
+        )
+        for kind in range(3):
+            content = product[:, kind * width : (kind + 1) * width]
+            content = content + bias_ref[part * 3 + kind : part * 3 + kind + 1, :]
+            if kind < 2:
+                content = (
+                    content * cos_ref[...]
+                    + pltpu.roll(content, 8, 1) * up_ref[...]
+                    + pltpu.roll(content, width - 8, 1) * down_ref[...]
+                )
+            out_ref[part, kind] = content.astype(out_ref.dtype)
+
+
+def whole_specs(count):
+    return [pl.BlockSpec(memory_space=pltpu.VMEM)] * count
+
+
+def lane_tables(offset):
+    lane = jnp.arange(2 * HD, dtype=jnp.int32) % HD
+    halfway = ROT // 2
+    exponent = (lane % halfway).astype(jnp.float32) * (2.0 / ROT)
+    frequency = jnp.exp(-math.log(10000.0) * exponent)
+    angles = offset.astype(jnp.float32)[:, None] * frequency[None, :]
+    cosine, sine = (jnp.cos(angles), jnp.sin(angles))
+    cosine = jnp.where(lane < ROT, cosine, 1.0)
+    upper = jnp.where((lane >= halfway) & (lane < ROT), sine, 0.0)
+    lower = jnp.where(lane < halfway, -sine, 0.0)
+    return (cosine, upper, lower)
+
+
+def line_gather(own, at_z):
+    down, above = [own], [own]
+    for step in range(1, LINE):
+        down.append(
+            lax.ppermute(down[-1], "z", [(k, k - 1) for k in range(1, LINE - step + 1)])
+        )
+        above.append(
+            lax.ppermute(above[-1], "z", [(k, k + 1) for k in range(step - 1, LINE - 1)])
+        )
+    blocks = [own]
+    for step in range(1, LINE):
+        blocks.append(jnp.where(at_z + step < LINE, down[step], above[LINE - step]))
+    return jnp.concatenate(blocks + [flip(block, "c") for block in blocks], axis=0)
+
+
+def line_reduce(keep, send):
+    together = keep + flip(send, "c").astype(jnp.float32)
+    parts = together.reshape((LINE, QUARTER) + together.shape[1:])
+    down = above = None
+    for step in range(1, LINE):
+        falling, rising = parts[step], parts[LINE - step]
+        if down is not None:
+            falling, rising = falling + down.astype(jnp.float32), rising + above.astype(jnp.float32)
+        down = lax.ppermute(
+            falling.astype(jnp.bfloat16), "z", [(k, k - 1) for k in range(LINE - step, LINE)]
+        )
+        above = lax.ppermute(
+            rising.astype(jnp.bfloat16), "z", [(k, k + 1) for k in range(step)]
+        )
+    return parts[0] + down.astype(jnp.float32) + above.astype(jnp.float32)
+
+
+def line_trade(parts, at_z):
+    held = jnp.zeros_like(parts)
+    mine = lax.dynamic_index_in_dim(parts, at_z, 0, keepdims=True)
+    held = lax.dynamic_update_slice_in_dim(held, mine, at_z, 0)
+    for step in range(1, LINE):
+        going = lax.dynamic_index_in_dim(parts, lax.rem(at_z + step, LINE), 0, keepdims=True)
+        came = lax.ppermute(going, "z", [(k, (k + step) % LINE) for k in range(LINE)])
+        held = lax.dynamic_update_slice_in_dim(held, came, lax.rem(at_z + LINE - step, LINE), 0)
+    return held
+
+
+def widen(parts, at_z, first):
+    held = line_trade(parts, at_z)
+    held = held.reshape(held.shape[0] * held.shape[1], held.shape[2])
+    if first == "y":
+        held = jnp.concatenate([held, flip(held, "y")], axis=1)
+        return jnp.concatenate([held, flip(held, "x")], axis=0)
+    held = jnp.concatenate([held, flip(held, "x")], axis=0)
+    return jnp.concatenate([held, flip(held, "y")], axis=1)
+
+
+def narrow(total, at_z, first):
+    floats, halves = jnp.float32, jnp.bfloat16
+    half_rows, half_cols = total.shape[0] // 2, total.shape[1] // 2
+    if first == "x":
+        came = flip(total[half_rows:].astype(halves), "x").astype(floats)
+        total = total[:half_rows] + came
+        came = flip(total[:, half_cols:].astype(halves), "y").astype(floats)
+        total = total[:, :half_cols] + came
+    else:
+        came = flip(total[:, half_cols:].astype(halves), "y").astype(floats)
+        total = total[:, :half_cols] + came
+        came = flip(total[half_rows:].astype(halves), "x").astype(floats)
+        total = total[:half_rows] + came
+    parts = total.astype(halves).reshape(LINE, half_rows // LINE, half_cols)
+    return line_trade(parts, at_z)
+
+
+def block_device(
+    block_input,
+    doc_lengths,
+    ln1_gain,
+    ln1_bias,
+    w_qkv,
+    qkv_bias,
+    w_out,
+    ln2_gain,
+    ln2_bias,
+    w_gate_up,
+    w_down,
+    grad_y,
+):
+    floats, halves = jnp.float32, jnp.bfloat16
+    at_z, at_x, at_y, at_c = (lax.axis_index(name) for name in ("z", "x", "y", "c"))
+    model_width = block_input.shape[2]
+    shard_len = block_input.shape[1]
+    head_cols = w_out.shape[1]
+    hidden_cols = w_down.shape[1]
+    rows_owned = w_out.shape[0]
+    wide = -(-hidden_cols // (LINE * QUARTER)) * QUARTER
+    cut = head_cols // LINE
+    tokens = 2 * LINE * QUARTER
+
+    def features(content):
+        lead = content.shape[:-1]
+        split = content.reshape(lead + (LINE, 2, rows_owned))
+        near = lax.dynamic_index_in_dim(split, at_x, split.ndim - 2, keepdims=False)
+        far = lax.dynamic_index_in_dim(split, 1 - at_x, split.ndim - 2, keepdims=False)
+        flat = lead + (LINE * rows_owned,)
+        return jnp.concatenate([near.reshape(flat), far.reshape(flat)], axis=-1)
+
+    def plain_features(content):
+        lead = content.shape[:-1]
+        split = content.reshape(lead + (2, LINE, rows_owned))
+        even = jnp.where(at_x == 0, split[..., 0, :, :], split[..., 1, :, :])
+        odd = jnp.where(at_x == 0, split[..., 1, :, :], split[..., 0, :, :])
+        return jnp.stack([even, odd], axis=-2).reshape(lead + (model_width,))
+
+    def own_rows(content):
+        seq_rows = lax.dynamic_index_in_dim(content, at_y, 0, keepdims=False)
+        return features(lax.dynamic_slice_in_dim(seq_rows, at_c * QUARTER, QUARTER, 0))
+
+    def spread_output(content):
+        content = plain_features(content).astype(halves)
+        beside = flip(content, "c")
+        pair = jnp.concatenate(
+            [
+                jnp.where(at_c == 0, content, beside),
+                jnp.where(at_c == 0, beside, content),
+            ],
+            axis=0,
+        )
+        across = flip(pair, "y")
+        return jnp.stack(
+            [jnp.where(at_y == 0, pair, across), jnp.where(at_y == 0, across, pair)], axis=0
+        )
+
+    def quarters(matrix, size):
+        grown = jnp.pad(matrix, ((0, 0), (0, LINE * size - matrix.shape[1])))
+        return jnp.swapaxes(grown.reshape(matrix.shape[0], LINE, size), 0, 1)
+
+    part_qkv = jnp.concatenate([quarters(w_qkv[:, kind], cut) for kind in range(3)], axis=2)
+    part_out = quarters(w_out, cut)
+    part_gate_up = jnp.concatenate([quarters(w_gate_up[:, kind], wide) for kind in range(2)], axis=2)
+    part_down = quarters(w_down, wide)
+
+    lengths = lax.dynamic_index_in_dim(doc_lengths, at_y, 0, keepdims=False)
+    doc_ends = jnp.cumsum(lengths)
+
+    def begin_of(places):
+        passed = (places[:, None] >= doc_ends[None, :]).astype(jnp.int32)
+        return jnp.sum(passed * lengths[None, :], axis=-1)
+
+    length = 2 * tokens
+    block = 256
+    all_places = jnp.arange(length, dtype=jnp.int32)
+    begin_all = begin_of(all_places)
+    block_begin = begin_all.reshape(length // block, block)[:, 0]
+    first_block = block_begin // block
+    block_ends = (jnp.arange(length // block, dtype=jnp.int32) + 1) * block
+    last_block = jnp.sum((block_begin[None, :] < block_ends[:, None]).astype(jnp.int32), axis=1)
+    rel = jnp.arange(tokens, dtype=jnp.int32)
+    rel_c, rel_z, rel_r = rel // (LINE * QUARTER), (rel // QUARTER) % LINE, rel % QUARTER
+    places = (
+        ((at_z + rel_z) % LINE) * (2 * shard_len)
+        + at_x * shard_len
+        + jnp.abs(at_c - rel_c) * QUARTER
+        + rel_r
+    )
+    row_tables = lane_tables(places - begin_of(places))
+    all_tables = lane_tables(all_places - begin_all)
+    place = jnp.stack([at_z, at_x, at_c]).astype(jnp.int32)
+
+    input_wide = own_rows(block_input).astype(floats)
+    gain1, shift1, gain2, shift2 = (features(v) for v in (ln1_gain, ln1_bias, ln2_gain, ln2_bias))
+    first_norm, normed1, inverse1 = layer_norm(input_wide, gain1, shift1)
+    first_low = line_gather(first_norm.astype(halves), at_z)
+    full_qkv = widen(part_qkv, at_z, "y")
+    full_out = widen(part_out, at_z, "y")
+    full_gate_up = widen(part_gate_up, at_z, "x")
+    full_down = widen(part_down, at_z, "y")
+    grad_rows = line_gather(own_rows(grad_y), at_z)
+
+    own_bias = lax.dynamic_slice_in_dim(qkv_bias, at_z * cut, cut, 1)
+    bias_parts = jnp.concatenate([own_bias, flip(own_bias, "y")], axis=0)
+    projected = pl.pallas_call(
+        qkv_kernel,
+        out_shape=jax.ShapeDtypeStruct((2, 3, tokens, cut), halves),
+        in_specs=whole_specs(6),
+        out_specs=pl.BlockSpec(memory_space=pltpu.VMEM),
+        name="project",
+    )(first_low, full_qkv, bias_parts, *row_tables)
+    crossed = at_x ^ at_y
+    qkv_own = lax.dynamic_index_in_dim(projected, crossed, 0, keepdims=False)
+    qkv_other = flip(lax.dynamic_index_in_dim(projected, 1 - crossed, 0, keepdims=False), "x")
+
+    smem = pl.BlockSpec(memory_space=pltpu.SMEM)
+    half_shape = jax.ShapeDtypeStruct((tokens, cut), halves)
+    out_own, out_other, lse = pl.pallas_call(
+        functools.partial(attend_kernel, block),
+        out_shape=(half_shape, half_shape, jax.ShapeDtypeStruct((2, length), floats)),
+        in_specs=[smem, smem] + whole_specs(3),
+        out_specs=tuple(whole_specs(3)),
+        scratch_shapes=[pltpu.VMEM((length, cut), halves)] * 3
+        + [pltpu.VMEM((cut, length), halves), pltpu.VMEM((cut, length), floats)],
+        name="attend",
+    )(place, first_block, begin_all[None, :], qkv_own, qkv_other)
+
+    def join_heads(own, other):
+        near = jnp.where(crossed == 0, own, other)
+        far = jnp.where(crossed == 0, other, own)
+        return jnp.concatenate([near, far], axis=-1)
+
+    attended = join_heads(out_own, flip(out_other, "x"))
+    half = tokens // 2
+
+    def spread(left, right):
+        send = lax.dot_general(
+            left[half:], right, (((1,), (1,)), ((), ())), preferred_element_type=floats
+        ).astype(halves)
+        keep = lax.dot_general(
+            left[:half], right, (((1,), (1,)), ((), ())), preferred_element_type=floats
+        )
+        return line_reduce(keep, send)
+
+    residual = input_wide + spread(attended, full_out)
+    second_norm, normed2, inverse2 = layer_norm(residual, gain2, shift2)
+    second_low = line_gather(second_norm.astype(halves), at_z)
+    gate_up = jnp.dot(second_low, full_gate_up, preferred_element_type=floats)
+    gate_up = gate_up.reshape(tokens, 2, 2, wide)
+    gate, up_part = gate_up[:, :, 0], gate_up[:, :, 1]
+    sigmoid_gate = jax.nn.sigmoid(gate)
+    hidden = (gate * sigmoid_gate * up_part).astype(halves).reshape(tokens, 2 * wide)
+    grad_hidden = jnp.dot(grad_rows, full_down, preferred_element_type=floats)
+    grad_hidden = grad_hidden.reshape(tokens, 2, wide)
+    grad_gate = grad_hidden * up_part * sigmoid_gate * (1.0 + gate * (1.0 - sigmoid_gate))
+    grad_upper = grad_hidden * gate * sigmoid_gate
+    grad_gate_up = jnp.stack([grad_gate, grad_upper], axis=2).astype(halves)
+    grad_gate_up = grad_gate_up.reshape(tokens, 4 * wide)
+
+    grad_second = spread(grad_gate_up, full_gate_up)
+    block_output = spread_output(residual + spread(hidden, full_down))
+
+    def product(left_rows, right_rows):
+        return lax.dot_general(
+            left_rows, right_rows, (((0,), (0,)), ((), ())), preferred_element_type=floats
+        )
+
+    grad_own = own_rows(grad_y).astype(floats)
+    g_gate_up = narrow(product(second_low, grad_gate_up), at_z, "x")
+    g_down = narrow(product(grad_rows, hidden), at_z, "y")
+    grad_residual = grad_own + norm_back(grad_second, normed2, inverse2, gain2)
+    low_own = grad_residual.astype(halves)
+    residual_low = line_gather(low_own, at_z)
+    grad_attended = jnp.dot(residual_low, full_out, preferred_element_type=floats).astype(halves)
+    grad_near, grad_far = grad_attended[:, :cut], grad_attended[:, cut:]
+    grad_mine = jnp.where(crossed == 0, grad_near, grad_far)
+    grad_their = flip(jnp.where(crossed == 0, grad_far, grad_near), "x")
+
+    qkv_shape = jax.ShapeDtypeStruct((3, tokens, cut), halves)
+    back_own, back_other, bias_sums = pl.pallas_call(
+        functools.partial(attend_back_kernel, block),
+        out_shape=(qkv_shape, qkv_shape, jax.ShapeDtypeStruct((3, cut), floats)),
+        in_specs=[smem, smem] + whole_specs(11),
+        out_specs=tuple(whole_specs(3)),
+        scratch_shapes=[
+            pltpu.VMEM((length, cut), halves),
+            pltpu.VMEM((length, cut), halves),
+            pltpu.VMEM((cut, length), halves),
+            pltpu.VMEM((length, cut), halves),
+            pltpu.VMEM((length, cut), halves),
+            pltpu.VMEM((length, cut), halves),
+            pltpu.VMEM((cut, length), floats),
+            pltpu.VMEM((length, cut), floats),
+            pltpu.VMEM((length, cut), floats),
+            pltpu.VMEM((16, length), floats),
+        ],
+        name="attend_back",
+    )(
+        place,
+        last_block,
+        begin_all[None, :],
+        qkv_own,
+        qkv_other,
+        out_own,
+        out_other,
+        grad_mine,
+        grad_their,
+        lse,
+        *all_tables,
+    )
+    came_back = flip(back_other, "x")
+    near = jnp.where(crossed == 0, back_own, came_back)
+    far = jnp.where(crossed == 0, came_back, back_own)
+    grad_qkv = jnp.concatenate([near[0], near[1], near[2], far[0], far[1], far[2]], axis=1)
+    grad_first = spread(grad_qkv, full_qkv)
+    g_qkv = narrow(product(first_low, grad_qkv), at_z, "y")
+    g_out = narrow(product(residual_low, attended), at_z, "y")
+    grad_input = spread_output(grad_residual + norm_back(grad_first, normed1, inverse1, gain1))
+
+    sums = jnp.stack(
+        [
+            jnp.sum(grad_first * normed1, axis=0),
+            jnp.sum(grad_first, axis=0),
+            jnp.sum(grad_second * normed2, axis=0),
+            jnp.sum(grad_second, axis=0),
+        ]
+    )
+    sums = lax.psum(plain_features(sums), ("z", "x", "y", "c"))
+    bias_all = lax.all_gather(bias_sums, ("z", "x", "y"), axis=0)
+    bias_all = jnp.sum(bias_all.reshape(LINE, 2, 2, 3, cut), axis=2)
+    bias_all = lax.dynamic_index_in_dim(bias_all, at_y, 1, keepdims=False)
+    g_bias = jnp.swapaxes(bias_all, 0, 1).reshape(3, head_cols)
+
+    def columns(parts, offset, size, count):
+        matrix = jnp.swapaxes(parts[:, :, offset : offset + size], 0, 1)
+        return matrix.reshape(rows_owned, LINE * size)[:, :count].astype(floats)
+
+    grad_w_qkv = jnp.stack([columns(g_qkv, kind * cut, cut, head_cols) for kind in range(3)], axis=1)
+    grad_w_gate_up = jnp.stack(
+        [columns(g_gate_up, kind * wide, wide, hidden_cols) for kind in range(2)], axis=1
+    )
+    return (
+        block_output,
+        grad_input,
+        sums[0],
+        sums[1],
+        grad_w_qkv,
+        g_bias,
+        columns(g_out, 0, cut, head_cols),
+        sums[2],
+        sums[3],
+        grad_w_gate_up,
+        columns(g_down, 0, wide, hidden_cols),
+    )
+
+
 def solution(mesh):
+    sizes = (mesh.shape["fsdp"], mesh.shape["tp"])
+    if sizes == (2 * LINE, 4):
+        names = ("z", "x", "y", "c")
+        rows, cols = ("z", "x"), ("y", "c")
+        mesh = Mesh(mesh.devices.reshape(LINE, 2, 2, 2), names)
+        device_step = block_device
+    else:
+        rows, cols = "fsdp", "tp"
+        device_step = on_device
     placed = (
-        P(None, "fsdp", None),
+        P(None, rows, None),
         P(),
         P(),
         P(),
-        P("fsdp", None, "tp"),
-        P(None, "tp"),
-        P("fsdp", "tp"),
+        P(rows, None, cols),
+        P(None, cols),
+        P(rows, cols),
         P(),
         P(),
-        P("fsdp", None, "tp"),
-        P("fsdp", "tp"),
-        P(None, "fsdp", None),
+        P(rows, None, cols),
+        P(rows, cols),
+        P(None, rows, None),
     )
     return jax.shard_map(
-        on_device,
+        device_step,
         mesh=mesh,
         in_specs=placed,
         out_specs=(
-            P(None, "fsdp", None),
-            P(None, "fsdp", None),
+            P(None, rows, None),
+            P(None, rows, None),
             P(),
             P(),
-            P("fsdp", None, "tp"),
-            P(None, "tp"),
-            P("fsdp", "tp"),
+            P(rows, None, cols),
+            P(None, cols),
+            P(rows, cols),
             P(),
             P(),
-            P("fsdp", None, "tp"),
-            P("fsdp", "tp"),
+            P(rows, None, cols),
+            P(rows, cols),
         ),
         check_vma=False,
     )

time: 1820 us -> 1010 us (0.55)
  waiting for transfers between devices: 1200 us -> 411 us
  starting transfers between devices: 1.54 us -> 174 us
  matrix products: 208 us -> 69.9 us
  local copies, waits for them, and re-layouts: 204 us -> 95.5 us
  Pallas kernels: 0 us -> 65.3 us
  blocking collectives: 34.6 us -> 96.2 us
  other arithmetic: 126 us -> 84.9 us
    reduce_scatter x5 -> x0, waiting for transfers between devices: 526 us -> none  [the longest x1 359 us: on_device(): lax.psum_scatter(jnp.concatenate([product(first_low, grad_qkv), product(r...]
    all_gather x8 -> x0, waiting for transfers between devices: 503 us -> none  [the longest x1 159 us: fetch_weights(): lax.all_gather(w_gate_up, 'fsdp', axis=0, tiled=True)]
    ppermute x0 -> x117, waiting for transfers between devices: none -> 411 us  [the longest x45 164 us: flip(): return lax.ppermute(block, axis, FLIP)]
    ppermute x0 -> x117, starting transfers between devices: none -> 174 us  [the longest x24 48.8 us: line_trade(): lax.ppermute(going, 'z', [(k, (k + step) % LINE) for k in range(LINE)])]
    psum x4 -> x0, waiting for transfers between devices: 173 us -> none  [the longest x2 69.9 us: on_device(): lax.psum(attn_part.astype(jnp.bfloat16), 'tp').astype(jnp.float32)]
    dot_general x72 -> x11, matrix products: 184 us -> 49.7 us  [the longest x4 17.3 us: spread(): lax.dot_general(left[half:], right, (((1,), (1,)), ((), ())), preferred_e...]
    pallas_call x0 -> x3, Pallas kernels: none -> 65.3 us  [the longest x1 28.3 us: block_device(): pl.pallas_call(functools.partial(attend_kernel, block), out_shape=(half_s...]
    reduce_sum x30 -> x6, other arithmetic: 47.6 us -> 4.53 us  [the longest x1 2.01 us: block_device(): jnp.sum(grad_first * normed1, axis=0)]
  transfers between devices with their start and end apart: 17 -> 117, of which waited for: 15 -> 42; matrix products, arithmetic and copies ran while one was open for 14% -> 18% of each run, Pallas kernels for 0% -> 7%
where the time goes in v1:
time: 1010 us; the launch traced here: 1000 us
  waiting for transfers between devices  411 us (41%)
  starting transfers between devices  174 us (17%)
  blocking collectives  96.2 us (10%)
  local copies, waits for them, and re-layouts  95.5 us (9%)
  other arithmetic  84.9 us (8%)
  matrix products  69.9 us (7%)
  Pallas kernels  65.3 us (6%)
    ppermute x45, waiting for transfers between devices, flip(): return lax.ppermute(block, axis, FLIP)  164 us
    ppermute x24, waiting for transfers between devices, line_trade(): lax.ppermute(going, 'z', [(k, (k + step) % LINE) for k in range(LINE)])  99.6 us
    ppermute x12, waiting for transfers between devices, line_gather(): lax.ppermute(above[-1], 'z', [(k, k + 1) for k in range(step - 1, LINE -...  78.7 us
    psum x1, blocking collectives, block_device(): sums = lax.psum(plain_features(sums), ('z', 'x', 'y', 'c'))  57.7 us
    ppermute x12, waiting for transfers between devices, line_reduce(): lax.ppermute(falling.astype(jnp.bfloat16), 'z', [(k, k - 1) for k in rang...  56.3 us
    ppermute x24, starting transfers between devices, line_trade(): lax.ppermute(going, 'z', [(k, (k + step) % LINE) for k in range(LINE)])  48.8 us
    all_gather x1, blocking collectives, block_device(): bias_all = lax.all_gather(bias_sums, ('z', 'x', 'y'), axis=0)  38.5 us
    ppermute x45, starting transfers between devices, flip(): return lax.ppermute(block, axis, FLIP)  33.3 us
  transfers between devices with their start and end apart: 117, of which 42 were waited for; matrix products, arithmetic and copies ran while one was open for 18% of the time, Pallas kernels for 7%

profile of v1, /device:TPU:24, one launch (start us, length us, event | category | flops | bytes accessed | tf_op | source)
XLA Modules:
  0.0 999.7 jit_solution(16636744813910711884)
XLA Ops:
  8.4 5.4 collective-permute-start
  19.6 13.6 %collective-permute-done.10 = bf16[1,256,384]{2,1,0:T(8,128)(2,1)S(1)} collective-permute-done((bf16[1,256,384]{2,1,0:T(8,128)(2,1)S(1)}, bf16[1,256,384]{2,1,0:T(8,128)(2,1)S(1)}, u32[]{:S(2)}, u32[]{:S(2)}) %collective-permute-start.10) | collective-permute-done | bytes 196640 | tf_op jit(solution)/shard_map/ppermute | solution.py:734
  48.3 4.9 collective-permute-done.2
  56.8 13.2 %collective-permute-done.18 = bf16[1,256,128]{2,1,0:T(8,128)(2,1)S(1)} collective-permute-done((bf16[1,256,128]{2,1,0:T(8,128)(2,1)S(1)}, bf16[1,256,128]{2,1,0:T(8,128)(2,1)S(1)}, u32[]{:S(2)}, u32[]{:S(2)}) %collective-permute-start.18) | collective-permute-done | bytes 65568 | tf_op jit(solution)/shard_map/ppermute | solution.py:734
  82.7 22.7 %collective-permute-done.14 = bf16[1024,768]{1,0:T(8,128)(2,1)S(1)} collective-permute-done((bf16[1024,768]{1,0:T(8,128)(2,1)S(1)}, bf16[1024,768]{1,0:T(8,128)(2,1)S(1)}, u32[]{:S(2)}, u32[]{:S(2)}) %collective-permute-start.14) | collective-permute-done | bytes 1572896 | tf_op jit(solution)/shard_map/ppermute | solution.py:427
  107.6 9.5 project.1
  124.2 4.2 collective-permute-done.21
  130.4 9.6 collective-permute-done.16.other_ref
  140.9 28.3 %attend.1 = (bf16[1024,128]{1,0:T(8,128)(2,1)}, bf16[1024,128]{1,0:T(8,128)(2,1)}, f32[2,2048]{1,0:T(2,128)}) custom-call(s32[3]{0:T(128)} %pad_add_fusion.place_ref, s32[8]{0:T(128)} %and_select_fusion.2.first_ref, s32[1,2048]{1,0:T(1,128)} %bitcast.326, bf16[3,1024,128]{2,1,0:T(8,128)(2,1)} %get-tuple-element.184.own_ref, bf16[3,1024,128]{2,1,0:T(8,128)(2,1)} %copy-done.25), custom_call_target="tpu_custom_call" | custom-call | tf_op jit(solution)/shard_map/attend/pallas_call | solution.py:886
  191.9 5.9 fusion.29
  208.0 7.4 collective-permute-done.24
  215.6 4.4 collective-permute-start.59
  222.0 7.4 collective-permute-done.40
  232.9 11.3 %collective-permute-done.41 = bf16[1,256,768]{2,1,0:T(8,128)(2,1)S(1)} collective-permute-done((bf16[1,256,768]{2,1,0:T(8,128)(2,1)S(1)}, bf16[1,256,768]{2,1,0:T(8,128)(2,1)S(1)}, u32[]{:S(2)}, u32[]{:S(2)}) %collective-permute-start.41) | collective-permute-done | bytes 393248 | tf_op jit(solution)/shard_map/ppermute | solution.py:734
  248.6 5.5 collective-permute-done.25
  255.7 6.5 collective-permute-done.48
  263.7 13.6 %collective-permute-done.62 = bf16[128,2048]{1,0:T(8,128)(2,1)S(1)} collective-permute-done((bf16[128,2048]{1,0:T(8,128)(2,1)S(1)}, bf16[128,2048]{1,0:T(8,128)(2,1)S(1)}, u32[]{:S(2)}, u32[]{:S(2)}) %collective-permute-start.62) | collective-permute-done | bytes 524320 | tf_op jit(solution)/shard_map/ppermute | solution.py:703
  281.6 8.2 collective-permute-done.26
  289.7 5.2 collective-permute-done.29
  301.4 5.1 collective-permute-start.30
  306.5 7.5 collective-permute-done.31
  319.2 13.6 %collective-permute-done.32 = bf16[128,2048]{1,0:T(8,128)(2,1)} collective-permute-done((bf16[128,2048]{1,0:T(8,128)(2,1)S(1)}, bf16[128,2048]{1,0:T(8,128)(2,1)}, u32[]{:S(2)}, u32[]{:S(2)}) %collective-permute-start.32) | collective-permute-done | bytes 524320 | tf_op jit(solution)/shard_map/ppermute | solution.py:703
  334.1 5.2 fusion.94
  343.7 4.0 collective-permute-done.33
  356.8 28.5 %collective-permute-done.44 = bf16[2048,768]{1,0:T(8,128)(2,1)} collective-permute-done((bf16[2048,768]{1,0:T(8,128)(2,1)}, bf16[2048,768]{1,0:T(8,128)(2,1)}, u32[]{:S(2)}, u32[]{:S(2)}) %collective-permute-start.44) | collective-permute-done | bytes 3145760 | tf_op jit(solution)/shard_map/ppermute | solution.py:427
  385.4 9.9 fusion.95
  401.1 5.0 fusion.1
  409.6 4.0 fusion.7
  423.1 5.4 fusion.112
  433.7 4.4 convolution_convert_fusion.3
  440.2 7.8 convolution_convert_fusion.2
  448.4 9.6 fusion.111
  472.1 6.1 convert_add_fusion.1
  478.4 7.7 collective-permute-start.70
  486.1 4.2 convert_add_fusion.2
  490.3 61.9 %collective-permute-done.113 = bf16[1024,384]{1,0:T(8,128)(2,1)} collective-permute-done((bf16[1024,384]{1,0:T(8,128)(2,1)}, bf16[1024,384]{1,0:T(8,128)(2,1)}, u32[]{:S(2)}, u32[]{:S(2)}) %collective-permute-start.113) | collective-permute-done | bytes 786464 | tf_op jit(solution)/shard_map/ppermute | solution.py:427
  553.7 7.8 collective-permute-start.115
  562.0 3.6 collective-permute-start.51
  565.6 5.6 collective-permute-done.114
  572.7 3.6 collective-permute-start.116
  576.4 27.8 %collective-permute-done.116 = bf16[1,256,384]{2,1,0:T(8,128)(2,1)S(1)} collective-permute-done((bf16[1,256,384]{2,1,0:T(8,128)(2,1)S(1)}, bf16[1,256,384]{2,1,0:T(8,128)(2,1)S(1)}, u32[]{:S(2)}, u32[]{:S(2)}) %collective-permute-start.116) | collective-permute-done | bytes 196640 | tf_op jit(solution)/shard_map/ppermute | solution.py:734
  607.2 10.7 %collective-permute-done.71 = bf16[128,2048]{1,0:T(8,128)(2,1)S(1)} collective-permute-done((bf16[128,2048]{1,0:T(8,128)(2,1)S(1)}, bf16[128,2048]{1,0:T(8,128)(2,1)S(1)}, u32[]{:S(2)}, u32[]{:S(2)}) %collective-permute-start.71) | collective-permute-done | bytes 524320 | tf_op jit(solution)/shard_map/ppermute | solution.py:719
  619.6 7.8 collective-permute-done.52
  628.5 4.4 collective-permute-start.53
  638.4 3.7 slice_add_fusion
  645.4 8.9 collective-permute-done.72
  656.0 6.3 collective-permute-done.56
  669.3 10.7 %collective-permute-start.76 = (bf16[128,2048]{1,0:T(8,128)(2,1)S(1)}, bf16[128,2048]{1,0:T(8,128)(2,1)}, u32[]{:S(2)}, u32[]{:S(2)}) collective-permute-start(bf16[128,2048]{1,0:T(8,128)(2,1)S(1)} %get-tuple-element.116), channel_id=1, source_target_pairs={{8,0},{16,8},{24,16},{9,1},{17,9},{25,17},{10,2},{18,10},{26,18},{... | collective-permute-start | bytes 1572872 | tf_op jit(solution)/shard_map/ppermute | solution.py:700
  680.0 8.2 collective-permute-done.77
  692.9 11.2 %collective-permute-done.78 = bf16[128,2048]{1,0:T(8,128)(2,1)S(1)} collective-permute-done((bf16[128,2048]{1,0:T(8,128)(2,1)}, bf16[128,2048]{1,0:T(8,128)(2,1)S(1)}, u32[]{:S(2)}, u32[]{:S(2)}) %collective-permute-start.78) | collective-permute-done | bytes 524320 | tf_op jit(solution)/shard_map/ppermute | solution.py:703
  712.0 15.4 %collective-permute-done.79 = bf16[128,2048]{1,0:T(8,128)(2,1)S(1)} collective-permute-done((bf16[128,2048]{1,0:T(8,128)(2,1)S(1)}, bf16[128,2048]{1,0:T(8,128)(2,1)S(1)}, u32[]{:S(2)}, u32[]{:S(2)}) %collective-permute-start.79) | collective-permute-done | bytes 524320 | tf_op jit(solution)/shard_map/ppermute | solution.py:703
  738.2 10.4 %collective-permute-done.109 = bf16[1,256,768]{2,1,0:T(8,128)(2,1)S(1)} collective-permute-done((bf16[1,256,768]{2,1,0:T(8,128)(2,1)S(1)}, bf16[1,256,768]{2,1,0:T(8,128)(2,1)S(1)}, u32[]{:S(2)}, u32[]{:S(2)}) %collective-permute-start.109) | collective-permute-done | bytes 393248 | tf_op jit(solution)/shard_map/ppermute | solution.py:734
  752.5 27.5 %attend_back.1 = (bf16[3,1024,128]{2,1,0:T(8,128)(2,1)}, bf16[3,1024,128]{2,1,0:T(8,128)(2,1)}, f32[3,128]{1,0:T(4,128)}) custom-call(s32[3]{0:T(128)} %pad_add_fusion.place_ref, s32[8]{0:T(128)} %convert_reduce_fusion.1.last_ref, s32[1,2048]{1,0:T(1,128)} %bitcast.327, bf16[3,1024,128]{2,1,0:T(8,128)(2,1)} %get-tuple-element.184.own_ref, ...), custom_call_target="tpu_custom_call" | custom-call | tf_op jit(solution)/shard_map/attend_back/pallas_call | solution.py:948
  786.1 3.8 copy.385
  791.9 7.7 collective-permute-done.87
  806.9 38.5 %all-gather.1 = f32[16,3,128]{2,1,0:T(4,128)S(1)} all-gather(f32[1,3,128]{2,1,0:T(4,128)S(1)} %bitcast.345), channel_id=2, replica_groups=mesh['z'=4,'x'=2,'y'=2,'c'=2] {'z','x','y'}, dimensions={0}, use_global_device_ids=true | all-gather | bytes 26112 | tf_op jit(solution)/shard_map/all_gather | solution.py:997
  845.5 4.0 collective-permute-start.103
  849.6 3.8 fusion.110
  866.7 17.0 %collective-permute-done.97 = bf16[2048,384]{1,0:T(8,128)(2,1)S(1)} collective-permute-done((bf16[2048,384]{1,0:T(8,128)(2,1)S(1)}, bf16[2048,384]{1,0:T(8,128)(2,1)S(1)}, u32[]{:S(2)}, u32[]{:S(2)}) %collective-permute-start.97) | collective-permute-done | bytes 1572896 | tf_op jit(solution)/shard_map/ppermute | solution.py:427
  885.8 5.8 collective-permute-done.90
  893.5 4.1 collective-permute-done.98
  908.4 10.0 collective-permute-start.101
  920.9 6.0 collective-permute-done.101
  937.8 57.7 %psum.7 = f32[4,2048]{1,0:T(4,128)S(1)} all-reduce(f32[4,2048]{1,0:T(4,128)S(1)} %reshape.609), channel_id=1, replica_groups=mesh['z'=4,'x'=2,'y'=2,'c'=2] {'z','x','y','c'}, use_global_device_ids=true, to_apply=%region_16.17 | all-reduce | flops 8192 | bytes 65536 | tf_op jit(solution)/shard_map/psum | solution.py:996
  (642 shorter events, 287.2 us)
Async XLA Ops:
  7.1 70.8 %collective-permute-start.6 = (bf16[128,2048]{1,0:T(8,128)(2,1)}, bf16[128,2048]{1,0:T(8,128)(2,1)}, u32[]{:S(2)}, u32[]{:S(2)}) collective-permute-start(bf16[128,2048]{1,0:T(8,128)(2,1)} %get-tuple-element.142), channel_id=1, source_target_pairs={{0,1},{1,0},{2,3},{3,2},{4,5},{5,4},{6,7},{7,6},{8,9},{9,8},{10,11... | collective-permute-start | bytes 1572872 | tf_op jit(solution)/shard_map/ppermute | solution.py:427
  7.1 29.6 %collective-permute-start.1 = (bf16[128,2048]{1,0:T(8,128)(2,1)}, bf16[128,2048]{1,0:T(8,128)(2,1)}, u32[]{:S(2)}, u32[]{:S(2)}) collective-permute-start(bf16[128,2048]{1,0:T(8,128)(2,1)} %get-tuple-element.142), channel_id=1, source_target_pairs={{0,8},{8,16},{16,24},{1,9},{9,17},{17,25},{2,10},{10,18},{18,26},{... | collective-permute-start | bytes 1572872 | tf_op jit(solution)/shard_map/ppermute | solution.py:703
  8.4 38.4 %collective-permute-start = (bf16[128,2048]{1,0:T(8,128)(2,1)}, bf16[128,2048]{1,0:T(8,128)(2,1)}, u32[]{:S(2)}, u32[]{:S(2)}) collective-permute-start(bf16[128,2048]{1,0:T(8,128)(2,1)} %get-tuple-element.142), channel_id=1, source_target_pairs={{8,0},{16,8},{24,16},{9,1},{17,9},{25,17},{10,2},{18,10},{26,18},{... | collective-permute-start | bytes 1572872 | tf_op jit(solution)/shard_map/ppermute | solution.py:700
  14.5 24.4 %collective-permute-start.11 = (bf16[1,256,384]{2,1,0:T(8,128)(2,1)S(1)}, bf16[1,256,384]{2,1,0:T(8,128)(2,1)}, u32[]{:S(2)}, u32[]{:S(2)}) collective-permute-start(bf16[1,256,384]{2,1,0:T(8,128)(2,1)S(1)} %get-tuple-element.208), channel_id=1, source_target_pairs={{0,16},{8,24},{16,0},{24,8},{1,17},{9,25},{17,1},{25,9},{2,18},{10... | collective-permute-start | bytes 589832 | tf_op jit(solution)/shard_map/ppermute | solution.py:734
  42.1 27.9 %collective-permute-start.13 = (bf16[1024,384]{1,0:T(8,128)(2,1)S(1)}, bf16[1024,384]{1,0:T(8,128)(2,1)S(1)}, u32[]{:S(2)}, u32[]{:S(2)}) collective-permute-start(bf16[1024,384]{1,0:T(8,128)(2,1)S(1)} %bitcast.276), channel_id=1, source_target_pairs={{0,2},{2,0},{1,3},{3,1},{4,6},{6,4},{5,7},{7,5},{8,10},{10,8},{9,1... | collective-permute-start | bytes 2359304 | tf_op jit(solution)/shard_map/ppermute | solution.py:427
  46.8 24.9 %collective-permute-start.4 = (bf16[128,2048]{1,0:T(8,128)(2,1)}, bf16[128,2048]{1,0:T(8,128)(2,1)}, u32[]{:S(2)}, u32[]{:S(2)}) collective-permute-start(bf16[128,2048]{1,0:T(8,128)(2,1)} %collective-permute-done), channel_id=1, source_target_pairs={{8,0},{16,8},{9,1},{17,9},{10,2},{18,10},{11,3},{19,11},{12,4},{20... | collective-permute-start | bytes 1572872 | tf_op jit(solution)/shard_map/ppermute | solution.py:700
  53.1 19.2 %collective-permute-start.3 = (bf16[128,2048]{1,0:T(8,128)(2,1)S(1)}, bf16[128,2048]{1,0:T(8,128)(2,1)}, u32[]{:S(2)}, u32[]{:S(2)}) collective-permute-start(bf16[128,2048]{1,0:T(8,128)(2,1)S(1)} %collective-permute-done.2), channel_id=1, source_target_pairs={{16,24},{17,25},{18,26},{19,27},{20,28},{21,29},{22,30},{23,31}} | collective-permute-start | bytes 1572872 | tf_op jit(solution)/shard_map/ppermute | solution.py:703
  69.9 51.1 %collective-permute-start.19 = (bf16[1,256,128]{2,1,0:T(8,128)(2,1)S(1)}, bf16[1,256,128]{2,1,0:T(8,128)(2,1)S(1)}, u32[]{:S(2)}, u32[]{:S(2)}) collective-permute-start(bf16[1,256,128]{2,1,0:T(8,128)(2,1)S(1)} %bitcast.329), channel_id=1, source_target_pairs={{0,16},{8,24},{16,0},{24,8},{1,17},{9,25},{17,1},{25,9},{2,18},{10... | collective-permute-start | bytes 196616 | tf_op jit(solution)/shard_map/ppermute | solution.py:734
  70.1 35.3 %collective-permute-start.14 = (bf16[1024,768]{1,0:T(8,128)(2,1)S(1)}, bf16[1024,768]{1,0:T(8,128)(2,1)S(1)}, u32[]{:S(2)}, u32[]{:S(2)}) collective-permute-start(bf16[1024,768]{1,0:T(8,128)(2,1)S(1)} %pad_maximum_fusion.6), channel_id=1, source_target_pairs={{0,4},{4,0},{1,5},{5,1},{2,6},{6,2},{3,7},{7,3},{8,12},{12,8},{9,1... | collective-permute-start | bytes 4718600 | tf_op jit(solution)/shard_map/ppermute | solution.py:427
  79.8 41.2 %collective-permute-start.20 = (bf16[1,256,128]{2,1,0:T(8,128)(2,1)S(1)}, bf16[1,256,128]{2,1,0:T(8,128)(2,1)}, u32[]{:S(2)}, u32[]{:S(2)}) collective-permute-start(bf16[1,256,128]{2,1,0:T(8,128)(2,1)S(1)} %bitcast.328), channel_id=1, source_target_pairs={{0,24},{8,0},{16,8},{24,16},{1,25},{9,1},{17,9},{25,17},{2,26},{10... | collective-permute-start | bytes 196616 | tf_op jit(solution)/shard_map/ppermute | solution.py:734
  119.6 20.4 %collective-permute-start.16 = (bf16[3,1024,128]{2,1,0:T(8,128)(2,1)S(1)}, bf16[3,1024,128]{2,1,0:T(8,128)(2,1)S(1)}, u32[]{:S(2)}, u32[]{:S(2)}) collective-permute-start(bf16[3,1024,128]{2,1,0:T(8,128)(2,1)S(1)} %get-tuple-element.183), channel_id=1, source_target_pairs={{0,4},{4,0},{1,5},{5,1},{2,6},{6,2},{3,7},{7,3},{8,12},{12,8},{9,1... | collective-permute-start | bytes 2359304 | tf_op jit(solution)/shard_map/ppermute | solution.py:427
  129.3 50.7 %collective-permute-start.22 = (bf16[1024,256]{1,0:T(8,128)(2,1)}, bf16[1024,256]{1,0:T(8,128)(2,1)}, u32[]{:S(2)}, u32[]{:S(2)}) collective-permute-start(bf16[1024,256]{1,0:T(8,128)(2,1)} %pad_maximum_fusion.15), channel_id=1, source_target_pairs={{0,4},{4,0},{1,5},{5,1},{2,6},{6,2},{3,7},{7,3},{8,12},{12,8},{9,1... | collective-permute-start | bytes 1572872 | tf_op jit(solution)/shard_map/ppermute | solution.py:427
  172.6 30.7 %collective-permute-start.45 = (bf16[1,256,384]{2,1,0:T(8,128)(2,1)}, bf16[1,256,384]{2,1,0:T(8,128)(2,1)}, u32[]{:S(2)}, u32[]{:S(2)}) collective-permute-start(bf16[1,256,384]{2,1,0:T(8,128)(2,1)} %bitcast.40), channel_id=1, source_target_pairs={{0,8},{8,16},{16,24},{24,0},{1,9},{9,17},{17,25},{25,1},{2,10},{10... | collective-permute-start | bytes 589832 | tf_op jit(solution)/shard_map/ppermute | solution.py:734
  174.9 30.7 %collective-permute-start.46 = (bf16[1,256,384]{2,1,0:T(8,128)(2,1)}, bf16[1,256,384]{2,1,0:T(8,128)(2,1)}, u32[]{:S(2)}, u32[]{:S(2)}) collective-permute-start(bf16[1,256,384]{2,1,0:T(8,128)(2,1)} %bitcast.41), channel_id=1, source_target_pairs={{0,16},{8,24},{16,0},{24,8},{1,17},{9,25},{17,1},{25,9},{2,18},{10... | collective-permute-start | bytes 589832 | tf_op jit(solution)/shard_map/ppermute | solution.py:734
  176.8 38.7 %collective-permute-start.47 = (bf16[1,256,384]{2,1,0:T(8,128)(2,1)}, bf16[1,256,384]{2,1,0:T(8,128)(2,1)}, u32[]{:S(2)}, u32[]{:S(2)}) collective-permute-start(bf16[1,256,384]{2,1,0:T(8,128)(2,1)} %bitcast.42), channel_id=1, source_target_pairs={{0,24},{8,0},{16,8},{24,16},{1,25},{9,1},{17,9},{25,17},{2,26},{10... | collective-permute-start | bytes 589832 | tf_op jit(solution)/shard_map/ppermute | solution.py:734
  187.1 34.2 %collective-permute-start.42 = (bf16[1,256,768]{2,1,0:T(8,128)(2,1)}, bf16[1,256,768]{2,1,0:T(8,128)(2,1)}, u32[]{:S(2)}, u32[]{:S(2)}) collective-permute-start(bf16[1,256,768]{2,1,0:T(8,128)(2,1)} %get-tuple-element.179), channel_id=1, source_target_pairs={{0,24},{8,0},{16,8},{24,16},{1,25},{9,1},{17,9},{25,17},{2,26},{10... | collective-permute-start | bytes 1179656 | tf_op jit(solution)/shard_map/ppermute | solution.py:734
  205.6 23.8 %collective-permute-start.40 = (bf16[1,256,768]{2,1,0:T(8,128)(2,1)S(1)}, bf16[1,256,768]{2,1,0:T(8,128)(2,1)S(1)}, u32[]{:S(2)}, u32[]{:S(2)}) collective-permute-start(bf16[1,256,768]{2,1,0:T(8,128)(2,1)S(1)} %copy-done.57), channel_id=1, source_target_pairs={{0,8},{8,16},{16,24},{24,0},{1,9},{9,17},{17,25},{25,1},{2,10},{10... | collective-permute-start | bytes 1179656 | tf_op jit(solution)/shard_map/ppermute | solution.py:734
  215.4 28.7 %collective-permute-start.41 = (bf16[1,256,768]{2,1,0:T(8,128)(2,1)S(1)}, bf16[1,256,768]{2,1,0:T(8,128)(2,1)S(1)}, u32[]{:S(2)}, u32[]{:S(2)}) collective-permute-start(bf16[1,256,768]{2,1,0:T(8,128)(2,1)S(1)} %copy-done.56), channel_id=1, source_target_pairs={{0,16},{8,24},{16,0},{24,8},{1,17},{9,25},{17,1},{25,9},{2,18},{10... | collective-permute-start | bytes 1179656 | tf_op jit(solution)/shard_map/ppermute | solution.py:734
  215.6 31.2 %collective-permute-start.59 = (bf16[128,2048]{1,0:T(8,128)(2,1)S(1)}, bf16[128,2048]{1,0:T(8,128)(2,1)S(1)}, u32[]{:S(2)}, u32[]{:S(2)}) collective-permute-start(bf16[128,2048]{1,0:T(8,128)(2,1)S(1)} %get-tuple-element.216), channel_id=1, source_target_pairs={{8,0},{16,8},{24,16},{9,1},{17,9},{25,17},{10,2},{18,10},{26,18},{... | collective-permute-start | bytes 1572872 | tf_op jit(solution)/shard_map/ppermute | solution.py:700
  220.0 27.1 %collective-permute-start.61 = (bf16[128,2048]{1,0:T(8,128)(2,1)S(1)}, bf16[128,2048]{1,0:T(8,128)(2,1)S(1)}, u32[]{:S(2)}, u32[]{:S(2)}) collective-permute-start(bf16[128,2048]{1,0:T(8,128)(2,1)S(1)} %collective-permute-done.60), channel_id=1, source_target_pairs={{8,16},{16,24},{9,17},{17,25},{10,18},{18,26},{11,19},{19,27},{12,... | collective-permute-start | bytes 1572872 | tf_op jit(solution)/shard_map/ppermute | solution.py:703
  221.3 26.6 %collective-permute-start.27 = (bf16[128,2048]{1,0:T(8,128)(2,1)S(1)}, bf16[128,2048]{1,0:T(8,128)(2,1)S(1)}, u32[]{:S(2)}, u32[]{:S(2)}) collective-permute-start(bf16[128,2048]{1,0:T(8,128)(2,1)S(1)} %get-tuple-element.162), channel_id=1, source_target_pairs={{0,8},{1,9},{2,10},{3,11},{4,12},{5,13},{6,14},{7,15}} | collective-permute-start | bytes 1572872 | tf_op jit(solution)/shard_map/ppermute | solution.py:722
  229.4 24.6 %collective-permute-start.25 = (bf16[128,2048]{1,0:T(8,128)(2,1)S(1)}, bf16[128,2048]{1,0:T(8,128)(2,1)S(1)}, u32[]{:S(2)}, u32[]{:S(2)}) collective-permute-start(bf16[128,2048]{1,0:T(8,128)(2,1)S(1)} %add_convert_fusion.16), channel_id=1, source_target_pairs={{16,8},{24,16},{17,9},{25,17},{18,10},{26,18},{19,11},{27,19},{20,... | collective-permute-start | bytes 1572872 | tf_op jit(solution)/shard_map/ppermute | solution.py:719
  246.8 50.8 %collective-permute-start.65 = (bf16[128,2048]{1,0:T(8,128)(2,1)S(1)}, bf16[128,2048]{1,0:T(8,128)(2,1)S(1)}, u32[]{:S(2)}, u32[]{:S(2)}) collective-permute-start(bf16[128,2048]{1,0:T(8,128)(2,1)S(1)} %get-tuple-element.216), channel_id=1, source_target_pairs={{0,1},{1,0},{2,3},{3,2},{4,5},{5,4},{6,7},{7,6},{8,9},{9,8},{10,11... | collective-permute-start | bytes 1572872 | tf_op jit(solution)/shard_map/ppermute | solution.py:427
  247.1 51.8 %collective-permute-start.43 = (bf16[1024,768]{1,0:T(8,128)(2,1)S(1)}, bf16[1024,768]{1,0:T(8,128)(2,1)S(1)}, u32[]{:S(2)}, u32[]{:S(2)}) collective-permute-start(bf16[1024,768]{1,0:T(8,128)(2,1)S(1)} %bitcast.282), channel_id=1, source_target_pairs={{0,4},{4,0},{1,5},{5,1},{2,6},{6,2},{3,7},{7,3},{8,12},{12,8},{9,1... | collective-permute-start | bytes 4718600 | tf_op jit(solution)/shard_map/ppermute | solution.py:427
  254.1 23.3 %collective-permute-start.62 = (bf16[128,2048]{1,0:T(8,128)(2,1)S(1)}, bf16[128,2048]{1,0:T(8,128)(2,1)S(1)}, u32[]{:S(2)}, u32[]{:S(2)}) collective-permute-start(bf16[128,2048]{1,0:T(8,128)(2,1)S(1)} %collective-permute-done.61), channel_id=1, source_target_pairs={{16,24},{17,25},{18,26},{19,27},{20,28},{21,29},{22,30},{23,31}} | collective-permute-start | bytes 1572872 | tf_op jit(solution)/shard_map/ppermute | solution.py:703
  280.5 53.5 %collective-permute-start.49 = (bf16[1024,768]{1,0:T(8,128)(2,1)S(1)}, bf16[1024,768]{1,0:T(8,128)(2,1)S(1)}, u32[]{:S(2)}, u32[]{:S(2)}) collective-permute-start(bf16[1024,768]{1,0:T(8,128)(2,1)S(1)} %pad_maximum_fusion.7), channel_id=1, source_target_pairs={{0,4},{4,0},{1,5},{5,1},{2,6},{6,2},{3,7},{7,3},{8,12},{12,8},{9,1... | collective-permute-start | bytes 4718600 | tf_op jit(solution)/shard_map/ppermute | solution.py:427
  294.9 20.4 %collective-permute-start.67 = (bf16[128,2048]{1,0:T(8,128)(2,1)S(1)}, bf16[128,2048]{1,0:T(8,128)(2,1)S(1)}, u32[]{:S(2)}, u32[]{:S(2)}) collective-permute-start(bf16[128,2048]{1,0:T(8,128)(2,1)S(1)} %get-tuple-element.122), channel_id=1, source_target_pairs={{0,1},{1,0},{2,3},{3,2},{4,5},{5,4},{6,7},{7,6},{8,9},{9,8},{10,11... | collective-permute-start | bytes 1572872 | tf_op jit(solution)/shard_map/ppermute | solution.py:427
  315.3 70.0 %collective-permute-start.44 = (bf16[2048,768]{1,0:T(8,128)(2,1)}, bf16[2048,768]{1,0:T(8,128)(2,1)}, u32[]{:S(2)}, u32[]{:S(2)}) collective-permute-start(bf16[2048,768]{1,0:T(8,128)(2,1)} %pad_maximum_fusion.2), channel_id=1, source_target_pairs={{0,2},{2,0},{1,3},{3,1},{4,6},{6,4},{5,7},{7,5},{8,10},{10,8},{9,1... | collective-permute-start | bytes 9437192 | tf_op jit(solution)/shard_map/ppermute | solution.py:427
  317.6 25.2 %collective-permute-start.34 = (bf16[128,2048]{1,0:T(8,128)(2,1)}, bf16[128,2048]{1,0:T(8,128)(2,1)}, u32[]{:S(2)}, u32[]{:S(2)}) collective-permute-start(bf16[128,2048]{1,0:T(8,128)(2,1)} %collective-permute-done.30), channel_id=1, source_target_pairs={{8,0},{16,8},{9,1},{17,9},{10,2},{18,10},{11,3},{19,11},{12,4},{20... | collective-permute-start | bytes 1572872 | tf_op jit(solution)/shard_map/ppermute | solution.py:700
  432.2 35.4 %collective-permute-start.112 = (bf16[2048,384]{1,0:T(8,128)(2,1)}, bf16[2048,384]{1,0:T(8,128)(2,1)}, u32[]{:S(2)}, u32[]{:S(2)}) collective-permute-start(bf16[2048,384]{1,0:T(8,128)(2,1)} %slice.573), channel_id=1, source_target_pairs={{0,2},{2,0},{1,3},{3,1},{4,6},{6,4},{5,7},{7,5},{8,10},{10,8},{9,1... | collective-permute-start | bytes 4718600 | tf_op jit(solution)/shard_map/ppermute | solution.py:427
  438.1 48.0 %collective-permute-start.50 = (bf16[512,2048]{1,0:T(8,128)(2,1)}, bf16[512,2048]{1,0:T(8,128)(2,1)}, u32[]{:S(2)}, u32[]{:S(2)}) collective-permute-start(bf16[512,2048]{1,0:T(8,128)(2,1)} %convolution_convert_fusion.3), channel_id=1, source_target_pairs={{0,1},{1,0},{2,3},{3,2},{4,5},{5,4},{6,7},{7,6},{8,9},{9,8},{10,11... | collective-permute-start | bytes 6291464 | tf_op jit(solution)/shard_map/ppermute | solution.py:427
  447.9 24.1 %collective-permute-start.69 = (bf16[512,2048]{1,0:T(8,128)(2,1)}, bf16[512,2048]{1,0:T(8,128)(2,1)}, u32[]{:S(2)}, u32[]{:S(2)}) collective-permute-start(bf16[512,2048]{1,0:T(8,128)(2,1)} %convolution_convert_fusion.2), channel_id=1, source_target_pairs={{0,1},{1,0},{2,3},{3,2},{4,5},{5,4},{6,7},{7,6},{8,9},{9,8},{10,11... | collective-permute-start | bytes 6291464 | tf_op jit(solution)/shard_map/ppermute | solution.py:427
  465.2 173.2 %collective-permute-start.107 = (bf16[1024,1536]{1,0:T(8,128)(2,1)S(1)}, bf16[1024,1536]{1,0:T(8,128)(2,1)S(1)}, u32[]{:S(2)}, u32[]{:S(2)}) collective-permute-start(bf16[1024,1536]{1,0:T(8,128)(2,1)S(1)} %slice.572), channel_id=1, source_target_pairs={{0,4},{4,0},{1,5},{5,1},{2,6},{6,2},{3,7},{7,3},{8,12},{12,8},{9,1... | collective-permute-start | bytes 9437192 | tf_op jit(solution)/shard_map/ppermute | solution.py:427
  471.2 81.0 %collective-permute-start.113 = (bf16[1024,384]{1,0:T(8,128)(2,1)}, bf16[1024,384]{1,0:T(8,128)(2,1)}, u32[]{:S(2)}, u32[]{:S(2)}) collective-permute-start(bf16[1024,384]{1,0:T(8,128)(2,1)} %slice.576), channel_id=1, source_target_pairs={{0,4},{4,0},{1,5},{5,1},{2,6},{6,2},{3,7},{7,3},{8,12},{12,8},{9,1... | collective-permute-start | bytes 2359304 | tf_op jit(solution)/shard_map/ppermute | solution.py:427
  478.4 94.3 %collective-permute-start.70 = (bf16[128,2048]{1,0:T(8,128)(2,1)S(1)}, bf16[128,2048]{1,0:T(8,128)(2,1)S(1)}, u32[]{:S(2)}, u32[]{:S(2)}) collective-permute-start(bf16[128,2048]{1,0:T(8,128)(2,1)S(1)} %get-tuple-element.153), channel_id=1, source_target_pairs={{24,16},{25,17},{26,18},{27,19},{28,20},{29,21},{30,22},{31,23}} | collective-permute-start | bytes 1572872 | tf_op jit(solution)/shard_map/ppermute | solution.py:719
  562.0 43.7 %collective-permute-start.51 = (bf16[128,2048]{1,0:T(8,128)(2,1)S(1)}, bf16[128,2048]{1,0:T(8,128)(2,1)S(1)}, u32[]{:S(2)}, u32[]{:S(2)}) collective-permute-start(bf16[128,2048]{1,0:T(8,128)(2,1)S(1)} %get-tuple-element.157), channel_id=1, source_target_pairs={{24,16},{25,17},{26,18},{27,19},{28,20},{29,21},{30,22},{31,23}} | collective-permute-start | bytes 1572872 | tf_op jit(solution)/shard_map/ppermute | solution.py:719
  571.2 48.4 %collective-permute-start.54 = (bf16[128,2048]{1,0:T(8,128)(2,1)S(1)}, bf16[128,2048]{1,0:T(8,128)(2,1)S(1)}, u32[]{:S(2)}, u32[]{:S(2)}) collective-permute-start(bf16[128,2048]{1,0:T(8,128)(2,1)S(1)} %get-tuple-element.158), channel_id=1, source_target_pairs={{0,8},{1,9},{2,10},{3,11},{4,12},{5,13},{6,14},{7,15}} | collective-permute-start | bytes 1572872 | tf_op jit(solution)/shard_map/ppermute | solution.py:722
  572.0 35.2 %collective-permute-start.73 = (bf16[128,2048]{1,0:T(8,128)(2,1)S(1)}, bf16[128,2048]{1,0:T(8,128)(2,1)S(1)}, u32[]{:S(2)}, u32[]{:S(2)}) collective-permute-start(bf16[128,2048]{1,0:T(8,128)(2,1)S(1)} %get-tuple-element.154), channel_id=1, source_target_pairs={{0,8},{1,9},{2,10},{3,11},{4,12},{5,13},{6,14},{7,15}} | collective-permute-start | bytes 1572872 | tf_op jit(solution)/shard_map/ppermute | solution.py:722
  572.7 31.6 %collective-permute-start.116 = (bf16[1,256,384]{2,1,0:T(8,128)(2,1)S(1)}, bf16[1,256,384]{2,1,0:T(8,128)(2,1)S(1)}, u32[]{:S(2)}, u32[]{:S(2)}) collective-permute-start(bf16[1,256,384]{2,1,0:T(8,128)(2,1)S(1)} %get-tuple-element.192), channel_id=1, source_target_pairs={{0,24},{8,0},{16,8},{24,16},{1,25},{9,1},{17,9},{25,17},{2,26},{10... | collective-permute-start | bytes 589832 | tf_op jit(solution)/shard_map/ppermute | solution.py:734
  605.8 21.6 %collective-permute-start.52 = (bf16[128,2048]{1,0:T(8,128)(2,1)S(1)}, bf16[128,2048]{1,0:T(8,128)(2,1)S(1)}, u32[]{:S(2)}, u32[]{:S(2)}) collective-permute-start(bf16[128,2048]{1,0:T(8,128)(2,1)S(1)} %add_convert_fusion.11), channel_id=1, source_target_pairs={{16,8},{24,16},{17,9},{25,17},{18,10},{26,18},{19,11},{27,19},{20,... | collective-permute-start | bytes 1572872 | tf_op jit(solution)/shard_map/ppermute | solution.py:719
  628.5 27.4 %collective-permute-start.53 = (bf16[128,2048]{1,0:T(8,128)(2,1)}, bf16[128,2048]{1,0:T(8,128)(2,1)S(1)}, u32[]{:S(2)}, u32[]{:S(2)}) collective-permute-start(bf16[128,2048]{1,0:T(8,128)(2,1)} %get-tuple-element.155), channel_id=1, source_target_pairs={{8,0},{16,8},{24,16},{9,1},{17,9},{25,17},{10,2},{18,10},{26,18},{... | collective-permute-start | bytes 1572872 | tf_op jit(solution)/shard_map/ppermute | solution.py:719
  633.7 20.6 %collective-permute-start.72 = (bf16[128,2048]{1,0:T(8,128)(2,1)}, bf16[128,2048]{1,0:T(8,128)(2,1)}, u32[]{:S(2)}, u32[]{:S(2)}) collective-permute-start(bf16[128,2048]{1,0:T(8,128)(2,1)} %get-tuple-element.151), channel_id=1, source_target_pairs={{8,0},{16,8},{24,16},{9,1},{17,9},{25,17},{10,2},{18,10},{26,18},{... | collective-permute-start | bytes 1572872 | tf_op jit(solution)/shard_map/ppermute | solution.py:719
  643.5 61.9 %collective-permute-start.108 = (bf16[1024,768]{1,0:T(8,128)(2,1)}, bf16[1024,768]{1,0:T(8,128)(2,1)}, u32[]{:S(2)}, u32[]{:S(2)}) collective-permute-start(bf16[1024,768]{1,0:T(8,128)(2,1)} %slice.574), channel_id=1, source_target_pairs={{0,2},{2,0},{1,3},{3,1},{4,6},{6,4},{5,7},{7,5},{8,10},{10,8},{9,1... | collective-permute-start | bytes 4718600 | tf_op jit(solution)/shard_map/ppermute | solution.py:427
  666.2 23.3 %collective-permute-start.57 = (bf16[128,2048]{1,0:T(8,128)(2,1)S(1)}, bf16[128,2048]{1,0:T(8,128)(2,1)}, u32[]{:S(2)}, u32[]{:S(2)}) collective-permute-start(bf16[128,2048]{1,0:T(8,128)(2,1)S(1)} %convert_element_type.374), channel_id=1, source_target_pairs={{0,1},{1,0},{2,3},{3,2},{4,5},{5,4},{6,7},{7,6},{8,9},{9,8},{10,11... | collective-permute-start | bytes 1572872 | tf_op jit(solution)/shard_map/ppermute | solution.py:427
  666.3 22.0 %collective-permute-start.77 = (bf16[128,2048]{1,0:T(8,128)(2,1)S(1)}, bf16[128,2048]{1,0:T(8,128)(2,1)}, u32[]{:S(2)}, u32[]{:S(2)}) collective-permute-start(bf16[128,2048]{1,0:T(8,128)(2,1)S(1)} %get-tuple-element.116), channel_id=1, source_target_pairs={{0,8},{8,16},{16,24},{1,9},{9,17},{17,25},{2,10},{10,18},{18,26},{... | collective-permute-start | bytes 1572872 | tf_op jit(solution)/shard_map/ppermute | solution.py:703
  668.8 60.8 %collective-permute-start.82 = (bf16[128,2048]{1,0:T(8,128)(2,1)S(1)}, bf16[128,2048]{1,0:T(8,128)(2,1)}, u32[]{:S(2)}, u32[]{:S(2)}) collective-permute-start(bf16[128,2048]{1,0:T(8,128)(2,1)S(1)} %get-tuple-element.116), channel_id=1, source_target_pairs={{0,1},{1,0},{2,3},{3,2},{4,5},{5,4},{6,7},{7,6},{8,9},{9,8},{10,11... | collective-permute-start | bytes 1572872 | tf_op jit(solution)/shard_map/ppermute | solution.py:427
  669.3 22.9 %collective-permute-start.76 = (bf16[128,2048]{1,0:T(8,128)(2,1)S(1)}, bf16[128,2048]{1,0:T(8,128)(2,1)}, u32[]{:S(2)}, u32[]{:S(2)}) collective-permute-start(bf16[128,2048]{1,0:T(8,128)(2,1)S(1)} %get-tuple-element.116), channel_id=1, source_target_pairs={{8,0},{16,8},{24,16},{9,1},{17,9},{25,17},{10,2},{18,10},{26,18},{... | collective-permute-start | bytes 1572872 | tf_op jit(solution)/shard_map/ppermute | solution.py:700
  691.7 112.0 %collective-permute-start.58 = (bf16[256,2048]{1,0:T(8,128)(2,1)}, bf16[256,2048]{1,0:T(8,128)(2,1)}, u32[]{:S(2)}, u32[]{:S(2)}) collective-permute-start(bf16[256,2048]{1,0:T(8,128)(2,1)} %pad_maximum_fusion.9), channel_id=1, source_target_pairs={{0,2},{2,0},{1,3},{3,1},{4,6},{6,4},{5,7},{7,5},{8,10},{10,8},{9,1... | collective-permute-start | bytes 3145736 | tf_op jit(solution)/shard_map/ppermute | solution.py:427
  692.2 18.9 %collective-permute-start.80 = (bf16[128,2048]{1,0:T(8,128)(2,1)}, bf16[128,2048]{1,0:T(8,128)(2,1)S(1)}, u32[]{:S(2)}, u32[]{:S(2)}) collective-permute-start(bf16[128,2048]{1,0:T(8,128)(2,1)} %collective-permute-done.76), channel_id=1, source_target_pairs={{8,0},{16,8},{9,1},{17,9},{10,2},{18,10},{11,3},{19,11},{12,4},{20... | collective-permute-start | bytes 1572872 | tf_op jit(solution)/shard_map/ppermute | solution.py:700
  704.1 23.3 %collective-permute-start.79 = (bf16[128,2048]{1,0:T(8,128)(2,1)S(1)}, bf16[128,2048]{1,0:T(8,128)(2,1)S(1)}, u32[]{:S(2)}, u32[]{:S(2)}) collective-permute-start(bf16[128,2048]{1,0:T(8,128)(2,1)S(1)} %collective-permute-done.78), channel_id=1, source_target_pairs={{16,24},{17,25},{18,26},{19,27},{20,28},{21,29},{22,30},{23,31}} | collective-permute-start | bytes 1572872 | tf_op jit(solution)/shard_map/ppermute | solution.py:703
  708.3 43.5 %collective-permute-start.111 = (bf16[1,256,768]{2,1,0:T(8,128)(2,1)S(1)}, bf16[1,256,768]{2,1,0:T(8,128)(2,1)S(1)}, u32[]{:S(2)}, u32[]{:S(2)}) collective-permute-start(bf16[1,256,768]{2,1,0:T(8,128)(2,1)S(1)} %get-tuple-element.171), channel_id=1, source_target_pairs={{0,24},{8,0},{16,8},{24,16},{1,25},{9,1},{17,9},{25,17},{2,26},{10... | collective-permute-start | bytes 1179656 | tf_op jit(solution)/shard_map/ppermute | solution.py:734
  730.7 21.0 %collective-permute-start.110 = (bf16[1,256,768]{2,1,0:T(8,128)(2,1)S(1)}, bf16[1,256,768]{2,1,0:T(8,128)(2,1)S(1)}, u32[]{:S(2)}, u32[]{:S(2)}) collective-permute-start(bf16[1,256,768]{2,1,0:T(8,128)(2,1)S(1)} %get-tuple-element.172), channel_id=1, source_target_pairs={{0,16},{8,24},{16,0},{24,8},{1,17},{9,25},{17,1},{25,9},{2,18},{10... | collective-permute-start | bytes 1179656 | tf_op jit(solution)/shard_map/ppermute | solution.py:734
  780.0 19.6 %collective-permute-start.87 = (bf16[3,1024,128]{2,1,0:T(8,128)(2,1)}, bf16[3,1024,128]{2,1,0:T(8,128)(2,1)}, u32[]{:S(2)}, u32[]{:S(2)}) collective-permute-start(bf16[3,1024,128]{2,1,0:T(8,128)(2,1)} %get-tuple-element.21), channel_id=1, source_target_pairs={{0,4},{4,0},{1,5},{5,1},{2,6},{6,2},{3,7},{7,3},{8,12},{12,8},{9,1... | collective-permute-start | bytes 2359304 | tf_op jit(solution)/shard_map/ppermute | solution.py:427
  791.4 54.1 %collective-permute-start.102 = (bf16[2048,128]{1,0:T(8,128)(2,1)S(1)}, bf16[2048,128]{1,0:T(8,128)(2,1)S(1)}, u32[]{:S(2)}, u32[]{:S(2)}) collective-permute-start(bf16[2048,128]{1,0:T(8,128)(2,1)S(1)} %slice.578), channel_id=1, source_target_pairs={{0,2},{2,0},{1,3},{3,1},{4,6},{6,4},{5,7},{7,5},{8,10},{10,8},{9,1... | collective-permute-start | bytes 1572872 | tf_op jit(solution)/shard_map/ppermute | solution.py:427
  803.6 52.2 %collective-permute-start.88 = (bf16[512,2048]{1,0:T(8,128)(2,1)S(1)}, bf16[512,2048]{1,0:T(8,128)(2,1)S(1)}, u32[]{:S(2)}, u32[]{:S(2)}) collective-permute-start(bf16[512,2048]{1,0:T(8,128)(2,1)S(1)} %convolution_convert_fusion.1), channel_id=1, source_target_pairs={{0,1},{1,0},{2,3},{3,2},{4,5},{5,4},{6,7},{7,6},{8,9},{9,8},{10,11... | collective-permute-start | bytes 6291464 | tf_op jit(solution)/shard_map/ppermute | solution.py:427
  853.5 30.2 %collective-permute-start.97 = (bf16[2048,384]{1,0:T(8,128)(2,1)S(1)}, bf16[2048,384]{1,0:T(8,128)(2,1)S(1)}, u32[]{:S(2)}, u32[]{:S(2)}) collective-permute-start(bf16[2048,384]{1,0:T(8,128)(2,1)S(1)} %slice.575), channel_id=1, source_target_pairs={{0,2},{2,0},{1,3},{3,1},{4,6},{6,4},{5,7},{7,5},{8,10},{10,8},{9,1... | collective-permute-start | bytes 4718600 | tf_op jit(solution)/shard_map/ppermute | solution.py:427
  860.0 33.5 %collective-permute-start.106 = (bf16[1,256,128]{2,1,0:T(8,128)(2,1)S(1)}, bf16[1,256,128]{2,1,0:T(8,128)(2,1)S(1)}, u32[]{:S(2)}, u32[]{:S(2)}) collective-permute-start(bf16[1,256,128]{2,1,0:T(8,128)(2,1)S(1)} %get-tuple-element.226), channel_id=1, source_target_pairs={{0,24},{8,0},{16,8},{24,16},{1,25},{9,1},{17,9},{25,17},{2,26},{10... | collective-permute-start | bytes 196616 | tf_op jit(solution)/shard_map/ppermute | solution.py:734
  860.1 25.7 %collective-permute-start.105 = (bf16[1,256,128]{2,1,0:T(8,128)(2,1)S(1)}, bf16[1,256,128]{2,1,0:T(8,128)(2,1)S(1)}, u32[]{:S(2)}, u32[]{:S(2)}) collective-permute-start(bf16[1,256,128]{2,1,0:T(8,128)(2,1)S(1)} %get-tuple-element.227), channel_id=1, source_target_pairs={{0,16},{8,24},{16,0},{24,8},{1,17},{9,25},{17,1},{25,9},{2,18},{10... | collective-permute-start | bytes 196616 | tf_op jit(solution)/shard_map/ppermute | solution.py:734
  863.3 22.1 %collective-permute-start.104 = (bf16[1,256,128]{2,1,0:T(8,128)(2,1)S(1)}, bf16[1,256,128]{2,1,0:T(8,128)(2,1)S(1)}, u32[]{:S(2)}, u32[]{:S(2)}) collective-permute-start(bf16[1,256,128]{2,1,0:T(8,128)(2,1)S(1)} %get-tuple-element.228), channel_id=1, source_target_pairs={{0,8},{8,16},{16,24},{24,0},{1,9},{9,17},{17,25},{25,1},{2,10},{10... | collective-permute-start | bytes 196616 | tf_op jit(solution)/shard_map/ppermute | solution.py:734
  865.9 19.9 %collective-permute-start.92 = (bf16[128,2048]{1,0:T(8,128)(2,1)S(1)}, bf16[128,2048]{1,0:T(8,128)(2,1)S(1)}, u32[]{:S(2)}, u32[]{:S(2)}) collective-permute-start(bf16[128,2048]{1,0:T(8,128)(2,1)S(1)} %get-tuple-element.150), channel_id=1, source_target_pairs={{0,8},{1,9},{2,10},{3,11},{4,12},{5,13},{6,14},{7,15}} | collective-permute-start | bytes 1572872 | tf_op jit(solution)/shard_map/ppermute | solution.py:722
  898.8 21.1 %collective-permute-start.100 = (bf16[1,256,384]{2,1,0:T(8,128)(2,1)}, bf16[1,256,384]{2,1,0:T(8,128)(2,1)}, u32[]{:S(2)}, u32[]{:S(2)}) collective-permute-start(bf16[1,256,384]{2,1,0:T(8,128)(2,1)} %get-tuple-element.200), channel_id=1, source_target_pairs={{0,16},{8,24},{16,0},{24,8},{1,17},{9,25},{17,1},{25,9},{2,18},{10... | collective-permute-start | bytes 589832 | tf_op jit(solution)/shard_map/ppermute | solution.py:734
  902.4 24.6 %collective-permute-start.91 = (bf16[128,2048]{1,0:T(8,128)(2,1)}, bf16[128,2048]{1,0:T(8,128)(2,1)S(1)}, u32[]{:S(2)}, u32[]{:S(2)}) collective-permute-start(bf16[128,2048]{1,0:T(8,128)(2,1)} %get-tuple-element.147), channel_id=1, source_target_pairs={{8,0},{16,8},{24,16},{9,1},{17,9},{25,17},{10,2},{18,10},{26,18},{... | collective-permute-start | bytes 1572872 | tf_op jit(solution)/shard_map/ppermute | solution.py:719
  905.8 21.2 %collective-permute-start.94 = (bf16[128,2048]{1,0:T(8,128)(2,1)}, bf16[128,2048]{1,0:T(8,128)(2,1)}, u32[]{:S(2)}, u32[]{:S(2)}) collective-permute-start(bf16[128,2048]{1,0:T(8,128)(2,1)} %add_convert_fusion), channel_id=1, source_target_pairs={{0,8},{8,16},{16,24},{1,9},{9,17},{17,25},{2,10},{10,18},{18,26},{... | collective-permute-start | bytes 1572872 | tf_op jit(solution)/shard_map/ppermute | solution.py:722
  935.7 60.5 %collective-permute-start.96 = (bf16[256,2048]{1,0:T(8,128)(2,1)S(1)}, bf16[256,2048]{1,0:T(8,128)(2,1)}, u32[]{:S(2)}, u32[]{:S(2)}) collective-permute-start(bf16[256,2048]{1,0:T(8,128)(2,1)S(1)} %pad_maximum_fusion.10), channel_id=1, source_target_pairs={{0,2},{2,0},{1,3},{3,1},{4,6},{6,4},{5,7},{7,5},{8,10},{10,8},{9,1... | collective-permute-start | bytes 3145736 | tf_op jit(solution)/shard_map/ppermute | solution.py:427
  (143 other events, 2743.1 us)

commit v2 on v1

--- a/solution.py
+++ b/solution.py
@@ -655,15 +655,545 @@
         fetch_rows(place_ref, out_own, out_other, lambda rows, held=held: held[rows, :], write)
 
 
-def qkv_kernel(rows_ref, weight_ref, bias_ref, cos_ref, up_ref, down_ref, out_ref):
+MESH_IDS = pl.DeviceIdType.MESH
+CHUNKS = 4
+CHUNK = QUARTER // CHUNKS
+
+
+def remote(source, goal, send_sem, recv_sem, where):
+    return pltpu.make_async_remote_copy(
+        src_ref=source,
+        dst_ref=goal,
+        send_sem=send_sem,
+        recv_sem=recv_sem,
+        device_id=where,
+        device_id_type=MESH_IDS,
+    )
+
+
+class Sent:
+    def __init__(self):
+        self.moves = []
+
+    def start(self, move, condition=None):
+        self.moves.append((move, condition))
+        guarded(condition, move.start)
+
+    def finish(self):
+        for move, condition in self.moves:
+            guarded(condition, move.wait_send)
+
+
+def guarded(condition, action):
+    if condition is None:
+        action()
+    else:
+        pl.when(condition)(action)
+
+
+def greet(others):
+    barrier = pltpu.get_barrier_semaphore()
+    count = 0
+    for where, condition in others:
+        def signal(where=where):
+            pl.semaphore_signal(barrier, inc=1, device_id=where, device_id_type=MESH_IDS)
+
+        guarded(condition, signal)
+        count = count + (1 if condition is None else condition.astype(jnp.int32))
+    pl.semaphore_wait(barrier, count)
+
+
+def line_peers(at_z, at_c):
+    return [
+        ({"z": jnp.maximum(at_z - 1, 0)}, at_z > 0),
+        ({"z": jnp.minimum(at_z + 1, LINE - 1)}, at_z < LINE - 1),
+        ({"c": 1 - at_c}, None),
+    ]
+
+
+class Reduce:
+    def __init__(self, sent, at_z, at_c, send_ref, keep_ref, acc_ref, scratch):
+        self.sent, self.at_z, self.at_c = sent, at_z, at_c
+        self.send_ref, self.keep_ref, self.acc_ref = send_ref, keep_ref, acc_ref
+        (
+            self.came,
+            self.down_from,
+            self.above_from,
+            self.down_to,
+            self.above_to,
+            self.core_out,
+            self.core_in,
+            self.down_out,
+            self.down_in,
+            self.above_out,
+            self.above_in,
+        ) = scratch
+
+    def core_move(self, block, part):
+        rows = pl.ds(block * QUARTER + part * CHUNK, CHUNK)
+        return remote(
+            self.send_ref.at[rows, :],
+            self.came.at[rows, :],
+            self.core_out.at[block, part],
+            self.core_in.at[block, part],
+            {"c": 1 - self.at_c},
+        )
+
+    def down_move(self, step, part):
+        rows = pl.ds(part * CHUNK, CHUNK)
+        return remote(
+            self.down_from.at[step - 1, rows, :],
+            self.down_to.at[step - 1, rows, :],
+            self.down_out.at[step - 1, part],
+            self.down_in.at[step - 1, part],
+            {"z": jnp.maximum(self.at_z - 1, 0)},
+        )
+
+    def above_move(self, step, part):
+        rows = pl.ds(part * CHUNK, CHUNK)
+        return remote(
+            self.above_from.at[step - 1, rows, :],
+            self.above_to.at[step - 1, rows, :],
+            self.above_out.at[step - 1, part],
+            self.above_in.at[step - 1, part],
+            {"z": jnp.minimum(self.at_z + 1, LINE - 1)},
+        )
+
+    def local(self, block, part):
+        rows = pl.ds(block * QUARTER + part * CHUNK, CHUNK)
+        return self.keep_ref[rows, :] + self.came[rows, :].astype(jnp.float32)
+
+    def stage(self, step, part):
+        at_z, rows = self.at_z, pl.ds(part * CHUNK, CHUNK)
+        last = LINE - 1
+        if step == 0:
+            for block in (1, 3, 2, 0):
+                self.sent.start(self.core_move(block, part))
+            return
+        if step <= last:
+            for block in {1: (1, 3), 2: (2,), 3: (0,)}[step]:
+                self.core_move(block, part).wait_recv()
+            falling = at_z >= LINE - step
+            rising = at_z <= step - 1
+
+            def lead_down():
+                self.down_from[step - 1, rows, :] = self.local(step, part).astype(jnp.bfloat16)
+
+            def add_down():
+                self.down_move(step - 1, part).wait_recv()
+                held = self.down_to[step - 2, rows, :].astype(jnp.float32)
+                self.down_from[step - 1, rows, :] = (self.local(step, part) + held).astype(
+                    jnp.bfloat16
+                )
+
+            def lead_above():
+                self.above_from[step - 1, rows, :] = self.local(LINE - step, part).astype(
+                    jnp.bfloat16
+                )
+
+            def add_above():
+                self.above_move(step - 1, part).wait_recv()
+                held = self.above_to[step - 2, rows, :].astype(jnp.float32)
+                self.above_from[step - 1, rows, :] = (
+                    self.local(LINE - step, part) + held
+                ).astype(jnp.bfloat16)
+
+            pl.when(at_z == last)(lead_down)
+            if step > 1:
+                pl.when(falling & (at_z < last))(add_down)
+            self.sent.start(self.down_move(step, part), falling)
+            pl.when(at_z == 0)(lead_above)
+            if step > 1:
+                pl.when(rising & (at_z > 0))(add_above)
+            self.sent.start(self.above_move(step, part), rising)
+            return
+        self.acc_ref[...] = self.local(0, part)
+
+        @pl.when(at_z < last)
+        def _():
+            self.down_move(last, part).wait_recv()
+            self.acc_ref[...] += self.down_to[last - 1, rows, :].astype(jnp.float32)
+
+        @pl.when(at_z > 0)
+        def _():
+            self.above_move(last, part).wait_recv()
+            self.acc_ref[...] += self.above_to[last - 1, rows, :].astype(jnp.float32)
+
+
+def reduce_scratch(width):
+    halves = jnp.bfloat16
+    steps = (LINE - 1, CHUNKS)
+    dma = pltpu.SemaphoreType.DMA
+    return [
+        pltpu.VMEM((LINE * QUARTER, width), halves),
+        pltpu.VMEM((LINE - 1, QUARTER, width), halves),
+        pltpu.VMEM((LINE - 1, QUARTER, width), halves),
+        pltpu.VMEM((LINE - 1, QUARTER, width), halves),
+        pltpu.VMEM((LINE - 1, QUARTER, width), halves),
+        dma((LINE, CHUNKS)),
+        dma((LINE, CHUNKS)),
+        dma(steps),
+        dma(steps),
+        dma(steps),
+        dma(steps),
+    ]
+
+
+class Gather:
+    def __init__(self, sent, at_z, at_c, full_ref, scratch):
+        self.sent, self.at_z, self.at_c, self.full = sent, at_z, at_c, full_ref
+        (
+            self.down_out,
+            self.down_in,
+            self.above_out,
+            self.above_in,
+            self.core_out,
+            self.core_in,
+        ) = scratch
+
+    def rows(self, slot, part):
+        return pl.ds(slot * QUARTER + part * CHUNK, CHUNK)
+
+    def down_move(self, step, part):
+        return remote(
+            self.full.at[self.rows(step - 1, part), :],
+            self.full.at[self.rows(step, part), :],
+            self.down_out.at[step - 1, part],
+            self.down_in.at[step - 1, part],
+            {"z": jnp.maximum(self.at_z - 1, 0)},
+        )
+
+    def above_move(self, step, part):
+        return remote(
+            self.full.at[self.rows((LINE + 1 - step) % LINE, part), :],
+            self.full.at[self.rows(LINE - step, part), :],
+            self.above_out.at[step - 1, part],
+            self.above_in.at[step - 1, part],
+            {"z": jnp.minimum(self.at_z + 1, LINE - 1)},
+        )
+
+    def core_move(self, slot, part):
+        return remote(
+            self.full.at[self.rows(slot, part), :],
+            self.full.at[self.rows(LINE + slot, part), :],
+            self.core_out.at[slot, part],
+            self.core_in.at[slot, part],
+            {"c": 1 - self.at_c},
+        )
+
+    def stage(self, step, part):
+        at_z, last = self.at_z, LINE - 1
+        if step == 0:
+            self.sent.start(self.down_move(1, part), at_z > 0)
+            self.sent.start(self.above_move(1, part), at_z < last)
+            self.sent.start(self.core_move(0, part))
+            return
+        if step <= last:
+            from_above = at_z + step <= last
+            from_below = at_z >= step
+            guarded(from_above, self.down_move(step, part).wait_recv)
+            if step < last:
+                self.sent.start(self.down_move(step + 1, part), from_above & (at_z > 0))
+            guarded(from_below, self.above_move(step, part).wait_recv)
+            if step < last:
+                self.sent.start(self.above_move(step + 1, part), from_below & (at_z < last))
+            self.sent.start(self.core_move(step, part), from_above)
+            self.sent.start(self.core_move(LINE - step, part), from_below)
+            return
+        for slot in range(LINE):
+            self.core_move(slot, part).wait_recv()
+
+
+def gather_scratch():
+    dma = pltpu.SemaphoreType.DMA
+    steps = (LINE - 1, CHUNKS)
+    return [dma(steps)] * 4 + [dma((LINE, CHUNKS))] * 2
+
+
+def pipeline(stages):
+    for tick in range(CHUNKS + len(stages) - 1):
+        for depth in reversed(range(len(stages))):
+            part = tick - depth
+            if 0 <= part < CHUNKS:
+                stages[depth](part)
+
+
+def row_norm(matrix_in):
+    center = jnp.mean(matrix_in, axis=-1, keepdims=True)
+    centered = matrix_in - center
+    inverse = lax.rsqrt(jnp.mean(centered * centered, axis=-1, keepdims=True) + epsilon)
+    return (centered * inverse, inverse)
+
+
+REDUCE_REFS = 11
+GATHER_REFS = 6
+
+
+def middle_kernel(
+    send_ref, keep_ref, base_ref, gain_ref, shift_ref, full_ref, residual_ref, acc_ref, *scratch
+):
+    at_z, at_c = lax.axis_index("z"), lax.axis_index("c")
+    greet(line_peers(at_z, at_c))
+    sent = Sent()
+    reduce = Reduce(sent, at_z, at_c, send_ref, keep_ref, acc_ref, scratch[:REDUCE_REFS])
+    gather = Gather(sent, at_z, at_c, full_ref, scratch[REDUCE_REFS:])
+
+    def settle(part):
+        rows = pl.ds(part * CHUNK, CHUNK)
+        reduce.stage(LINE, part)
+        residual = base_ref[rows, :] + acc_ref[...]
+        residual_ref[rows, :] = residual
+        normed = row_norm(residual)[0]
+        full_ref[rows, :] = (normed * gain_ref[...] + shift_ref[...]).astype(full_ref.dtype)
+        gather.stage(0, part)
+
+    pipeline(
+        [functools.partial(reduce.stage, step) for step in range(LINE)]
+        + [settle]
+        + [functools.partial(gather.stage, step) for step in range(1, LINE + 1)]
+    )
+    sent.finish()
+
+
+def middle_back_kernel(
+    send_ref,
+    keep_ref,
+    residual_ref,
+    grad_ref,
+    gain_ref,
+    full_ref,
+    turned_ref,
+    sums_ref,
+    acc_ref,
+    *scratch,
+):
+    at_z, at_c = lax.axis_index("z"), lax.axis_index("c")
+    greet(line_peers(at_z, at_c))
+    sent = Sent()
+    reduce = Reduce(sent, at_z, at_c, send_ref, keep_ref, acc_ref, scratch[:REDUCE_REFS])
+    gather = Gather(sent, at_z, at_c, full_ref, scratch[REDUCE_REFS:])
+    sums_ref[...] = jnp.zeros_like(sums_ref)
+
+    def settle(part):
+        rows = pl.ds(part * CHUNK, CHUNK)
+        reduce.stage(LINE, part)
+        incoming = acc_ref[...]
+        normed, inverse = row_norm(residual_ref[rows, :])
+        sums_ref[0:1, :] += jnp.sum(incoming * normed, axis=0, keepdims=True)
+        sums_ref[1:2, :] += jnp.sum(incoming, axis=0, keepdims=True)
+        turned = grad_ref[rows, :].astype(jnp.float32) + norm_back(
+            incoming, normed, inverse, gain_ref[...]
+        )
+        turned_ref[rows, :] = turned
+        full_ref[rows, :] = turned.astype(full_ref.dtype)
+        gather.stage(0, part)
+
+    pipeline(
+        [functools.partial(reduce.stage, step) for step in range(LINE)]
+        + [settle]
+        + [functools.partial(gather.stage, step) for step in range(1, LINE + 1)]
+    )
+    sent.finish()
+
+
+def last_kernel(
+    send_ref,
+    keep_ref,
+    base_ref,
+    turned_ref,
+    gain_ref,
+    early_ref,
+    spread_ref,
+    total_ref,
+    acc_ref,
+    *scratch,
+):
+    at_z, at_x, at_y, at_c = (lax.axis_index(name) for name in ("z", "x", "y", "c"))
+    peers = [({"c": 1 - at_c}, None), ({"y": 1 - at_y}, None), ({"x": 1 - at_x}, None)]
+    peers += [({"z": lax.rem(at_z + step, LINE)}, None) for step in range(1, LINE)]
+    greet(peers)
+    sent = Sent()
+    reduce = Reduce(sent, at_z, at_c, send_ref, keep_ref, acc_ref, scratch[:REDUCE_REFS])
+    spread_out, spread_in, folds, came, lines, fold_out, fold_in, line_out, line_in = scratch[
+        REDUCE_REFS:
+    ]
+    folds[0] = early_ref[...]
+    half = folds.shape[2] // 2
+    span = half // LINE
+
+    def spread_move(kind, part, arriving=False):
+        slot, where, across = {
+            "core": (0, {"c": 1 - at_c}, False),
+            "across": (1, {"y": 1 - at_y}, False),
+            "both": (2, {"c": 1 - at_c}, True),
+        }[kind]
+        seq, core = (1 - at_y if across else at_y), at_c
+        if arriving:
+            seq = 1 - seq if kind == "across" else seq
+            core = 1 - core if kind != "across" else core
+        rows = pl.ds(pl.multiple_of(core * QUARTER + part * CHUNK, CHUNK), CHUNK)
+        return remote(
+            spread_ref.at[seq, rows, :],
+            spread_ref.at[seq, rows, :],
+            spread_out.at[slot, part],
+            spread_in.at[slot, part],
+            where,
+        )
+
+    def settle(part):
+        rows = pl.ds(part * CHUNK, CHUNK)
+        reduce.stage(LINE, part)
+        incoming = acc_ref[...]
+        normed, inverse = row_norm(base_ref[rows, :])
+        folds[0, 0:1, :] += jnp.sum(incoming * normed, axis=0, keepdims=True)
+        folds[0, 1:2, :] += jnp.sum(incoming, axis=0, keepdims=True)
+        turned = turned_ref[rows, :] + norm_back(incoming, normed, inverse, gain_ref[...])
+        turned = turned.astype(spread_ref.dtype)
+        goal = pl.ds(pl.multiple_of(at_c * QUARTER + part * CHUNK, CHUNK), CHUNK)
+        for rel_x in range(2):
+            for line in range(LINE):
+                lanes = pl.multiple_of((2 * line + jnp.abs(at_x - rel_x)) * span, span)
+                start = rel_x * half + line * span
+                spread_ref[at_y, goal, pl.ds(lanes, span)] = turned[:, start : start + span]
+        sent.start(spread_move("across", part))
+        sent.start(spread_move("core", part))
+
+    def pass_on(part):
+        spread_move("across", part, arriving=True).wait_recv()
+        sent.start(spread_move("both", part))
+
+    pipeline(
+        [functools.partial(reduce.stage, step) for step in range(LINE)] + [settle, pass_on]
+    )
+    for slot, where in enumerate(({"c": 1 - at_c}, {"y": 1 - at_y}, {"x": 1 - at_x})):
+        move = remote(folds.at[slot], came.at[slot], fold_out.at[slot], fold_in.at[slot], where)
+        sent.start(move)
+        move.wait_recv()
+        if slot < 2:
+            folds[slot + 1] = folds[slot] + came[slot]
+        else:
+            folds[3, :, :half] = folds[2, :, :half] + came[2, :, half:]
+            folds[3, :, half:] = folds[2, :, half:] + came[2, :, :half]
+
+    def line_move(step, arriving=False):
+        origin = lax.rem(at_z + LINE - step, LINE) if arriving else at_z
+        return remote(
+            folds.at[3],
+            lines.at[origin],
+            line_out.at[step - 1],
+            line_in.at[step - 1],
+            {"z": lax.rem(at_z + step, LINE)},
+        )
+
+    for step in range(1, LINE):
+        sent.start(line_move(step))
+    lines[at_z] = folds[3]
+    for step in range(1, LINE):
+        line_move(step, arriving=True).wait_recv()
+    total_ref[...] = (lines[0] + lines[1]) + (lines[2] + lines[3])
+    for part in range(CHUNKS):
+        spread_move("core", part, arriving=True).wait_recv()
+        spread_move("both", part, arriving=True).wait_recv()
+    sent.finish()
+
+
+def open_kernel(
+    own_ref, part_ref, full_ref, near_ref, over_x_ref, over_y_ref, over_xy_ref, local_sem, *scratch
+):
+    at_z, at_x, at_y, at_c = (lax.axis_index(name) for name in ("z", "x", "y", "c"))
+    peers = [({"c": 1 - at_c}, None), ({"y": 1 - at_y}, None), ({"x": 1 - at_x}, None)]
+    peers += [({"z": lax.rem(at_z + step, LINE)}, None) for step in range(1, LINE)]
+    greet(peers)
+    sent = Sent()
+    gather = Gather(sent, at_z, at_c, full_ref, scratch[:GATHER_REFS])
+    trade_out, trade_in, flip_out, flip_in = scratch[GATHER_REFS:]
+    rows_of = part_ref.shape[1]
+
+    def trade_move(step, arriving=False):
+        origin = lax.rem(at_z + LINE - step, LINE) if arriving else at_z
+        rows = pl.ds(pl.multiple_of(origin * rows_of, rows_of), rows_of)
+        return remote(
+            part_ref.at[lax.rem(at_z + step, LINE)],
+            near_ref.at[rows, :],
+            trade_out.at[step - 1],
+            trade_in.at[step - 1],
+            {"z": lax.rem(at_z + step, LINE)},
+        )
+
+    def flip_move(kind, source, goal, turn, where):
+        block = lax.rem(at_z + LINE - turn, LINE) * rows_of
+        rows = pl.ds(pl.multiple_of(block, rows_of), rows_of)
+        return remote(
+            source.at[rows, :],
+            goal.at[rows, :],
+            flip_out.at[kind, turn],
+            flip_in.at[kind, turn],
+            where,
+        )
+
+    def to_x(turn):
+        return flip_move(0, near_ref, over_x_ref, turn, {"x": 1 - at_x})
+
+    def to_y(turn):
+        return flip_move(1, near_ref, over_y_ref, turn, {"y": 1 - at_y})
+
+    def to_xy(turn):
+        if turn % 2 == 0:
+            return flip_move(2, over_x_ref, over_xy_ref, turn, {"y": 1 - at_y})
+        return flip_move(2, over_y_ref, over_xy_ref, turn, {"x": 1 - at_x})
+
+    for step in (2, 1, 3):
+        sent.start(trade_move(step))
+    mine = pltpu.make_async_copy(
+        part_ref.at[at_z],
+        near_ref.at[pl.ds(pl.multiple_of(at_z * rows_of, rows_of), rows_of), :],
+        local_sem.at[0],
+    )
+    mine.start()
+    rows_copy = pltpu.make_async_copy(
+        own_ref, full_ref.at[pl.ds(0, QUARTER), :], local_sem.at[1]
+    )
+    rows_copy.start()
+    mine.wait()
+    sent.start(to_x(0))
+    sent.start(to_y(0))
+    rows_copy.wait()
+    for part in range(CHUNKS):
+        gather.stage(0, part)
+    for turn in range(1, LINE):
+        trade_move(turn, arriving=True).wait_recv()
+        sent.start(to_x(turn))
+        sent.start(to_y(turn))
+    for step in range(1, LINE):
+        for part in range(CHUNKS):
+            gather.stage(step, part)
+        if step == 1:
+            for turn in range(LINE):
+                if turn % 2 == 0:
+                    to_x(turn).wait_recv()
+                else:
+                    to_y(turn).wait_recv()
+                sent.start(to_xy(turn))
+    for part in range(CHUNKS):
+        gather.stage(LINE, part)
+    for turn in range(LINE):
+        if turn % 2 == 0:
+            to_y(turn).wait_recv()
+        else:
+            to_x(turn).wait_recv()
+        to_xy(turn).wait_recv()
+    sent.finish()
+
+
+def qkv_kernel(
+    rows_ref, near_ref, over_x_ref, over_y_ref, over_xy_ref, bias_ref, cos_ref, up_ref, down_ref, out_ref
+):
     floats = jnp.float32
     width = 2 * HD
-    for part in range(2):
-        product = jnp.dot(
-            rows_ref[...],
-            weight_ref[:, part * 3 * width : (part + 1) * 3 * width],
-            preferred_element_type=floats,
-        )
+    half = near_ref.shape[0]
+    for part, (first, second) in enumerate(((near_ref, over_x_ref), (over_y_ref, over_xy_ref))):
+        product = jnp.dot(rows_ref[:, :half], first[...], preferred_element_type=floats)
+        product = product + jnp.dot(rows_ref[:, half:], second[...], preferred_element_type=floats)
         for kind in range(3):
             content = product[:, kind * width : (kind + 1) * width]
             content = content + bias_ref[part * 3 + kind : part * 3 + kind + 1, :]
@@ -676,8 +1206,72 @@
             out_ref[part, kind] = content.astype(out_ref.dtype)
 
 
+def feed_kernel(
+    low_ref,
+    grad_ref,
+    up_near,
+    up_x,
+    up_y,
+    up_xy,
+    down_near,
+    down_x,
+    down_y,
+    down_xy,
+    hidden_ref,
+    turned_ref,
+):
+    floats = jnp.float32
+    half, wide = down_near.shape
+    pieces = ((up_near, up_x, down_near, down_x), (up_y, up_xy, down_y, down_xy))
+    for part, (gate_a, gate_b, back_a, back_b) in enumerate(pieces):
+        gate_up = jnp.dot(low_ref[:, :half], gate_a[...], preferred_element_type=floats)
+        gate_up = gate_up + jnp.dot(low_ref[:, half:], gate_b[...], preferred_element_type=floats)
+        grad_hidden = jnp.dot(grad_ref[:, :half], back_a[...], preferred_element_type=floats)
+        grad_hidden = grad_hidden + jnp.dot(
+            grad_ref[:, half:], back_b[...], preferred_element_type=floats
+        )
+        gate, up_part = gate_up[:, :wide], gate_up[:, wide:]
+        sigmoid_gate = jax.nn.sigmoid(gate)
+        silu = gate * sigmoid_gate
+        hidden_ref[:, part * wide : (part + 1) * wide] = (silu * up_part).astype(hidden_ref.dtype)
+        grad_gate = grad_hidden * up_part * sigmoid_gate * (1.0 + gate * (1.0 - sigmoid_gate))
+        base = 2 * part * wide
+        turned_ref[:, base : base + wide] = grad_gate.astype(turned_ref.dtype)
+        turned_ref[:, base + wide : base + 2 * wide] = (grad_hidden * silu).astype(turned_ref.dtype)
+
+
+def spread_kernel(left_ref, near_ref, over_x_ref, over_y_ref, over_xy_ref, send_ref, keep_ref):
+    floats = jnp.float32
+    half, width = near_ref.shape
+    rows = left_ref.shape[0] // 2
+    for base, (first, second) in ((0, (near_ref, over_y_ref)), (half, (over_x_ref, over_xy_ref))):
+        for goal, lines in ((send_ref, slice(rows, 2 * rows)), (keep_ref, slice(0, rows))):
+            product = lax.dot_general(
+                left_ref[lines, :width], first[...], (((1,), (1,)), ((), ())), preferred_element_type=floats
+            )
+            product = product + lax.dot_general(
+                left_ref[lines, width:], second[...], (((1,), (1,)), ((), ())), preferred_element_type=floats
+            )
+            goal[:, base : base + half] = product.astype(goal.dtype)
+
+
 def whole_specs(count):
     return [pl.BlockSpec(memory_space=pltpu.VMEM)] * count
+
+
+def remote_call(kernel, number, shapes, scratch, name):
+    def call(*operands):
+        return pl.pallas_call(
+            kernel,
+            out_shape=shapes,
+            in_specs=whole_specs(len(operands)),
+            out_specs=tuple(whole_specs(len(shapes))),
+            scratch_shapes=scratch,
+            compiler_params=pltpu.CompilerParams(collective_id=number, has_side_effects=True),
+            name=name,
+        )(*operands)
+
+    return call
 
 
 def lane_tables(offset):
@@ -736,14 +1330,13 @@
     return held
 
 
-def widen(parts, at_z, first):
-    held = line_trade(parts, at_z)
-    held = held.reshape(held.shape[0] * held.shape[1], held.shape[2])
-    if first == "y":
-        held = jnp.concatenate([held, flip(held, "y")], axis=1)
-        return jnp.concatenate([held, flip(held, "x")], axis=0)
-    held = jnp.concatenate([held, flip(held, "x")], axis=0)
-    return jnp.concatenate([held, flip(held, "y")], axis=1)
+def widen(parts, at_z):
+    near = line_trade(parts, at_z)
+    near = near.reshape(near.shape[0] * near.shape[1], near.shape[2])
+    half = near.shape[0] // 2
+    over_x, over_y = flip(near, "x"), flip(near, "y")
+    over_xy = jnp.concatenate([flip(over_x[:half], "y"), flip(over_y[half:], "x")], axis=0)
+    return (near, over_x, over_y, over_xy)
 
 
 def narrow(total, at_z, first):
@@ -860,12 +1453,21 @@
 
     input_wide = own_rows(block_input).astype(floats)
     gain1, shift1, gain2, shift2 = (features(v) for v in (ln1_gain, ln1_bias, ln2_gain, ln2_bias))
-    first_norm, normed1, inverse1 = layer_norm(input_wide, gain1, shift1)
-    first_low = line_gather(first_norm.astype(halves), at_z)
-    full_qkv = widen(part_qkv, at_z, "y")
-    full_out = widen(part_out, at_z, "y")
-    full_gate_up = widen(part_gate_up, at_z, "x")
-    full_down = widen(part_down, at_z, "y")
+    first_norm = layer_norm(input_wide, gain1, shift1)[0]
+    half_rows = model_width // 2
+    piece = jax.ShapeDtypeStruct((half_rows, 3 * cut), halves)
+    full_shape = jax.ShapeDtypeStruct((tokens, model_width), halves)
+    dma = pltpu.SemaphoreType.DMA
+    first_low, *pieces_qkv = remote_call(
+        open_kernel,
+        1,
+        (full_shape, piece, piece, piece, piece),
+        [dma((2,))] + gather_scratch() + [dma((LINE - 1,))] * 2 + [dma((3, LINE))] * 2,
+        "open",
+    )(first_norm.astype(halves), part_qkv)
+    pieces_out = widen(part_out, at_z)
+    pieces_gate_up = widen(part_gate_up, at_z)
+    pieces_down = widen(part_down, at_z)
     grad_rows = line_gather(own_rows(grad_y), at_z)
 
     own_bias = lax.dynamic_slice_in_dim(qkv_bias, at_z * cut, cut, 1)
@@ -873,10 +1475,10 @@
     projected = pl.pallas_call(
         qkv_kernel,
         out_shape=jax.ShapeDtypeStruct((2, 3, tokens, cut), halves),
-        in_specs=whole_specs(6),
+        in_specs=whole_specs(9),
         out_specs=pl.BlockSpec(memory_space=pltpu.VMEM),
         name="project",
-    )(first_low, full_qkv, bias_parts, *row_tables)
+    )(first_low, *pieces_qkv, bias_parts, *row_tables)
     crossed = at_x ^ at_y
     qkv_own = lax.dynamic_index_in_dim(projected, crossed, 0, keepdims=False)
     qkv_other = flip(lax.dynamic_index_in_dim(projected, 1 - crossed, 0, keepdims=False), "x")
@@ -900,46 +1502,67 @@
 
     attended = join_heads(out_own, flip(out_other, "x"))
     half = tokens // 2
-
-    def spread(left, right):
-        send = lax.dot_general(
-            left[half:], right, (((1,), (1,)), ((), ())), preferred_element_type=floats
-        ).astype(halves)
-        keep = lax.dot_general(
-            left[:half], right, (((1,), (1,)), ((), ())), preferred_element_type=floats
-        )
-        return line_reduce(keep, send)
-
-    residual = input_wide + spread(attended, full_out)
-    second_norm, normed2, inverse2 = layer_norm(residual, gain2, shift2)
-    second_low = line_gather(second_norm.astype(halves), at_z)
-    gate_up = jnp.dot(second_low, full_gate_up, preferred_element_type=floats)
-    gate_up = gate_up.reshape(tokens, 2, 2, wide)
-    gate, up_part = gate_up[:, :, 0], gate_up[:, :, 1]
-    sigmoid_gate = jax.nn.sigmoid(gate)
-    hidden = (gate * sigmoid_gate * up_part).astype(halves).reshape(tokens, 2 * wide)
-    grad_hidden = jnp.dot(grad_rows, full_down, preferred_element_type=floats)
-    grad_hidden = grad_hidden.reshape(tokens, 2, wide)
-    grad_gate = grad_hidden * up_part * sigmoid_gate * (1.0 + gate * (1.0 - sigmoid_gate))
-    grad_upper = grad_hidden * gate * sigmoid_gate
-    grad_gate_up = jnp.stack([grad_gate, grad_upper], axis=2).astype(halves)
-    grad_gate_up = grad_gate_up.reshape(tokens, 4 * wide)
-
-    grad_second = spread(grad_gate_up, full_gate_up)
-    block_output = spread_output(residual + spread(hidden, full_down))
+    send_shape = jax.ShapeDtypeStruct((half, model_width), halves)
+    keep_shape = jax.ShapeDtypeStruct((half, model_width), floats)
+    own_shape = jax.ShapeDtypeStruct((QUARTER, model_width), floats)
+    acc = pltpu.VMEM((CHUNK, model_width), floats)
+
+    def spread(left, pieces):
+        return pl.pallas_call(
+            spread_kernel,
+            out_shape=(send_shape, keep_shape),
+            in_specs=whole_specs(5),
+            out_specs=tuple(whole_specs(2)),
+            name="spread",
+        )(left, *pieces)
+
+    second_low, residual = remote_call(
+        middle_kernel,
+        2,
+        (full_shape, own_shape),
+        [acc] + reduce_scratch(model_width) + gather_scratch(),
+        "middle",
+    )(*spread(attended, pieces_out), input_wide, gain2[None, :], shift2[None, :])
+    step_rows = tokens // 2
+    hidden, grad_gate_up = pl.pallas_call(
+        feed_kernel,
+        out_shape=(
+            jax.ShapeDtypeStruct((tokens, 2 * wide), halves),
+            jax.ShapeDtypeStruct((tokens, 4 * wide), halves),
+        ),
+        grid=(tokens // step_rows,),
+        in_specs=[pl.BlockSpec((step_rows, model_width), lambda row: (row, 0))] * 2 + whole_specs(8),
+        out_specs=(
+            pl.BlockSpec((step_rows, 2 * wide), lambda row: (row, 0)),
+            pl.BlockSpec((step_rows, 4 * wide), lambda row: (row, 0)),
+        ),
+        name="feed",
+    )(second_low, grad_rows, *pieces_gate_up, *pieces_down)
+    residual_low, grad_residual, sums2 = remote_call(
+        middle_back_kernel,
+        3,
+        (full_shape, own_shape, jax.ShapeDtypeStruct((8, model_width), floats)),
+        [acc] + reduce_scratch(model_width) + gather_scratch(),
+        "middle_back",
+    )(*spread(grad_gate_up, pieces_gate_up), residual, own_rows(grad_y), gain2[None, :])
+    (second_low, grad_rows, hidden, grad_gate_up, out_left) = lax.optimization_barrier(
+        (second_low, grad_rows, hidden, grad_gate_up, hidden, residual_low)
+    )[:5]
+    out_send, out_keep = spread(out_left, pieces_down)
+    block_output = spread_output(residual + line_reduce(out_keep, out_send))
 
     def product(left_rows, right_rows):
         return lax.dot_general(
             left_rows, right_rows, (((0,), (0,)), ((), ())), preferred_element_type=floats
         )
 
-    grad_own = own_rows(grad_y).astype(floats)
+    out_near, out_x, out_y, out_xy = pieces_out
+    full_out = jnp.concatenate(
+        [jnp.concatenate([out_near, out_y], axis=1), jnp.concatenate([out_x, out_xy], axis=1)], axis=0
+    )
+    grad_attended = jnp.dot(residual_low, full_out, preferred_element_type=floats).astype(halves)
     g_gate_up = narrow(product(second_low, grad_gate_up), at_z, "x")
     g_down = narrow(product(grad_rows, hidden), at_z, "y")
-    grad_residual = grad_own + norm_back(grad_second, normed2, inverse2, gain2)
-    low_own = grad_residual.astype(halves)
-    residual_low = line_gather(low_own, at_z)
-    grad_attended = jnp.dot(residual_low, full_out, preferred_element_type=floats).astype(halves)
     grad_near, grad_far = grad_attended[:, :cut], grad_attended[:, cut:]
     grad_mine = jnp.where(crossed == 0, grad_near, grad_far)
     grad_their = flip(jnp.where(crossed == 0, grad_far, grad_near), "x")
@@ -980,23 +1603,39 @@
     near = jnp.where(crossed == 0, back_own, came_back)
     far = jnp.where(crossed == 0, came_back, back_own)
     grad_qkv = jnp.concatenate([near[0], near[1], near[2], far[0], far[1], far[2]], axis=1)
-    grad_first = spread(grad_qkv, full_qkv)
+    rows_wide = jax.ShapeDtypeStruct((2, shard_len, model_width), halves)
+    early = jnp.roll(sums2, 2, axis=0)
+    grad_input, sums = remote_call(
+        last_kernel,
+        4,
+        (rows_wide, jax.ShapeDtypeStruct((8, model_width), floats)),
+        [acc]
+        + reduce_scratch(model_width)
+        + [
+            dma((3, CHUNKS)),
+            dma((3, CHUNKS)),
+            pltpu.VMEM((4, 8, model_width), floats),
+            pltpu.VMEM((3, 8, model_width), floats),
+            pltpu.VMEM((LINE, 8, model_width), floats),
+            dma((3,)),
+            dma((3,)),
+            dma((LINE - 1,)),
+            dma((LINE - 1,)),
+        ],
+        "last",
+    )(*spread(grad_qkv, pieces_qkv), input_wide, grad_residual, gain1[None, :], early)
+    sums = plain_features(sums[:4])
     g_qkv = narrow(product(first_low, grad_qkv), at_z, "y")
     g_out = narrow(product(residual_low, attended), at_z, "y")
-    grad_input = spread_output(grad_residual + norm_back(grad_first, normed1, inverse1, gain1))
-
-    sums = jnp.stack(
-        [
-            jnp.sum(grad_first * normed1, axis=0),
-            jnp.sum(grad_first, axis=0),
-            jnp.sum(grad_second * normed2, axis=0),
-            jnp.sum(grad_second, axis=0),
-        ]
-    )
-    sums = lax.psum(plain_features(sums), ("z", "x", "y", "c"))
-    bias_all = lax.all_gather(bias_sums, ("z", "x", "y"), axis=0)
-    bias_all = jnp.sum(bias_all.reshape(LINE, 2, 2, 3, cut), axis=2)
-    bias_all = lax.dynamic_index_in_dim(bias_all, at_y, 1, keepdims=False)
+    bias_sums = bias_sums + flip(bias_sums, "y")
+    bias_sums = jnp.where(crossed == 0, bias_sums, flip(bias_sums, "x"))
+    bias_all = jnp.zeros((LINE, 3, cut), floats)
+    bias_all = lax.dynamic_update_slice_in_dim(bias_all, bias_sums[None], at_z, 0)
+    for step in range(1, LINE):
+        came = lax.ppermute(bias_sums, "z", [(k, (k + step) % LINE) for k in range(LINE)])
+        bias_all = lax.dynamic_update_slice_in_dim(
+            bias_all, came[None], lax.rem(at_z + LINE - step, LINE), 0
+        )
     g_bias = jnp.swapaxes(bias_all, 0, 1).reshape(3, head_cols)
 
     def columns(parts, offset, size, count):

time: 1010 us -> 863 us (0.85)
  Pallas kernels: 65.3 us -> 380 us
  waiting for transfers between devices: 411 us -> 205 us
  blocking collectives: 96.2 us -> 0 us
  starting transfers between devices: 174 us -> 117 us
  matrix products: 69.9 us -> 24.2 us
  other arithmetic: 84.9 us -> 52.3 us
  local copies, waits for them, and re-layouts: 95.5 us -> 76.8 us
    pallas_call x0 -> x9, Pallas kernels: none -> 323 us  [the longest x4 268 us: call(): pl.pallas_call(kernel, out_shape=shapes, in_specs=whole_specs(len(operand...]
    ppermute x12 -> x3, waiting for transfers between devices: 78.7 us -> 0.01 us  [line_gather(): lax.ppermute(above[-1], 'z', [(k, k + 1) for k in range(step - 1, LINE -...]
    psum x1 -> x0, blocking collectives: 57.7 us -> none  [block_device(): sums = lax.psum(plain_features(sums), ('z', 'x', 'y', 'c'))]
    ppermute x12 -> x3, waiting for transfers between devices: 56.3 us -> 4.24 us  [line_reduce(): lax.ppermute(falling.astype(jnp.bfloat16), 'z', [(k, k - 1) for k in rang...]
    dot_general x10 -> x0, matrix products: 47.1 us -> none  [the longest x4 17.3 us: spread(): lax.dot_general(left[half:], right, (((1,), (1,)), ((), ())), preferred_e...]
    all_gather x1 -> x0, blocking collectives: 38.5 us -> none  [block_device(): bias_all = lax.all_gather(bias_sums, ('z', 'x', 'y'), axis=0)]
    ppermute x45 -> x34, waiting for transfers between devices: 164 us -> 128 us  [flip(): return lax.ppermute(block, axis, FLIP)]
    ppermute x24 -> x21, waiting for transfers between devices: 99.6 us -> 68.2 us  [line_trade(): lax.ppermute(going, 'z', [(k, (k + step) % LINE) for k in range(LINE)])]
  transfers between devices with their start and end apart: 117 -> 70, of which waited for: 42 -> 25; matrix products, arithmetic and copies ran while one was open for 18% -> 16% of each run, Pallas kernels for 7% -> 31%
where the time goes in v2:
time: 863 us; the launch traced here: 858 us
  Pallas kernels  380 us (44%)
  waiting for transfers between devices  205 us (24%)
  starting transfers between devices  117 us (14%)
  local copies, waits for them, and re-layouts  76.8 us (9%)
  other arithmetic  52.3 us (6%)
  matrix products  24.2 us (3%)
    pallas_call x4, Pallas kernels, call(): pl.pallas_call(kernel, out_shape=shapes, in_specs=whole_specs(len(operand...  268 us
    ppermute x34, waiting for transfers between devices, flip(): return lax.ppermute(block, axis, FLIP)  128 us
    ppermute x21, waiting for transfers between devices, line_trade(): lax.ppermute(going, 'z', [(k, (k + step) % LINE) for k in range(LINE)])  68.2 us
    ppermute x34, starting transfers between devices, flip(): return lax.ppermute(block, axis, FLIP)  37.8 us
    ppermute x21, starting transfers between devices, line_trade(): lax.ppermute(going, 'z', [(k, (k + step) % LINE) for k in range(LINE)])  37.1 us
    pallas_call x4, Pallas kernels, spread(): pl.pallas_call(spread_kernel, out_shape=(send_shape, keep_shape), in_spec...  36.1 us
    unnamed x162, local copies, waits for them, and re-layouts  29.6 us
    pallas_call x1, Pallas kernels, block_device(): pl.pallas_call(functools.partial(attend_back_kernel, block), out_shape=(q...  23.7 us
  transfers between devices with their start and end apart: 70, of which 25 were waited for; matrix products, arithmetic and copies ran while one was open for 16% of the time, Pallas kernels for 31%

profile of v2, /device:TPU:24, one launch (start us, length us, event | category | flops | bytes accessed | tf_op | source)
XLA Modules:
  0.0 857.9 jit_solution(13002669693189338091)
XLA Ops:
  11.8 3.4 collective-permute-start.27
  26.1 2.3 fusion.73
  30.9 3.2 fusion.18
  34.1 5.9 fusion.5
  48.3 53.6 %open.1 = (bf16[1024,2048]{1,0:T(8,128)(2,1)}, bf16[1024,384]{1,0:T(8,128)(2,1)}, bf16[1024,384]{1,0:T(8,128)(2,1)}, bf16[1024,384]{1,0:T(8,128)(2,1)}, bf16[1024,384]{1,0:T(8,128)(2,1)}) custom-call(bf16[128,2048]{1,0:T(8,128)(2,1)} %add_convert_fusion.4.own_ref, bf16[4,256,384]{2,1,0:T(8,128)(2,1)} %pad_maximum_fusion.2.part_ref), custom_call_target="tpu_custom_call" | custom-call | tf_op jit(solution)/shard_map/open/pallas_call | solution.py:1264
  103.3 9.5 %project.1 = bf16[2,3,1024,128]{3,2,1,0:T(8,128)(2,1)} custom-call(bf16[1024,2048]{1,0:T(8,128)(2,1)} %get-tuple-element.44.rows_ref, bf16[1024,384]{1,0:T(8,128)(2,1)} %get-tuple-element.45.near_ref, bf16[1024,384]{1,0:T(8,128)(2,1)} %get-tuple-element.46.over_x_ref, bf16[1024,384]{1,0:T(8,128)(2,1)} %get-tuple-element.47.over_y_ref, ...), custom_call_target="tpu_custom_call" | custom-call | tf_op jit(solution)/shard_map/project/pallas_call | solution.py:1475
  112.9 3.0 collective-permute-start.29
  120.5 2.6 dynamic-slice_bitcast_fusion
  130.5 5.3 collective-permute-done.20
  135.9 19.4 %collective-permute-start.10 = (bf16[128,2048]{1,0:T(8,128)(2,1)S(1)}, bf16[128,2048]{1,0:T(8,128)(2,1)}, u32[]{:S(2)}, u32[]{:S(2)}) collective-permute-start(bf16[128,2048]{1,0:T(8,128)(2,1)S(1)} %get-tuple-element.162.grad_ref), channel_id=1, source_target_pairs={{8,0},{16,8},{24,16},{9,1},{17,9},{25,17},{10,2},{18,10},{26,18},{... | collective-permute-start | bytes 1572872 | tf_op jit(solution)/shard_map/ppermute | solution.py:1294
  155.3 5.2 collective-permute-done.21
  169.3 23.5 %attend.1 = (bf16[1024,128]{1,0:T(8,128)(2,1)}, bf16[1024,128]{1,0:T(8,128)(2,1)}, f32[2,2048]{1,0:T(2,128)}) custom-call(s32[3]{0:T(128)} %pad_add_fusion.place_ref, s32[8]{0:T(128)} %and_select_fusion.2.first_ref, s32[1,2048]{1,0:T(1,128)} %bitcast.225, bf16[3,1024,128]{2,1,0:T(8,128)(2,1)} %get-tuple-element.137.own_ref, ...), custom_call_target="tpu_custom_call" | custom-call | tf_op jit(solution)/shard_map/attend/pallas_call | solution.py:1488
  198.5 1.8 slice.266
  200.3 6.5 collective-permute-start.32
  206.9 1.8 slice.267
  213.1 5.9 spread.4
  219.0 79.5 %middle.1 = (bf16[1024,2048]{1,0:T(8,128)(2,1)}, f32[128,2048]{1,0:T(8,128)}) custom-call(bf16[512,2048]{1,0:T(8,128)(2,1)} %get-tuple-element.51.send_ref, f32[512,2048]{1,0:T(8,128)} %get-tuple-element.52.keep_ref, f32[128,2048]{1,0:T(8,128)} %fusion.70.base_ref, f32[1,2048]{1,0:T(1,128)} %bitcast.229, f32[1,2048]{1,0:T(1,128)} %bitcast.231), custom_call_target="tpu_custom_call" | custom-call | tf_op jit(solution)/shard_map/middle/pallas_call | solution.py:1264
  303.0 2.3 constant_dynamic-update-slice_fusion.8
  305.5 2.0 constant_dynamic-update-slice_fusion.7
  307.9 2.0 constant_dynamic-update-slice_fusion.6
  309.9 25.5 %collective-permute-done.23.up_x.over_x_ref = bf16[1024,768]{1,0:T(8,128)(2,1)S(1)} collective-permute-done((bf16[1024,768]{1,0:T(8,128)(2,1)S(1)}, bf16[1024,768]{1,0:T(8,128)(2,1)S(1)}, u32[]{:S(2)}, u32[]{:S(2)}) %collective-permute-start.23) | collective-permute-done | bytes 1572896 | tf_op jit(solution)/shard_map/ppermute | solution.py:427
  335.5 2.3 constant_dynamic-update-slice_fusion.5
  341.9 13.5 %collective-permute-done.25 = bf16[512,768]{1,0:T(8,128)(2,1)S(1)} collective-permute-done((bf16[512,768]{1,0:T(8,128)(2,1)S(1)}, bf16[512,768]{1,0:T(8,128)(2,1)S(1)}, u32[]{:S(2)}, u32[]{:S(2)}) %collective-permute-start.25) | collective-permute-done | bytes 786464 | tf_op jit(solution)/shard_map/ppermute | solution.py:427
  355.5 2.0 collective-permute-done.26
  358.7 18.4 %feed.1 = (bf16[1024,768]{1,0:T(8,128)(2,1)}, bf16[1024,1536]{1,0:T(8,128)(2,1)}) custom-call(bf16[1024,2048]{1,0:T(8,128)(2,1)} %get-tuple-element.73.low_ref, bf16[1024,2048]{1,0:T(8,128)(2,1)} %constant_dynamic-update-slice_fusion.2.grad_ref, bf16[1024,768]{1,0:T(8,128)(2,1)} %bitcast.187, bf16[1024,768]{1,0:T(8,128)(2,1)} %copy-done.5, ...), custom_call_target="tpu_custom_call" | custom-call | tf_op jit(solution)/shard_map/feed/pallas_call | solution.py:1527
  377.1 12.5 %spread.5 = (bf16[512,2048]{1,0:T(8,128)(2,1)}, f32[512,2048]{1,0:T(8,128)}) custom-call(bf16[1024,1536]{1,0:T(8,128)(2,1)} %get-tuple-element.74.left_ref, bf16[1024,768]{1,0:T(8,128)(2,1)} %bitcast.188, bf16[1024,768]{1,0:T(8,128)(2,1)} %copy-done.5, bf16[1024,768]{1,0:T(8,128)(2,1)} %copy-done.6, bf16[1024,768]{1,0:T(8,128)(2,1)} %copy-done.7), custom_call_target="tpu_custom_call" | custom-call | tf_op jit(solution)/shard_map/spread/pallas_call | solution.py:1511
  389.6 69.9 %middle_back.1 = (bf16[1024,2048]{1,0:T(8,128)(2,1)}, f32[128,2048]{1,0:T(8,128)}, f32[8,2048]{1,0:T(8,128)}) custom-call(bf16[512,2048]{1,0:T(8,128)(2,1)} %get-tuple-element.57.send_ref, f32[512,2048]{1,0:T(8,128)} %get-tuple-element.58.keep_ref, f32[128,2048]{1,0:T(8,128)} %get-tuple-element.53.residual_ref, bf16[128,2048]{1,0:T(8,128)(2,1)} %copy-done.18, ...), custom_call_target="tpu_custom_call" | custom-call | tf_op jit(solution)/shard_map/middle_back/pallas_call | solution.py:1264
  459.6 8.9 %spread.6 = (bf16[512,2048]{1,0:T(8,128)(2,1)}, f32[512,2048]{1,0:T(8,128)}) custom-call(bf16[1024,768]{1,0:T(8,128)(2,1)} %get-tuple-element.76.left_ref, bf16[1024,384]{1,0:T(8,128)(2,1)} %bitcast.192, bf16[1024,384]{1,0:T(8,128)(2,1)} %collective-permute-done.30.down_x.over_x_ref, bf16[1024,384]{1,0:T(8,128)(2,1)} %collective-permute-done.31.down_y.over_y_ref, ...), custom_call_target="tpu_custom_call" | custom-call | tf_op jit(solution)/shard_map/spread/pallas_call | solution.py:1511
  469.1 3.7 convolution_convert_fusion
  476.5 1.8 collective-permute-start.55
  478.3 3.3 collective-permute-done.43.grad_other
  482.4 23.7 %attend_back.1 = (bf16[3,1024,128]{2,1,0:T(8,128)(2,1)}, bf16[3,1024,128]{2,1,0:T(8,128)(2,1)}, f32[3,128]{1,0:T(4,128)}) custom-call(s32[3]{0:T(128)} %pad_add_fusion.place_ref, s32[8]{0:T(128)} %convert_reduce_fusion.1.last_ref, s32[1,2048]{1,0:T(1,128)} %bitcast.226, bf16[3,1024,128]{2,1,0:T(8,128)(2,1)} %get-tuple-element.137.own_ref, ...), custom_call_target="tpu_custom_call" | custom-call | tf_op jit(solution)/shard_map/attend_back/pallas_call | solution.py:1571
  506.1 5.7 collective-permute-start.50
  511.8 9.6 %fusion.77 = f32[2048,1536]{1,0:T(8,128)S(1)} fusion(bf16[1024,2048]{1,0:T(8,128)(2,1)} %get-tuple-element.73.low_ref, bf16[1024,1536]{1,0:T(8,128)(2,1)} %get-tuple-element.74.left_ref), kind=kOutput, calls=%fused_computation.295 | convolution fusion | flops 6442450944 | bytes 19922944 | tf_op jit(solution)/shard_map/dot_general | solution.py:1555
  521.4 2.0 slice.422
  528.4 3.7 fusion.78
  532.1 60.5 %collective-permute-done.51 = f32[3,128]{1,0:T(4,128)S(1)} collective-permute-done((f32[3,128]{1,0:T(4,128)S(1)}, f32[3,128]{1,0:T(4,128)S(1)}, u32[]{:S(2)}, u32[]{:S(2)}) %collective-permute-start.51) | collective-permute-done | bytes 1568 | tf_op jit(solution)/shard_map/ppermute | solution.py:427
  597.2 4.6 collective-permute-done.56
  601.7 2.3 collective-permute-start.54
  608.6 5.8 collective-permute-done.58
  615.3 5.6 collective-permute-done.59
  628.1 8.8 %spread.7 = (bf16[512,2048]{1,0:T(8,128)(2,1)}, f32[512,2048]{1,0:T(8,128)}) custom-call(bf16[1024,768]{1,0:T(8,128)(2,1)} %fusion.29.left_ref, bf16[1024,384]{1,0:T(8,128)(2,1)} %get-tuple-element.45.near_ref, bf16[1024,384]{1,0:T(8,128)(2,1)} %get-tuple-element.46.over_x_ref, bf16[1024,384]{1,0:T(8,128)(2,1)} %get-tuple-element.47.over_y_ref, ...), custom_call_target="tpu_custom_call" | custom-call | tf_op jit(solution)/shard_map/spread/pallas_call | solution.py:1511
  636.9 65.3 %last.1 = (bf16[2,256,2048]{2,1,0:T(8,128)(2,1)}, f32[8,2048]{1,0:T(8,128)}) custom-call(bf16[512,2048]{1,0:T(8,128)(2,1)} %get-tuple-element.66.send_ref, f32[512,2048]{1,0:T(8,128)} %get-tuple-element.67.keep_ref, f32[128,2048]{1,0:T(8,128)} %fusion.70.base_ref, f32[128,2048]{1,0:T(8,128)} %get-tuple-element.68.turned_ref, f32[1,2048]{1,0:T(1,128)} %bitcast.228, ...), custom_call_target="tpu_custom_call" | custom-call | tf_op jit(solution)/shard_map/last/pallas_call | solution.py:1264
  703.2 5.8 fusion.76
  710.4 2.8 slice_add_fusion.1
  714.0 2.2 convert_add_fusion
  718.2 13.8 %collective-permute-done.66 = bf16[1024,384]{1,0:T(8,128)(2,1)S(1)} collective-permute-done((bf16[1024,384]{1,0:T(8,128)(2,1)S(1)}, bf16[1024,384]{1,0:T(8,128)(2,1)S(1)}, u32[]{:S(2)}, u32[]{:S(2)}) %collective-permute-start.66) | collective-permute-done | bytes 786464 | tf_op jit(solution)/shard_map/ppermute | solution.py:427
  736.8 2.3 collective-permute-done.67
  739.1 9.9 %collective-permute-start.69 = (bf16[1,256,384]{2,1,0:T(8,128)(2,1)S(1)}, bf16[1,256,384]{2,1,0:T(8,128)(2,1)S(1)}, u32[]{:S(2)}, u32[]{:S(2)}) collective-permute-start(bf16[1,256,384]{2,1,0:T(8,128)(2,1)S(1)} %get-tuple-element.142), channel_id=1, source_target_pairs={{0,24},{8,0},{16,8},{24,16},{1,25},{9,1},{17,9},{25,17},{2,26},{10... | collective-permute-start | bytes 589832 | tf_op jit(solution)/shard_map/ppermute | solution.py:1328
  752.8 4.9 collective-permute-start.36
  759.9 4.2 collective-permute-done.36
  766.1 5.0 collective-permute-start.37
  774.0 2.8 slice_add_fusion
  778.5 2.5 collective-permute-start.48
  781.0 4.5 collective-permute-done.47
  785.5 5.2 collective-permute-start.49
  793.0 4.8 collective-permute-done.48
  800.3 3.0 collective-permute-done.40
  807.2 4.3 collective-permute-done.61
  811.5 2.7 fusion
  815.0 2.0 collective-permute-start.64
  817.4 6.9 collective-permute-done.62
  824.4 24.6 %collective-permute-done.63 = bf16[1,256,768]{2,1,0:T(8,128)(2,1)S(1)} collective-permute-done((bf16[1,256,768]{2,1,0:T(8,128)(2,1)S(1)}, bf16[1,256,768]{2,1,0:T(8,128)(2,1)S(1)}, u32[]{:S(2)}, u32[]{:S(2)}) %collective-permute-start.63) | collective-permute-done | bytes 393248 | tf_op jit(solution)/shard_map/ppermute | solution.py:1328
  849.7 3.8 copy.161
  (439 shorter events, 139.1 us)
Async XLA Ops:
  1.5 100.4 %collective-permute-start = (f32[3,128]{1,0:T(4,128)S(1)}, f32[3,128]{1,0:T(4,128)}, u32[]{:S(2)}, u32[]{:S(2)}) collective-permute-start(f32[3,128]{1,0:T(4,128)S(1)} %constant_dynamic-slice_fusion.26), channel_id=1, source_target_pairs={{0,2},{2,0},{1,3},{3,1},{4,6},{6,4},{5,7},{7,5},{8,10},{10,8},{9,1... | collective-permute-start | bytes 4616 | tf_op jit(solution)/shard_map/ppermute | solution.py:427
  4.9 108.0 %collective-permute-start.3 = (bf16[1,256,128]{2,1,0:T(8,128)(2,1)}, bf16[1,256,128]{2,1,0:T(8,128)(2,1)}, u32[]{:S(2)}, u32[]{:S(2)}) collective-permute-start(bf16[1,256,128]{2,1,0:T(8,128)(2,1)} %bitcast.24), channel_id=1, source_target_pairs={{0,8},{8,16},{16,24},{24,0},{1,9},{9,17},{17,25},{25,1},{2,10},{10... | collective-permute-start | bytes 196616 | tf_op jit(solution)/shard_map/ppermute | solution.py:1328
  5.8 110.8 %collective-permute-start.4 = (bf16[1,256,128]{2,1,0:T(8,128)(2,1)}, bf16[1,256,128]{2,1,0:T(8,128)(2,1)}, u32[]{:S(2)}, u32[]{:S(2)}) collective-permute-start(bf16[1,256,128]{2,1,0:T(8,128)(2,1)} %bitcast.25), channel_id=1, source_target_pairs={{0,16},{8,24},{16,0},{24,8},{1,17},{9,25},{17,1},{25,9},{2,18},{10... | collective-permute-start | bytes 196616 | tf_op jit(solution)/shard_map/ppermute | solution.py:1328
  8.3 109.3 %collective-permute-start.5 = (bf16[1,256,128]{2,1,0:T(8,128)(2,1)}, bf16[1,256,128]{2,1,0:T(8,128)(2,1)}, u32[]{:S(2)}, u32[]{:S(2)}) collective-permute-start(bf16[1,256,128]{2,1,0:T(8,128)(2,1)} %bitcast.26), channel_id=1, source_target_pairs={{0,24},{8,0},{16,8},{24,16},{1,25},{9,1},{17,9},{25,17},{2,26},{10... | collective-permute-start | bytes 196616 | tf_op jit(solution)/shard_map/ppermute | solution.py:1328
  11.8 111.3 %collective-permute-start.27 = (bf16[1,256,384]{2,1,0:T(8,128)(2,1)}, bf16[1,256,384]{2,1,0:T(8,128)(2,1)}, u32[]{:S(2)}, u32[]{:S(2)}) collective-permute-start(bf16[1,256,384]{2,1,0:T(8,128)(2,1)} %bitcast.44), channel_id=1, source_target_pairs={{0,8},{8,16},{16,24},{24,0},{1,9},{9,17},{17,25},{25,1},{2,10},{10... | collective-permute-start | bytes 589832 | tf_op jit(solution)/shard_map/ppermute | solution.py:1328
  101.9 22.1 %collective-permute-start.28 = (bf16[1,256,384]{2,1,0:T(8,128)(2,1)}, bf16[1,256,384]{2,1,0:T(8,128)(2,1)}, u32[]{:S(2)}, u32[]{:S(2)}) collective-permute-start(bf16[1,256,384]{2,1,0:T(8,128)(2,1)} %bitcast.45), channel_id=1, source_target_pairs={{0,16},{8,24},{16,0},{24,8},{1,17},{9,25},{17,1},{25,9},{2,18},{10... | collective-permute-start | bytes 589832 | tf_op jit(solution)/shard_map/ppermute | solution.py:1328
  112.9 12.3 %collective-permute-start.29 = (bf16[1,256,384]{2,1,0:T(8,128)(2,1)}, bf16[1,256,384]{2,1,0:T(8,128)(2,1)S(1)}, u32[]{:S(2)}, u32[]{:S(2)}) collective-permute-start(bf16[1,256,384]{2,1,0:T(8,128)(2,1)} %bitcast.46), channel_id=1, source_target_pairs={{0,24},{8,0},{16,8},{24,16},{1,25},{9,1},{17,9},{25,17},{2,26},{10... | collective-permute-start | bytes 589832 | tf_op jit(solution)/shard_map/ppermute | solution.py:1328
  118.4 8.2 collective-permute-start.6
  120.0 8.2 collective-permute-start.7
  123.1 12.8 %collective-permute-start.20 = (bf16[1,256,768]{2,1,0:T(8,128)(2,1)S(1)}, bf16[1,256,768]{2,1,0:T(8,128)(2,1)S(1)}, u32[]{:S(2)}, u32[]{:S(2)}) collective-permute-start(bf16[1,256,768]{2,1,0:T(8,128)(2,1)S(1)} %copy-done.48), channel_id=1, source_target_pairs={{0,8},{8,16},{16,24},{24,0},{1,9},{9,17},{17,25},{25,1},{2,10},{10... | collective-permute-start | bytes 1179656 | tf_op jit(solution)/shard_map/ppermute | solution.py:1328
  124.0 36.4 %collective-permute-start.21 = (bf16[1,256,768]{2,1,0:T(8,128)(2,1)S(1)}, bf16[1,256,768]{2,1,0:T(8,128)(2,1)S(1)}, u32[]{:S(2)}, u32[]{:S(2)}) collective-permute-start(bf16[1,256,768]{2,1,0:T(8,128)(2,1)S(1)} %copy-done.47), channel_id=1, source_target_pairs={{0,16},{8,24},{16,0},{24,8},{1,17},{9,25},{17,1},{25,9},{2,18},{10... | collective-permute-start | bytes 1179656 | tf_op jit(solution)/shard_map/ppermute | solution.py:1328
  125.1 40.8 %collective-permute-start.1 = (bf16[3,1024,128]{2,1,0:T(8,128)(2,1)}, bf16[3,1024,128]{2,1,0:T(8,128)(2,1)}, u32[]{:S(2)}, u32[]{:S(2)}) collective-permute-start(bf16[3,1024,128]{2,1,0:T(8,128)(2,1)} %get-tuple-element.136), channel_id=1, source_target_pairs={{0,4},{4,0},{1,5},{5,1},{2,6},{6,2},{3,7},{7,3},{8,12},{12,8},{9,1... | collective-permute-start | bytes 2359304 | tf_op jit(solution)/shard_map/ppermute | solution.py:427
  126.6 35.2 %collective-permute-start.22 = (bf16[1,256,768]{2,1,0:T(8,128)(2,1)}, bf16[1,256,768]{2,1,0:T(8,128)(2,1)}, u32[]{:S(2)}, u32[]{:S(2)}) collective-permute-start(bf16[1,256,768]{2,1,0:T(8,128)(2,1)} %get-tuple-element.132), channel_id=1, source_target_pairs={{0,24},{8,0},{16,8},{24,16},{1,25},{9,1},{17,9},{25,17},{2,26},{10... | collective-permute-start | bytes 1179656 | tf_op jit(solution)/shard_map/ppermute | solution.py:1328
  128.2 37.2 %collective-permute-start.11 = (bf16[128,2048]{1,0:T(8,128)(2,1)S(1)}, bf16[128,2048]{1,0:T(8,128)(2,1)}, u32[]{:S(2)}, u32[]{:S(2)}) collective-permute-start(bf16[128,2048]{1,0:T(8,128)(2,1)S(1)} %get-tuple-element.162.grad_ref), channel_id=1, source_target_pairs={{0,8},{8,16},{16,24},{1,9},{9,17},{17,25},{2,10},{10,18},{18,26},{... | collective-permute-start | bytes 1572872 | tf_op jit(solution)/shard_map/ppermute | solution.py:1297
  135.9 58.4 %collective-permute-start.10 = (bf16[128,2048]{1,0:T(8,128)(2,1)S(1)}, bf16[128,2048]{1,0:T(8,128)(2,1)}, u32[]{:S(2)}, u32[]{:S(2)}) collective-permute-start(bf16[128,2048]{1,0:T(8,128)(2,1)S(1)} %get-tuple-element.162.grad_ref), channel_id=1, source_target_pairs={{8,0},{16,8},{24,16},{9,1},{17,9},{25,17},{10,2},{18,10},{26,18},{... | collective-permute-start | bytes 1572872 | tf_op jit(solution)/shard_map/ppermute | solution.py:1294
  160.4 36.6 %collective-permute-start.30 = (bf16[1024,384]{1,0:T(8,128)(2,1)S(1)}, bf16[1024,384]{1,0:T(8,128)(2,1)}, u32[]{:S(2)}, u32[]{:S(2)}) collective-permute-start(bf16[1024,384]{1,0:T(8,128)(2,1)S(1)} %bitcast.189), channel_id=1, source_target_pairs={{0,4},{4,0},{1,5},{5,1},{2,6},{6,2},{3,7},{7,3},{8,12},{12,8},{9,1... | collective-permute-start | bytes 2359304 | tf_op jit(solution)/shard_map/ppermute | solution.py:427
  161.7 45.1 %collective-permute-start.31 = (bf16[1024,384]{1,0:T(8,128)(2,1)S(1)}, bf16[1024,384]{1,0:T(8,128)(2,1)}, u32[]{:S(2)}, u32[]{:S(2)}) collective-permute-start(bf16[1024,384]{1,0:T(8,128)(2,1)S(1)} %bitcast.190), channel_id=1, source_target_pairs={{0,2},{2,0},{1,3},{3,1},{4,6},{6,4},{5,7},{7,5},{8,10},{10,8},{9,1... | collective-permute-start | bytes 2359304 | tf_op jit(solution)/shard_map/ppermute | solution.py:427
  165.4 27.4 %collective-permute-start.8 = (bf16[512,128]{1,0:T(8,128)(2,1)}, bf16[512,128]{1,0:T(8,128)(2,1)}, u32[]{:S(2)}, u32[]{:S(2)}) collective-permute-start(bf16[512,128]{1,0:T(8,128)(2,1)} %slice.262), channel_id=1, source_target_pairs={{0,2},{2,0},{1,3},{3,1},{4,6},{6,4},{5,7},{7,5},{8,10},{10,8},{9,1... | collective-permute-start | bytes 393224 | tf_op jit(solution)/shard_map/ppermute | solution.py:427
  165.9 42.8 %collective-permute-start.12 = (bf16[128,2048]{1,0:T(8,128)(2,1)}, bf16[128,2048]{1,0:T(8,128)(2,1)}, u32[]{:S(2)}, u32[]{:S(2)}) collective-permute-start(bf16[128,2048]{1,0:T(8,128)(2,1)} %collective-permute-done.11), channel_id=1, source_target_pairs={{8,16},{16,24},{9,17},{17,25},{10,18},{18,26},{11,19},{19,27},{12,... | collective-permute-start | bytes 1572872 | tf_op jit(solution)/shard_map/ppermute | solution.py:1297
  192.8 7.5 collective-permute-start.9
  194.2 15.9 %collective-permute-start.2 = (bf16[1024,128]{1,0:T(8,128)(2,1)}, bf16[1024,128]{1,0:T(8,128)(2,1)S(1)}, u32[]{:S(2)}, u32[]{:S(2)}) collective-permute-start(bf16[1024,128]{1,0:T(8,128)(2,1)} %get-tuple-element.50.att_other), channel_id=1, source_target_pairs={{0,4},{4,0},{1,5},{5,1},{2,6},{6,2},{3,7},{7,3},{8,12},{12,8},{9,1... | collective-permute-start | bytes 786440 | tf_op jit(solution)/shard_map/ppermute | solution.py:427
  197.0 104.1 %collective-permute-start.14 = (bf16[128,2048]{1,0:T(8,128)(2,1)}, bf16[128,2048]{1,0:T(8,128)(2,1)}, u32[]{:S(2)}, u32[]{:S(2)}) collective-permute-start(bf16[128,2048]{1,0:T(8,128)(2,1)} %collective-permute-done.10), channel_id=1, source_target_pairs={{8,0},{16,8},{9,1},{17,9},{10,2},{18,10},{11,3},{19,11},{12,4},{20... | collective-permute-start | bytes 1572872 | tf_op jit(solution)/shard_map/ppermute | solution.py:1294
  200.3 98.3 %collective-permute-start.32 = (bf16[512,384]{1,0:T(8,128)(2,1)}, bf16[512,384]{1,0:T(8,128)(2,1)}, u32[]{:S(2)}, u32[]{:S(2)}) collective-permute-start(bf16[512,384]{1,0:T(8,128)(2,1)} %slice.266), channel_id=1, source_target_pairs={{0,2},{2,0},{1,3},{3,1},{4,6},{6,4},{5,7},{7,5},{8,10},{10,8},{9,1... | collective-permute-start | bytes 1179656 | tf_op jit(solution)/shard_map/ppermute | solution.py:427
  206.9 128.6 %collective-permute-start.16 = (bf16[128,2048]{1,0:T(8,128)(2,1)S(1)}, bf16[128,2048]{1,0:T(8,128)(2,1)}, u32[]{:S(2)}, u32[]{:S(2)}) collective-permute-start(bf16[128,2048]{1,0:T(8,128)(2,1)S(1)} %get-tuple-element.162.grad_ref), channel_id=1, source_target_pairs={{0,1},{1,0},{2,3},{3,2},{4,5},{5,4},{6,7},{7,6},{8,9},{9,8},{10,11... | collective-permute-start | bytes 1572872 | tf_op jit(solution)/shard_map/ppermute | solution.py:427
  208.7 92.5 %collective-permute-start.33 = (bf16[512,384]{1,0:T(8,128)(2,1)}, bf16[512,384]{1,0:T(8,128)(2,1)}, u32[]{:S(2)}, u32[]{:S(2)}) collective-permute-start(bf16[512,384]{1,0:T(8,128)(2,1)} %slice.267), channel_id=1, source_target_pairs={{0,4},{4,0},{1,5},{5,1},{2,6},{6,2},{3,7},{7,3},{8,12},{12,8},{9,1... | collective-permute-start | bytes 1179656 | tf_op jit(solution)/shard_map/ppermute | solution.py:427
  210.1 92.9 %collective-permute-start.13 = (bf16[128,2048]{1,0:T(8,128)(2,1)}, bf16[128,2048]{1,0:T(8,128)(2,1)}, u32[]{:S(2)}, u32[]{:S(2)}) collective-permute-start(bf16[128,2048]{1,0:T(8,128)(2,1)} %collective-permute-done.12), channel_id=1, source_target_pairs={{16,24},{17,25},{18,26},{19,27},{20,28},{21,29},{22,30},{23,31}} | collective-permute-start | bytes 1572872 | tf_op jit(solution)/shard_map/ppermute | solution.py:1297
  298.5 36.8 %collective-permute-start.23 = (bf16[1024,768]{1,0:T(8,128)(2,1)S(1)}, bf16[1024,768]{1,0:T(8,128)(2,1)S(1)}, u32[]{:S(2)}, u32[]{:S(2)}) collective-permute-start(bf16[1024,768]{1,0:T(8,128)(2,1)S(1)} %bitcast.185), channel_id=1, source_target_pairs={{0,4},{4,0},{1,5},{5,1},{2,6},{6,2},{3,7},{7,3},{8,12},{12,8},{9,1... | collective-permute-start | bytes 4718600 | tf_op jit(solution)/shard_map/ppermute | solution.py:427
  301.1 36.7 %collective-permute-start.24 = (bf16[1024,768]{1,0:T(8,128)(2,1)S(1)}, bf16[1024,768]{1,0:T(8,128)(2,1)S(1)}, u32[]{:S(2)}, u32[]{:S(2)}) collective-permute-start(bf16[1024,768]{1,0:T(8,128)(2,1)S(1)} %bitcast.186), channel_id=1, source_target_pairs={{0,2},{2,0},{1,3},{3,1},{4,6},{6,4},{5,7},{7,5},{8,10},{10,8},{9,1... | collective-permute-start | bytes 4718600 | tf_op jit(solution)/shard_map/ppermute | solution.py:427
  305.3 34.1 %collective-permute-start.17 = (bf16[128,2048]{1,0:T(8,128)(2,1)S(1)}, bf16[128,2048]{1,0:T(8,128)(2,1)S(1)}, u32[]{:S(2)}, u32[]{:S(2)}) collective-permute-start(bf16[128,2048]{1,0:T(8,128)(2,1)S(1)} %get-tuple-element.117), channel_id=1, source_target_pairs={{0,1},{1,0},{2,3},{3,2},{4,5},{5,4},{6,7},{7,6},{8,9},{9,8},{10,11... | collective-permute-start | bytes 1572872 | tf_op jit(solution)/shard_map/ppermute | solution.py:427
  307.5 32.7 %collective-permute-start.18 = (bf16[128,2048]{1,0:T(8,128)(2,1)S(1)}, bf16[128,2048]{1,0:T(8,128)(2,1)S(1)}, u32[]{:S(2)}, u32[]{:S(2)}) collective-permute-start(bf16[128,2048]{1,0:T(8,128)(2,1)S(1)} %get-tuple-element.115), channel_id=1, source_target_pairs={{0,1},{1,0},{2,3},{3,2},{4,5},{5,4},{6,7},{7,6},{8,9},{9,8},{10,11... | collective-permute-start | bytes 1572872 | tf_op jit(solution)/shard_map/ppermute | solution.py:427
  335.4 20.0 %collective-permute-start.25 = (bf16[512,768]{1,0:T(8,128)(2,1)S(1)}, bf16[512,768]{1,0:T(8,128)(2,1)S(1)}, u32[]{:S(2)}, u32[]{:S(2)}) collective-permute-start(bf16[512,768]{1,0:T(8,128)(2,1)S(1)} %slice.264), channel_id=1, source_target_pairs={{0,2},{2,0},{1,3},{3,1},{4,6},{6,4},{5,7},{7,5},{8,10},{10,8},{9,1... | collective-permute-start | bytes 2359304 | tf_op jit(solution)/shard_map/ppermute | solution.py:427
  337.9 19.6 %collective-permute-start.26 = (bf16[512,768]{1,0:T(8,128)(2,1)S(1)}, bf16[512,768]{1,0:T(8,128)(2,1)S(1)}, u32[]{:S(2)}, u32[]{:S(2)}) collective-permute-start(bf16[512,768]{1,0:T(8,128)(2,1)S(1)} %slice.265), channel_id=1, source_target_pairs={{0,4},{4,0},{1,5},{5,1},{2,6},{6,2},{3,7},{7,3},{8,12},{12,8},{9,1... | collective-permute-start | bytes 2359304 | tf_op jit(solution)/shard_map/ppermute | solution.py:427
  468.5 245.5 %collective-permute-start.34 = (bf16[512,2048]{1,0:T(8,128)(2,1)}, bf16[512,2048]{1,0:T(8,128)(2,1)}, u32[]{:S(2)}, u32[]{:S(2)}) collective-permute-start(bf16[512,2048]{1,0:T(8,128)(2,1)} %get-tuple-element.62), channel_id=1, source_target_pairs={{0,1},{1,0},{2,3},{3,2},{4,5},{5,4},{6,7},{7,6},{8,9},{9,8},{10,11... | collective-permute-start | bytes 6291464 | tf_op jit(solution)/shard_map/ppermute | solution.py:427
  473.6 8.1 collective-permute-start.43
  476.5 116.1 %collective-permute-start.55 = (bf16[2048,128]{1,0:T(8,128)(2,1)S(1)}, bf16[2048,128]{1,0:T(8,128)(2,1)S(1)}, u32[]{:S(2)}, u32[]{:S(2)}) collective-permute-start(bf16[2048,128]{1,0:T(8,128)(2,1)S(1)} %slice.428), channel_id=1, source_target_pairs={{0,2},{2,0},{1,3},{3,1},{4,6},{6,4},{5,7},{7,5},{8,10},{10,8},{9,1... | collective-permute-start | bytes 1572872 | tf_op jit(solution)/shard_map/ppermute | solution.py:427
  506.1 18.9 %collective-permute-start.50 = (f32[3,128]{1,0:T(4,128)}, f32[3,128]{1,0:T(4,128)S(1)}, u32[]{:S(2)}, u32[]{:S(2)}) collective-permute-start(f32[3,128]{1,0:T(4,128)} %get-tuple-element.72), channel_id=1, source_target_pairs={{0,2},{2,0},{1,3},{3,1},{4,6},{6,4},{5,7},{7,5},{8,10},{10,8},{9,1... | collective-permute-start | bytes 4616 | tf_op jit(solution)/shard_map/ppermute | solution.py:427
  523.5 250.5 %collective-permute-start.60 = (bf16[1024,1536]{1,0:T(8,128)(2,1)}, bf16[1024,1536]{1,0:T(8,128)(2,1)}, u32[]{:S(2)}, u32[]{:S(2)}) collective-permute-start(bf16[1024,1536]{1,0:T(8,128)(2,1)} %slice.422), channel_id=1, source_target_pairs={{0,4},{4,0},{1,5},{5,1},{2,6},{6,2},{3,7},{7,3},{8,12},{12,8},{9,1... | collective-permute-start | bytes 9437192 | tf_op jit(solution)/shard_map/ppermute | solution.py:427
  525.0 67.6 %collective-permute-start.51 = (f32[3,128]{1,0:T(4,128)S(1)}, f32[3,128]{1,0:T(4,128)S(1)}, u32[]{:S(2)}, u32[]{:S(2)}) collective-permute-start(f32[3,128]{1,0:T(4,128)S(1)} %add.441), channel_id=1, source_target_pairs={{0,4},{4,0},{1,5},{5,1},{2,6},{6,2},{3,7},{7,3},{8,12},{12,8},{9,1... | collective-permute-start | bytes 4616 | tf_op jit(solution)/shard_map/ppermute | solution.py:427
  592.8 8.9 %collective-permute-start.56 = (bf16[1024,128]{1,0:T(8,128)(2,1)S(1)}, bf16[1024,128]{1,0:T(8,128)(2,1)S(1)}, u32[]{:S(2)}, u32[]{:S(2)}) collective-permute-start(bf16[1024,128]{1,0:T(8,128)(2,1)S(1)} %slice.431), channel_id=1, source_target_pairs={{0,4},{4,0},{1,5},{5,1},{2,6},{6,2},{3,7},{7,3},{8,12},{12,8},{9,1... | collective-permute-start | bytes 786440 | tf_op jit(solution)/shard_map/ppermute | solution.py:427
  596.4 25.3 %collective-permute-start.44 = (bf16[3,1024,128]{2,1,0:T(8,128)(2,1)}, bf16[3,1024,128]{2,1,0:T(8,128)(2,1)S(1)}, u32[]{:S(2)}, u32[]{:S(2)}) collective-permute-start(bf16[3,1024,128]{2,1,0:T(8,128)(2,1)} %get-tuple-element.65), channel_id=1, source_target_pairs={{0,4},{4,0},{1,5},{5,1},{2,6},{6,2},{3,7},{7,3},{8,12},{12,8},{9,1... | collective-permute-start | bytes 2359304 | tf_op jit(solution)/shard_map/ppermute | solution.py:427
  596.9 7.3 collective-permute-start.53
  607.1 103.3 %collective-permute-start.65 = (bf16[2048,384]{1,0:T(8,128)(2,1)}, bf16[2048,384]{1,0:T(8,128)(2,1)}, u32[]{:S(2)}, u32[]{:S(2)}) collective-permute-start(bf16[2048,384]{1,0:T(8,128)(2,1)} %slice.423), channel_id=1, source_target_pairs={{0,2},{2,0},{1,3},{3,1},{4,6},{6,4},{5,7},{7,5},{8,10},{10,8},{9,1... | collective-permute-start | bytes 4718600 | tf_op jit(solution)/shard_map/ppermute | solution.py:427
  614.4 6.4 collective-permute-start.59
  709.2 48.5 %collective-permute-start.45 = (bf16[2048,384]{1,0:T(8,128)(2,1)S(1)}, bf16[2048,384]{1,0:T(8,128)(2,1)S(1)}, u32[]{:S(2)}, u32[]{:S(2)}) collective-permute-start(bf16[2048,384]{1,0:T(8,128)(2,1)S(1)} %slice.425), channel_id=1, source_target_pairs={{0,2},{2,0},{1,3},{3,1},{4,6},{6,4},{5,7},{7,5},{8,10},{10,8},{9,1... | collective-permute-start | bytes 4718600 | tf_op jit(solution)/shard_map/ppermute | solution.py:427
  713.3 18.7 %collective-permute-start.66 = (bf16[1024,384]{1,0:T(8,128)(2,1)S(1)}, bf16[1024,384]{1,0:T(8,128)(2,1)S(1)}, u32[]{:S(2)}, u32[]{:S(2)}) collective-permute-start(bf16[1024,384]{1,0:T(8,128)(2,1)S(1)} %slice.426), channel_id=1, source_target_pairs={{0,4},{4,0},{1,5},{5,1},{2,6},{6,2},{3,7},{7,3},{8,12},{12,8},{9,1... | collective-permute-start | bytes 2359304 | tf_op jit(solution)/shard_map/ppermute | solution.py:427
  716.4 36.2 %collective-permute-start.35 = (bf16[128,2048]{1,0:T(8,128)(2,1)S(1)}, bf16[128,2048]{1,0:T(8,128)(2,1)S(1)}, u32[]{:S(2)}, u32[]{:S(2)}) collective-permute-start(bf16[128,2048]{1,0:T(8,128)(2,1)S(1)} %get-tuple-element.120), channel_id=1, source_target_pairs={{24,16},{25,17},{26,18},{27,19},{28,20},{29,21},{30,22},{31,23}} | collective-permute-start | bytes 1572872 | tf_op jit(solution)/shard_map/ppermute | solution.py:1313
  732.4 6.7 collective-permute-start.67
  733.8 16.9 %collective-permute-start.68 = (bf16[1,256,384]{2,1,0:T(8,128)(2,1)S(1)}, bf16[1,256,384]{2,1,0:T(8,128)(2,1)S(1)}, u32[]{:S(2)}, u32[]{:S(2)}) collective-permute-start(bf16[1,256,384]{2,1,0:T(8,128)(2,1)S(1)} %get-tuple-element.143), channel_id=1, source_target_pairs={{0,16},{8,24},{16,0},{24,8},{1,17},{9,25},{17,1},{25,9},{2,18},{10... | collective-permute-start | bytes 589832 | tf_op jit(solution)/shard_map/ppermute | solution.py:1328
  739.1 13.4 %collective-permute-start.69 = (bf16[1,256,384]{2,1,0:T(8,128)(2,1)S(1)}, bf16[1,256,384]{2,1,0:T(8,128)(2,1)S(1)}, u32[]{:S(2)}, u32[]{:S(2)}) collective-permute-start(bf16[1,256,384]{2,1,0:T(8,128)(2,1)S(1)} %get-tuple-element.142), channel_id=1, source_target_pairs={{0,24},{8,0},{16,8},{24,16},{1,25},{9,1},{17,9},{25,17},{2,26},{10... | collective-permute-start | bytes 589832 | tf_op jit(solution)/shard_map/ppermute | solution.py:1328
  750.7 9.2 %collective-permute-start.38 = (bf16[128,2048]{1,0:T(8,128)(2,1)S(1)}, bf16[128,2048]{1,0:T(8,128)(2,1)S(1)}, u32[]{:S(2)}, u32[]{:S(2)}) collective-permute-start(bf16[128,2048]{1,0:T(8,128)(2,1)S(1)} %get-tuple-element.121), channel_id=1, source_target_pairs={{0,8},{1,9},{2,10},{3,11},{4,12},{5,13},{6,14},{7,15}} | collective-permute-start | bytes 1572872 | tf_op jit(solution)/shard_map/ppermute | solution.py:1316
  752.8 11.3 %collective-permute-start.36 = (bf16[128,2048]{1,0:T(8,128)(2,1)S(1)}, bf16[128,2048]{1,0:T(8,128)(2,1)S(1)}, u32[]{:S(2)}, u32[]{:S(2)}) collective-permute-start(bf16[128,2048]{1,0:T(8,128)(2,1)S(1)} %add_convert_fusion.3), channel_id=1, source_target_pairs={{16,8},{24,16},{17,9},{25,17},{18,10},{26,18},{19,11},{27,19},{20,... | collective-permute-start | bytes 1572872 | tf_op jit(solution)/shard_map/ppermute | solution.py:1313
  758.1 13.5 %collective-permute-start.46 = (bf16[1024,384]{1,0:T(8,128)(2,1)S(1)}, bf16[1024,384]{1,0:T(8,128)(2,1)S(1)}, u32[]{:S(2)}, u32[]{:S(2)}) collective-permute-start(bf16[1024,384]{1,0:T(8,128)(2,1)S(1)} %slice.427), channel_id=1, source_target_pairs={{0,4},{4,0},{1,5},{5,1},{2,6},{6,2},{3,7},{7,3},{8,12},{12,8},{9,1... | collective-permute-start | bytes 2359304 | tf_op jit(solution)/shard_map/ppermute | solution.py:427
  765.5 25.3 %collective-permute-start.39 = (bf16[128,2048]{1,0:T(8,128)(2,1)}, bf16[128,2048]{1,0:T(8,128)(2,1)S(1)}, u32[]{:S(2)}, u32[]{:S(2)}) collective-permute-start(bf16[128,2048]{1,0:T(8,128)(2,1)} %get-tuple-element.119), channel_id=1, source_target_pairs={{0,8},{8,16},{1,9},{9,17},{2,10},{10,18},{3,11},{11,19},{4,12},{12... | collective-permute-start | bytes 1572872 | tf_op jit(solution)/shard_map/ppermute | solution.py:1316
  766.1 34.1 %collective-permute-start.37 = (bf16[128,2048]{1,0:T(8,128)(2,1)}, bf16[128,2048]{1,0:T(8,128)(2,1)S(1)}, u32[]{:S(2)}, u32[]{:S(2)}) collective-permute-start(bf16[128,2048]{1,0:T(8,128)(2,1)} %get-tuple-element.118), channel_id=1, source_target_pairs={{8,0},{16,8},{24,16},{9,1},{17,9},{25,17},{10,2},{18,10},{26,18},{... | collective-permute-start | bytes 1572872 | tf_op jit(solution)/shard_map/ppermute | solution.py:1313
  772.7 12.8 %collective-permute-start.47 = (bf16[1,256,384]{2,1,0:T(8,128)(2,1)}, bf16[1,256,384]{2,1,0:T(8,128)(2,1)S(1)}, u32[]{:S(2)}, u32[]{:S(2)}) collective-permute-start(bf16[1,256,384]{2,1,0:T(8,128)(2,1)} %get-tuple-element.151), channel_id=1, source_target_pairs={{0,8},{8,16},{16,24},{24,0},{1,9},{9,17},{17,25},{25,1},{2,10},{10... | collective-permute-start | bytes 589832 | tf_op jit(solution)/shard_map/ppermute | solution.py:1328
  778.2 33.4 %collective-permute-start.61 = (bf16[1024,768]{1,0:T(8,128)(2,1)}, bf16[1024,768]{1,0:T(8,128)(2,1)}, u32[]{:S(2)}, u32[]{:S(2)}) collective-permute-start(bf16[1024,768]{1,0:T(8,128)(2,1)} %slice.424), channel_id=1, source_target_pairs={{0,2},{2,0},{1,3},{3,1},{4,6},{6,4},{5,7},{7,5},{8,10},{10,8},{9,1... | collective-permute-start | bytes 4718600 | tf_op jit(solution)/shard_map/ppermute | solution.py:427
  778.5 19.3 %collective-permute-start.48 = (bf16[1,256,384]{2,1,0:T(8,128)(2,1)S(1)}, bf16[1,256,384]{2,1,0:T(8,128)(2,1)S(1)}, u32[]{:S(2)}, u32[]{:S(2)}) collective-permute-start(bf16[1,256,384]{2,1,0:T(8,128)(2,1)S(1)} %copy-done.52), channel_id=1, source_target_pairs={{0,16},{8,24},{16,0},{24,8},{1,17},{9,25},{17,1},{25,9},{2,18},{10... | collective-permute-start | bytes 589832 | tf_op jit(solution)/shard_map/ppermute | solution.py:1328
  785.5 12.2 %collective-permute-start.49 = (bf16[1,256,384]{2,1,0:T(8,128)(2,1)S(1)}, bf16[1,256,384]{2,1,0:T(8,128)(2,1)S(1)}, u32[]{:S(2)}, u32[]{:S(2)}) collective-permute-start(bf16[1,256,384]{2,1,0:T(8,128)(2,1)S(1)} %copy-done.51), channel_id=1, source_target_pairs={{0,24},{8,0},{16,8},{24,16},{1,25},{9,1},{17,9},{25,17},{2,26},{10... | collective-permute-start | bytes 589832 | tf_op jit(solution)/shard_map/ppermute | solution.py:1328
  791.7 11.6 %collective-permute-start.40 = (bf16[128,2048]{1,0:T(8,128)(2,1)}, bf16[128,2048]{1,0:T(8,128)(2,1)}, u32[]{:S(2)}, u32[]{:S(2)}) collective-permute-start(bf16[128,2048]{1,0:T(8,128)(2,1)} %add_convert_fusion), channel_id=1, source_target_pairs={{0,8},{8,16},{16,24},{1,9},{9,17},{17,25},{2,10},{10,18},{18,26},{... | collective-permute-start | bytes 1572872 | tf_op jit(solution)/shard_map/ppermute | solution.py:1316
  807.1 7.7 collective-permute-start.41
  814.5 9.9 %collective-permute-start.62 = (bf16[1,256,768]{2,1,0:T(8,128)(2,1)S(1)}, bf16[1,256,768]{2,1,0:T(8,128)(2,1)S(1)}, u32[]{:S(2)}, u32[]{:S(2)}) collective-permute-start(bf16[1,256,768]{2,1,0:T(8,128)(2,1)S(1)} %get-tuple-element.128), channel_id=1, source_target_pairs={{0,8},{8,16},{16,24},{24,0},{1,9},{9,17},{17,25},{25,1},{2,10},{10... | collective-permute-start | bytes 1179656 | tf_op jit(solution)/shard_map/ppermute | solution.py:1328
  814.8 34.1 %collective-permute-start.63 = (bf16[1,256,768]{2,1,0:T(8,128)(2,1)S(1)}, bf16[1,256,768]{2,1,0:T(8,128)(2,1)S(1)}, u32[]{:S(2)}, u32[]{:S(2)}) collective-permute-start(bf16[1,256,768]{2,1,0:T(8,128)(2,1)S(1)} %get-tuple-element.127), channel_id=1, source_target_pairs={{0,16},{8,24},{16,0},{24,8},{1,17},{9,25},{17,1},{25,9},{2,18},{10... | collective-permute-start | bytes 1179656 | tf_op jit(solution)/shard_map/ppermute | solution.py:1328
  815.0 34.0 %collective-permute-start.64 = (bf16[1,256,768]{2,1,0:T(8,128)(2,1)S(1)}, bf16[1,256,768]{2,1,0:T(8,128)(2,1)S(1)}, u32[]{:S(2)}, u32[]{:S(2)}) collective-permute-start(bf16[1,256,768]{2,1,0:T(8,128)(2,1)S(1)} %get-tuple-element.126), channel_id=1, source_target_pairs={{0,24},{8,0},{16,8},{24,16},{1,25},{9,1},{17,9},{25,17},{2,26},{10... | collective-permute-start | bytes 1179656 | tf_op jit(solution)/shard_map/ppermute | solution.py:1328
  817.1 36.5 %collective-permute-start.42 = (bf16[256,2048]{1,0:T(8,128)(2,1)S(1)}, bf16[256,2048]{1,0:T(8,128)(2,1)S(1)}, u32[]{:S(2)}, u32[]{:S(2)}) collective-permute-start(bf16[256,2048]{1,0:T(8,128)(2,1)S(1)} %pad_maximum_fusion.1), channel_id=1, source_target_pairs={{0,2},{2,0},{1,3},{3,1},{4,6},{6,4},{5,7},{7,5},{8,10},{10,8},{9,1... | collective-permute-start | bytes 3145736 | tf_op jit(solution)/shard_map/ppermute | solution.py:427
  (74 other events, 1145.4 us)

commit v3 on v2

--- a/solution.py
+++ b/solution.py
@@ -461,8 +461,26 @@
     return (keys <= queries) & (keys >= begin_row)
 
 
+def doc_begins(lengths_ref, begin_ref):
+    places = lax.broadcasted_iota(jnp.int32, begin_ref.shape, 1)
+    begin = jnp.zeros(begin_ref.shape, jnp.int32)
+    total = jnp.int32(0)
+    for doc in range(lengths_ref.shape[0]):
+        total = total + lengths_ref[doc]
+        begin = begin + jnp.where(places >= total, lengths_ref[doc], 0)
+    begin_ref[...] = begin
+
+
+def begin_at(lengths_ref, place):
+    begin, total = jnp.int32(0), jnp.int32(0)
+    for doc in range(lengths_ref.shape[0]):
+        total = total + lengths_ref[doc]
+        begin = begin + jnp.where(place >= total, lengths_ref[doc], 0)
+    return begin
+
+
 def attend_kernel(
-    block, place_ref, first_ref, begin_ref, own_ref, other_ref, out_own, out_other, lse_ref, qs, ks, vs, vt, ot
+    block, place_ref, lengths_ref, own_ref, other_ref, out_own, out_other, lse_ref, begin_ref, qs, ks, vs, vt, ot
 ):
     floats, halves = jnp.float32, jnp.bfloat16
     length = qs.shape[0]
@@ -471,13 +489,14 @@
     place_rows(place_ref, own_ref, other_ref, ks, lambda ref, rows: ref[1, rows, :])
     place_rows(place_ref, own_ref, other_ref, vs, lambda ref, rows: ref[2, rows, :])
     vt[...] = vs[...].astype(floats).T.astype(halves)
+    doc_begins(lengths_ref, begin_ref)
     lanes_of = lax.broadcasted_iota(jnp.int32, (block, 2 * HD), 1)
 
     def one_query(index, carry):
         query_at = pl.multiple_of(index * block, block)
         query_both = qs[pl.ds(query_at, block), :]
         begin_row = begin_ref[:, pl.ds(query_at, block)]
-        start = first_ref[index]
+        start = lax.div(begin_at(lengths_ref, query_at), block)
         for head in range(2):
             query_head = jnp.where(head_rows(lanes_of, head), query_both, jnp.zeros_like(query_both))
 
@@ -529,12 +548,10 @@
 def attend_back_kernel(
     block,
     place_ref,
-    last_ref,
-    begin_ref,
+    lengths_ref,
     own_ref,
     other_ref,
-    att_own,
-    att_other,
+    att_ref,
     grad_own,
     grad_other,
     lse_ref,
@@ -544,6 +561,7 @@
     out_own,
     out_other,
     bias_ref,
+    begin_ref,
     qs,
     ks,
     kt,
@@ -562,7 +580,8 @@
     place_rows(place_ref, own_ref, other_ref, ks, lambda ref, rows: ref[1, rows, :])
     place_rows(place_ref, own_ref, other_ref, vs, lambda ref, rows: ref[2, rows, :])
     place_rows(place_ref, grad_own, grad_other, gs, lambda ref, rows: ref[rows, :])
-    place_rows(place_ref, att_own, att_other, at, lambda ref, rows: ref[rows, :])
+    place_rows(place_ref, att_ref.at[0], att_ref.at[1], at, lambda ref, rows: ref[rows, :])
+    doc_begins(lengths_ref, begin_ref)
     kt[...] = (ks[...] * scale).astype(floats).T.astype(halves)
     pairs = gs[...].astype(floats) * at[...].astype(floats)
     whole_lanes = lax.broadcasted_iota(jnp.int32, (8, 2 * HD), 1)
@@ -582,7 +601,11 @@
         key_at = pl.multiple_of(index * block, block)
         key_both = ks[pl.ds(key_at, block), :]
         value_both = vs[pl.ds(key_at, block), :]
-        finish = last_ref[index]
+        key_end = key_at + block
+        finish = jnp.int32(0)
+        for step in range(length // block):
+            begins = begin_at(lengths_ref, step * block)
+            finish = finish + jnp.where(begins < key_end, 1, 0)
 
         def one_query(step, running):
             grad_key, grad_value = running
@@ -912,7 +935,7 @@
 
 def pipeline(stages):
     for tick in range(CHUNKS + len(stages) - 1):
-        for depth in reversed(range(len(stages))):
+        for depth in range(len(stages)):
             part = tick - depth
             if 0 <= part < CHUNKS:
                 stages[depth](part)
@@ -927,32 +950,6 @@
 
 REDUCE_REFS = 11
 GATHER_REFS = 6
-
-
-def middle_kernel(
-    send_ref, keep_ref, base_ref, gain_ref, shift_ref, full_ref, residual_ref, acc_ref, *scratch
-):
-    at_z, at_c = lax.axis_index("z"), lax.axis_index("c")
-    greet(line_peers(at_z, at_c))
-    sent = Sent()
-    reduce = Reduce(sent, at_z, at_c, send_ref, keep_ref, acc_ref, scratch[:REDUCE_REFS])
-    gather = Gather(sent, at_z, at_c, full_ref, scratch[REDUCE_REFS:])
-
-    def settle(part):
-        rows = pl.ds(part * CHUNK, CHUNK)
-        reduce.stage(LINE, part)
-        residual = base_ref[rows, :] + acc_ref[...]
-        residual_ref[rows, :] = residual
-        normed = row_norm(residual)[0]
-        full_ref[rows, :] = (normed * gain_ref[...] + shift_ref[...]).astype(full_ref.dtype)
-        gather.stage(0, part)
-
-    pipeline(
-        [functools.partial(reduce.stage, step) for step in range(LINE)]
-        + [settle]
-        + [functools.partial(gather.stage, step) for step in range(1, LINE + 1)]
-    )
-    sent.finish()
 
 
 def middle_back_kernel(
@@ -988,8 +985,10 @@
         full_ref[rows, :] = turned.astype(full_ref.dtype)
         gather.stage(0, part)
 
+    for part in range(CHUNKS):
+        reduce.stage(0, part)
     pipeline(
-        [functools.partial(reduce.stage, step) for step in range(LINE)]
+        [functools.partial(reduce.stage, step) for step in range(1, LINE)]
         + [settle]
         + [functools.partial(gather.stage, step) for step in range(1, LINE + 1)]
     )
@@ -1062,8 +1061,10 @@
         spread_move("across", part, arriving=True).wait_recv()
         sent.start(spread_move("both", part))
 
+    for part in range(CHUNKS):
+        reduce.stage(0, part)
     pipeline(
-        [functools.partial(reduce.stage, step) for step in range(LINE)] + [settle, pass_on]
+        [functools.partial(reduce.stage, step) for step in range(1, LINE)] + [settle, pass_on]
     )
     for slot, where in enumerate(({"c": 1 - at_c}, {"y": 1 - at_y}, {"x": 1 - at_x})):
         move = remote(folds.at[slot], came.at[slot], fold_out.at[slot], fold_in.at[slot], where)
@@ -1097,133 +1098,379 @@
     sent.finish()
 
 
+UNITS = 7
+
+
+def pair_peers(at_z, at_x, at_y, at_c):
+    peers = [({"c": 1 - at_c}, None), ({"y": 1 - at_y}, None), ({"x": 1 - at_x}, None)]
+    return peers + [({"z": lax.rem(at_z + step, LINE)}, None) for step in range(1, LINE)]
+
+
+def spots():
+    return tuple(lax.axis_index(name) for name in ("z", "x", "y", "c"))
+
+
+def feature_lanes(at_x, rel_x, line, span):
+    return pl.ds(pl.multiple_of((2 * line + jnp.abs(at_x - rel_x)) * span, span), span)
+
+
 def open_kernel(
-    own_ref, part_ref, full_ref, near_ref, over_x_ref, over_y_ref, over_xy_ref, local_sem, *scratch
+    lengths_ref,
+    rows_ref,
+    grad_ref,
+    gains_ref,
+    qkv_ref,
+    out_ref,
+    gate_ref,
+    up_ref,
+    down_ref,
+    full_ref,
+    base_ref,
+    grads_ref,
+    turned_ref,
+    cos_ref,
+    high_ref,
+    low_ref,
+    all_qkv,
+    all_out,
+    all_gate_up,
+    all_down,
+    local_sem,
+    *scratch,
 ):
-    at_z, at_x, at_y, at_c = (lax.axis_index(name) for name in ("z", "x", "y", "c"))
-    peers = [({"c": 1 - at_c}, None), ({"y": 1 - at_y}, None), ({"x": 1 - at_x}, None)]
-    peers += [({"z": lax.rem(at_z + step, LINE)}, None) for step in range(1, LINE)]
-    greet(peers)
+    floats = jnp.float32
+    at_z, at_x, at_y, at_c = spots()
+    greet(pair_peers(at_z, at_x, at_y, at_c))
     sent = Sent()
     gather = Gather(sent, at_z, at_c, full_ref, scratch[:GATHER_REFS])
     trade_out, trade_in, flip_out, flip_in = scratch[GATHER_REFS:]
-    rows_of = part_ref.shape[1]
-
-    def trade_move(step, arriving=False):
-        origin = lax.rem(at_z + LINE - step, LINE) if arriving else at_z
-        rows = pl.ds(pl.multiple_of(origin * rows_of, rows_of), rows_of)
+    rows_of, head_part = out_ref.shape[0], out_ref.shape[1] // LINE
+    wide = gate_ref.shape[1] // LINE
+
+    def unit(index, quarter):
+        if index < 3:
+            lanes = pl.ds(pl.multiple_of(quarter * head_part, head_part), head_part)
+            return qkv_ref.at[index, :, lanes], all_qkv, index * head_part, head_part
+        if index == 3:
+            lanes = pl.ds(pl.multiple_of(quarter * head_part, head_part), head_part)
+            return out_ref.at[:, lanes], all_out, 0, head_part
+        lanes = pl.ds(pl.multiple_of(quarter * wide, wide), wide)
+        if index < 6:
+            source = (gate_ref, up_ref)[index - 4]
+            return source.at[:, lanes], all_gate_up, (index - 4) * wide, wide
+        return down_ref.at[:, lanes], all_down, 0, wide
+
+    groups = ((0, 1, 2), (3,), (4, 5), (6,))
+    arrays = (all_qkv, all_out, all_gate_up, all_down)
+
+    def block_rows(turn):
+        block = lax.rem(at_z + LINE - turn, LINE) * rows_of
+        return pl.ds(pl.multiple_of(block, rows_of), rows_of)
+
+    def trade_move(index, step, arriving=False):
+        source, goal, base, size = unit(index, lax.rem(at_z + step, LINE))
+        rows = block_rows(step if arriving else 0)
         return remote(
-            part_ref.at[lax.rem(at_z + step, LINE)],
-            near_ref.at[rows, :],
-            trade_out.at[step - 1],
-            trade_in.at[step - 1],
+            source,
+            goal.at[0, 0, rows, base : base + size],
+            trade_out.at[index, step - 1],
+            trade_in.at[index, step - 1],
             {"z": lax.rem(at_z + step, LINE)},
         )
 
-    def flip_move(kind, source, goal, turn, where):
-        block = lax.rem(at_z + LINE - turn, LINE) * rows_of
-        rows = pl.ds(pl.multiple_of(block, rows_of), rows_of)
+    def local_move(index):
+        source, goal, base, size = unit(index, at_z)
+        return pltpu.make_async_copy(
+            source, goal.at[0, 0, block_rows(0), base : base + size], local_sem.at[index]
+        )
+
+    def flip_move(which, kind, turn):
+        rows = block_rows(turn)
+        array = arrays[which]
+        source, goal, where = (
+            ((0, 0), (1, 0), {"x": 1 - at_x}),
+            ((0, 0), (0, 1), {"y": 1 - at_y}),
+            ((1, 0), (1, 1), {"y": 1 - at_y})
+            if turn % 2 == 0
+            else ((0, 1), (1, 1), {"x": 1 - at_x}),
+        )[kind]
         return remote(
-            source.at[rows, :],
-            goal.at[rows, :],
-            flip_out.at[kind, turn],
-            flip_in.at[kind, turn],
+            array.at[source[0], source[1], rows, :],
+            array.at[goal[0], goal[1], rows, :],
+            flip_out.at[which * 3 + kind, turn],
+            flip_in.at[which * 3 + kind, turn],
             where,
         )
 
-    def to_x(turn):
-        return flip_move(0, near_ref, over_x_ref, turn, {"x": 1 - at_x})
-
-    def to_y(turn):
-        return flip_move(1, near_ref, over_y_ref, turn, {"y": 1 - at_y})
-
-    def to_xy(turn):
-        if turn % 2 == 0:
-            return flip_move(2, over_x_ref, over_xy_ref, turn, {"y": 1 - at_y})
-        return flip_move(2, over_y_ref, over_xy_ref, turn, {"x": 1 - at_x})
-
-    for step in (2, 1, 3):
-        sent.start(trade_move(step))
-    mine = pltpu.make_async_copy(
-        part_ref.at[at_z],
-        near_ref.at[pl.ds(pl.multiple_of(at_z * rows_of, rows_of), rows_of), :],
-        local_sem.at[0],
-    )
-    mine.start()
-    rows_copy = pltpu.make_async_copy(
-        own_ref, full_ref.at[pl.ds(0, QUARTER), :], local_sem.at[1]
-    )
-    rows_copy.start()
-    mine.wait()
-    sent.start(to_x(0))
-    sent.start(to_y(0))
-    rows_copy.wait()
+    def start_trades(which):
+        for step in (2, 1, 3):
+            for index in groups[which]:
+                sent.start(trade_move(index, step))
+
+    def pass_first(which, turn):
+        for index in groups[which]:
+            if turn == 0:
+                local_move(index).wait()
+            else:
+                trade_move(index, turn, arriving=True).wait_recv()
+        sent.start(flip_move(which, 0, turn))
+        sent.start(flip_move(which, 1, turn))
+
+    def pass_second(which, turn):
+        flip_move(which, 0 if turn % 2 == 0 else 1, turn).wait_recv()
+        sent.start(flip_move(which, 2, turn))
+
+    def pass_last(which, turn):
+        flip_move(which, 1 if turn % 2 == 0 else 0, turn).wait_recv()
+        flip_move(which, 2, turn).wait_recv()
+
+    for index in range(UNITS):
+        local_move(index).start()
+    start_trades(0)
+    start_trades(1)
+    for which in range(4):
+        pass_first(which, 0)
+
+    own = pl.ds(pl.multiple_of(at_c * QUARTER, QUARTER), QUARTER)
+    half = base_ref.shape[1] // 2
+    span = half // LINE
+    for rel_x in range(2):
+        for line in range(LINE):
+            lanes = feature_lanes(at_x, rel_x, line, span)
+            goal = slice(rel_x * half + line * span, rel_x * half + (line + 1) * span)
+            base_ref[:, goal] = rows_ref[at_y, own, lanes].astype(floats)
+            grads_ref[:, goal] = grad_ref[at_y, own, lanes]
+            turned_ref[:, goal] = gains_ref[:, lanes]
     for part in range(CHUNKS):
+        rows = pl.ds(part * CHUNK, CHUNK)
+        normed = row_norm(base_ref[rows, :])[0]
+        full_ref[rows, :] = (normed * turned_ref[0:1, :] + turned_ref[1:2, :]).astype(full_ref.dtype)
         gather.stage(0, part)
+    start_trades(2)
+
+    length = cos_ref.shape[0]
+    places = lax.broadcasted_iota(jnp.int32, (8, length), 1)
+    begin = jnp.zeros((8, length), jnp.int32)
+    total = jnp.int32(0)
+    for doc in range(lengths_ref.shape[1]):
+        size = lengths_ref[at_y, doc]
+        total = total + size
+        begin = begin + jnp.where(places >= total, size, 0)
+    halfway = ROT // 2
+    exponent = lax.broadcasted_iota(jnp.int32, (8, length), 0).astype(floats) * (2.0 / ROT)
+    angles = (places - begin).astype(floats) * jnp.exp(-math.log(10000.0) * exponent)
+    lane = lax.broadcasted_iota(jnp.int32, (8, 2 * HD), 1) % HD
+    kind = lax.broadcasted_iota(jnp.int32, (8, 2 * HD), 0)
+    low = jnp.where(lane == kind, 1.0, 0.0)
+    high = jnp.where(lane == kind + halfway, 1.0, 0.0)
+    still = jnp.where(lane[0:1] < ROT, 0.0, 1.0)
+
+    def expand(table, choice):
+        return lax.dot_general(
+            table,
+            choice,
+            (((0,), (0,)), ((), ())),
+            precision=lax.Precision.HIGHEST,
+            preferred_element_type=floats,
+        )
+
+    cosine, sine = jnp.cos(angles), jnp.sin(angles)
+    cos_ref[...] = expand(cosine, low + high) + still
+    high_ref[...] = expand(sine, high)
+    low_ref[...] = expand(sine, -low)
+
     for turn in range(1, LINE):
-        trade_move(turn, arriving=True).wait_recv()
-        sent.start(to_x(turn))
-        sent.start(to_y(turn))
-    for step in range(1, LINE):
-        for part in range(CHUNKS):
-            gather.stage(step, part)
-        if step == 1:
-            for turn in range(LINE):
-                if turn % 2 == 0:
-                    to_x(turn).wait_recv()
-                else:
-                    to_y(turn).wait_recv()
-                sent.start(to_xy(turn))
+        pass_first(0, turn)
+    for part in range(CHUNKS):
+        gather.stage(1, part)
+    start_trades(3)
+    for which in range(4):
+        pass_second(which, 0)
+    for turn in range(1, LINE):
+        pass_first(1, turn)
+    for turn in range(1, LINE):
+        pass_second(0, turn)
+    for part in range(CHUNKS):
+        gather.stage(2, part)
+    for turn in range(1, LINE):
+        pass_first(2, turn)
+        pass_second(1, turn)
+    for part in range(CHUNKS):
+        gather.stage(3, part)
+    for turn in range(1, LINE):
+        pass_first(3, turn)
+        pass_second(2, turn)
+    for turn in range(1, LINE):
+        pass_second(3, turn)
     for part in range(CHUNKS):
         gather.stage(LINE, part)
-    for turn in range(LINE):
-        if turn % 2 == 0:
-            to_y(turn).wait_recv()
-        else:
-            to_x(turn).wait_recv()
-        to_xy(turn).wait_recv()
+    for which in range(4):
+        for turn in range(LINE):
+            pass_last(which, turn)
     sent.finish()
 
 
-def qkv_kernel(
-    rows_ref, near_ref, over_x_ref, over_y_ref, over_xy_ref, bias_ref, cos_ref, up_ref, down_ref, out_ref
+def project_kernel(
+    rows_ref,
+    weight_ref,
+    bias_ref,
+    cos_ref,
+    high_ref,
+    low_ref,
+    own_ref,
+    other_ref,
+    going_ref,
+    out_sem,
+    in_sem,
 ):
     floats = jnp.float32
+    at_z, at_x, at_y, at_c = spots()
+    greet([({"x": 1 - at_x}, None)])
+    sent = Sent()
     width = 2 * HD
-    half = near_ref.shape[0]
-    for part, (first, second) in enumerate(((near_ref, over_x_ref), (over_y_ref, over_xy_ref))):
-        product = jnp.dot(rows_ref[:, :half], first[...], preferred_element_type=floats)
-        product = product + jnp.dot(rows_ref[:, half:], second[...], preferred_element_type=floats)
-        for kind in range(3):
-            content = product[:, kind * width : (kind + 1) * width]
-            content = content + bias_ref[part * 3 + kind : part * 3 + kind + 1, :]
-            if kind < 2:
-                content = (
-                    content * cos_ref[...]
-                    + pltpu.roll(content, 8, 1) * up_ref[...]
-                    + pltpu.roll(content, width - 8, 1) * down_ref[...]
-                )
-            out_ref[part, kind] = content.astype(out_ref.dtype)
+    half = weight_ref.shape[2]
+    crossed = at_x ^ at_y
+    group = 2 * QUARTER
+
+    def compute(part, goal, index):
+        rows = pl.ds(index * group, group)
+        product = jnp.dot(rows_ref[rows, :half], weight_ref[0, part], preferred_element_type=floats)
+        product = product + jnp.dot(
+            rows_ref[rows, half:], weight_ref[1, part], preferred_element_type=floats
+        )
+        for block in range(2):
+            rel = index * 2 + block
+            rel_c, rel_z = rel // LINE, rel % LINE
+            place = (
+                lax.rem(at_z + rel_z, LINE) * (4 * QUARTER)
+                + at_x * (2 * QUARTER)
+                + jnp.abs(at_c - rel_c) * QUARTER
+            )
+            table = pl.ds(pl.multiple_of(place, QUARTER), QUARTER)
+            lines = slice(block * QUARTER, (block + 1) * QUARTER)
+            for kind in range(3):
+                content = product[lines, kind * width : (kind + 1) * width]
+                content = content + bias_ref[part * 3 + kind]
+                if kind < 2:
+                    content = (
+                        content * cos_ref[table, :]
+                        + pltpu.roll(content, 8, 1) * high_ref[table, :]
+                        + pltpu.roll(content, width - 8, 1) * low_ref[table, :]
+                    )
+                goal[kind, pl.ds(rel * QUARTER, QUARTER), :] = content.astype(goal.dtype)
+
+    def move(index):
+        rows = pl.ds(index * group, group)
+        return remote(
+            going_ref.at[:, rows, :],
+            other_ref.at[:, rows, :],
+            out_sem.at[index],
+            in_sem.at[index],
+            {"x": 1 - at_x},
+        )
+
+    count = rows_ref.shape[0] // group
+    for index in range(count):
+        compute(1 - crossed, going_ref, index)
+        sent.start(move(index))
+    for index in range(count):
+        compute(crossed, own_ref, index)
+    for index in range(count):
+        move(index).wait_recv()
+    sent.finish()
+
+
+def middle_kernel(
+    own_ref,
+    going_ref,
+    weight_ref,
+    base_ref,
+    gains_ref,
+    full_ref,
+    residual_ref,
+    both_ref,
+    send_ref,
+    keep_ref,
+    acc_ref,
+    flip_out,
+    flip_in,
+    *scratch,
+):
+    floats = jnp.float32
+    at_z, at_x, at_y, at_c = spots()
+    greet(line_peers(at_z, at_c) + [({"x": 1 - at_x}, None)])
+    sent = Sent()
+    reduce = Reduce(sent, at_z, at_c, send_ref, keep_ref, acc_ref, scratch[:REDUCE_REFS])
+    gather = Gather(sent, at_z, at_c, full_ref, scratch[REDUCE_REFS:])
+    crossed = at_x ^ at_y
+    width = own_ref.shape[1]
+    half = weight_ref.shape[2]
+    rows_of = own_ref.shape[0] // 2
+
+    def flip_move(side):
+        rows = pl.ds(side * rows_of, rows_of)
+        return remote(
+            going_ref.at[rows, :],
+            both_ref.at[1, rows, :],
+            flip_out.at[side],
+            flip_in.at[side],
+            {"x": 1 - at_x},
+        )
+
+    sent.start(flip_move(1))
+    sent.start(flip_move(0))
+    both_ref[0] = own_ref[...]
+    for side, goal in ((1, send_ref), (0, keep_ref)):
+        flip_move(side).wait_recv()
+        rows = slice(side * rows_of, (side + 1) * rows_of)
+        for rel_x in range(2):
+            product = lax.dot_general(
+                both_ref[0, rows, :],
+                weight_ref[rel_x, crossed],
+                (((1,), (1,)), ((), ())),
+                preferred_element_type=floats,
+            )
+            product = product + lax.dot_general(
+                both_ref[1, rows, :],
+                weight_ref[rel_x, 1 - crossed],
+                (((1,), (1,)), ((), ())),
+                preferred_element_type=floats,
+            )
+            goal[:, rel_x * half : (rel_x + 1) * half] = product.astype(goal.dtype)
+        if side == 1:
+            for part in range(CHUNKS):
+                reduce.stage(0, part)
+
+    def settle(part):
+        rows = pl.ds(part * CHUNK, CHUNK)
+        reduce.stage(LINE, part)
+        residual = base_ref[rows, :] + acc_ref[...]
+        residual_ref[rows, :] = residual
+        normed = row_norm(residual)[0]
+        full_ref[rows, :] = (normed * gains_ref[2:3, :] + gains_ref[3:4, :]).astype(full_ref.dtype)
+        gather.stage(0, part)
+
+    pipeline(
+        [functools.partial(reduce.stage, step) for step in range(1, LINE)]
+        + [settle]
+        + [functools.partial(gather.stage, step) for step in range(1, LINE + 1)]
+    )
+    sent.finish()
 
 
 def feed_kernel(
     low_ref,
     grad_ref,
-    up_near,
-    up_x,
-    up_y,
-    up_xy,
-    down_near,
-    down_x,
-    down_y,
-    down_xy,
+    up_weight,
+    down_weight,
     hidden_ref,
     turned_ref,
 ):
     floats = jnp.float32
-    half, wide = down_near.shape
-    pieces = ((up_near, up_x, down_near, down_x), (up_y, up_xy, down_y, down_xy))
-    for part, (gate_a, gate_b, back_a, back_b) in enumerate(pieces):
+    half, wide = down_weight.shape[2:]
+    for part in range(2):
+        gate_a, gate_b = up_weight.at[0, part], up_weight.at[1, part]
+        back_a, back_b = down_weight.at[0, part], down_weight.at[1, part]
         gate_up = jnp.dot(low_ref[:, :half], gate_a[...], preferred_element_type=floats)
         gate_up = gate_up + jnp.dot(low_ref[:, half:], gate_b[...], preferred_element_type=floats)
         grad_hidden = jnp.dot(grad_ref[:, :half], back_a[...], preferred_element_type=floats)
@@ -1240,11 +1487,12 @@
         turned_ref[:, base + wide : base + 2 * wide] = (grad_hidden * silu).astype(turned_ref.dtype)
 
 
-def spread_kernel(left_ref, near_ref, over_x_ref, over_y_ref, over_xy_ref, send_ref, keep_ref):
+def spread_kernel(left_ref, weight_ref, send_ref, keep_ref):
     floats = jnp.float32
-    half, width = near_ref.shape
+    half, width = weight_ref.shape[2:]
     rows = left_ref.shape[0] // 2
-    for base, (first, second) in ((0, (near_ref, over_y_ref)), (half, (over_x_ref, over_xy_ref))):
+    for rel_x in range(2):
+        base, first, second = rel_x * half, weight_ref.at[rel_x, 0], weight_ref.at[rel_x, 1]
         for goal, lines in ((send_ref, slice(rows, 2 * rows)), (keep_ref, slice(0, rows))):
             product = lax.dot_general(
                 left_ref[lines, :width], first[...], (((1,), (1,)), ((), ())), preferred_element_type=floats
@@ -1259,13 +1507,13 @@
     return [pl.BlockSpec(memory_space=pltpu.VMEM)] * count
 
 
-def remote_call(kernel, number, shapes, scratch, name):
+def remote_call(kernel, number, shapes, scratch, name, in_specs=None, out_specs=None):
     def call(*operands):
         return pl.pallas_call(
             kernel,
             out_shape=shapes,
-            in_specs=whole_specs(len(operands)),
-            out_specs=tuple(whole_specs(len(shapes))),
+            in_specs=in_specs or whole_specs(len(operands)),
+            out_specs=tuple(out_specs or whole_specs(len(shapes))),
             scratch_shapes=scratch,
             compiler_params=pltpu.CompilerParams(collective_id=number, has_side_effects=True),
             name=name,
@@ -1415,114 +1663,125 @@
             [jnp.where(at_y == 0, pair, across), jnp.where(at_y == 0, across, pair)], axis=0
         )
 
-    def quarters(matrix, size):
-        grown = jnp.pad(matrix, ((0, 0), (0, LINE * size - matrix.shape[1])))
-        return jnp.swapaxes(grown.reshape(matrix.shape[0], LINE, size), 0, 1)
-
-    part_qkv = jnp.concatenate([quarters(w_qkv[:, kind], cut) for kind in range(3)], axis=2)
-    part_out = quarters(w_out, cut)
-    part_gate_up = jnp.concatenate([quarters(w_gate_up[:, kind], wide) for kind in range(2)], axis=2)
-    part_down = quarters(w_down, wide)
-
     lengths = lax.dynamic_index_in_dim(doc_lengths, at_y, 0, keepdims=False)
-    doc_ends = jnp.cumsum(lengths)
-
-    def begin_of(places):
-        passed = (places[:, None] >= doc_ends[None, :]).astype(jnp.int32)
-        return jnp.sum(passed * lengths[None, :], axis=-1)
-
     length = 2 * tokens
     block = 256
-    all_places = jnp.arange(length, dtype=jnp.int32)
-    begin_all = begin_of(all_places)
-    block_begin = begin_all.reshape(length // block, block)[:, 0]
-    first_block = block_begin // block
-    block_ends = (jnp.arange(length // block, dtype=jnp.int32) + 1) * block
-    last_block = jnp.sum((block_begin[None, :] < block_ends[:, None]).astype(jnp.int32), axis=1)
-    rel = jnp.arange(tokens, dtype=jnp.int32)
-    rel_c, rel_z, rel_r = rel // (LINE * QUARTER), (rel // QUARTER) % LINE, rel % QUARTER
-    places = (
-        ((at_z + rel_z) % LINE) * (2 * shard_len)
-        + at_x * shard_len
-        + jnp.abs(at_c - rel_c) * QUARTER
-        + rel_r
-    )
-    row_tables = lane_tables(places - begin_of(places))
-    all_tables = lane_tables(all_places - begin_all)
     place = jnp.stack([at_z, at_x, at_c]).astype(jnp.int32)
 
-    input_wide = own_rows(block_input).astype(floats)
-    gain1, shift1, gain2, shift2 = (features(v) for v in (ln1_gain, ln1_bias, ln2_gain, ln2_bias))
-    first_norm = layer_norm(input_wide, gain1, shift1)[0]
+    def grown(matrix):
+        return jnp.pad(matrix, ((0, 0), (0, LINE * wide - hidden_cols)))
+
+    smem = pl.BlockSpec(memory_space=pltpu.SMEM)
+    vmem = pl.BlockSpec(memory_space=pltpu.VMEM)
+    kept = pl.BlockSpec(memory_space=pl.ANY)
     half_rows = model_width // 2
-    piece = jax.ShapeDtypeStruct((half_rows, 3 * cut), halves)
     full_shape = jax.ShapeDtypeStruct((tokens, model_width), halves)
+    own_shape = jax.ShapeDtypeStruct((QUARTER, model_width), floats)
+    table_shape = jax.ShapeDtypeStruct((length, cut), floats)
     dma = pltpu.SemaphoreType.DMA
-    first_low, *pieces_qkv = remote_call(
+
+    def pieces(width):
+        return jax.ShapeDtypeStruct((2, 2, half_rows, width), halves)
+
+    (
+        first_low,
+        input_wide,
+        grad_own,
+        gains,
+        table_cos,
+        table_high,
+        table_low,
+        full_qkv,
+        full_out,
+        full_gate_up,
+        full_down,
+    ) = remote_call(
         open_kernel,
         1,
-        (full_shape, piece, piece, piece, piece),
-        [dma((2,))] + gather_scratch() + [dma((LINE - 1,))] * 2 + [dma((3, LINE))] * 2,
+        (
+            full_shape,
+            own_shape,
+            jax.ShapeDtypeStruct((QUARTER, model_width), halves),
+            jax.ShapeDtypeStruct((4, model_width), floats),
+            table_shape,
+            table_shape,
+            table_shape,
+            pieces(3 * cut),
+            pieces(cut),
+            pieces(2 * wide),
+            pieces(wide),
+        ),
+        [dma((UNITS,))] + gather_scratch() + [dma((UNITS, LINE - 1))] * 2 + [dma((12, LINE))] * 2,
         "open",
-    )(first_norm.astype(halves), part_qkv)
-    pieces_out = widen(part_out, at_z)
-    pieces_gate_up = widen(part_gate_up, at_z)
-    pieces_down = widen(part_down, at_z)
-    grad_rows = line_gather(own_rows(grad_y), at_z)
-
+        in_specs=[smem] + [vmem] * 8,
+        out_specs=[vmem] * 7 + [kept] * 4,
+    )(
+        doc_lengths,
+        block_input,
+        grad_y,
+        jnp.stack([ln1_gain, ln1_bias, ln2_gain, ln2_bias]),
+        jnp.swapaxes(w_qkv, 0, 1),
+        w_out,
+        grown(w_gate_up[:, 0]),
+        grown(w_gate_up[:, 1]),
+        grown(w_down),
+    )
+    crossed = at_x ^ at_y
     own_bias = lax.dynamic_slice_in_dim(qkv_bias, at_z * cut, cut, 1)
-    bias_parts = jnp.concatenate([own_bias, flip(own_bias, "y")], axis=0)
-    projected = pl.pallas_call(
-        qkv_kernel,
-        out_shape=jax.ShapeDtypeStruct((2, 3, tokens, cut), halves),
-        in_specs=whole_specs(9),
-        out_specs=pl.BlockSpec(memory_space=pltpu.VMEM),
-        name="project",
-    )(first_low, *pieces_qkv, bias_parts, *row_tables)
-    crossed = at_x ^ at_y
-    qkv_own = lax.dynamic_index_in_dim(projected, crossed, 0, keepdims=False)
-    qkv_other = flip(lax.dynamic_index_in_dim(projected, 1 - crossed, 0, keepdims=False), "x")
-
-    smem = pl.BlockSpec(memory_space=pltpu.SMEM)
+    bias_parts = jnp.concatenate([own_bias, flip(own_bias, "y")], axis=0)[:, None, :]
+    qkv_shape = jax.ShapeDtypeStruct((3, tokens, cut), halves)
+    qkv_own, qkv_other = remote_call(
+        project_kernel,
+        5,
+        (qkv_shape, qkv_shape),
+        [pltpu.VMEM((3, tokens, cut), halves), dma((LINE,)), dma((LINE,))],
+        "project",
+    )(first_low, full_qkv, bias_parts, table_cos, table_high, table_low)
+
+    grad_lines = [grad_own]
+    for step in range(1, LINE):
+        grad_lines.append(
+            lax.ppermute(grad_own, "z", [(k, (k + LINE - step) % LINE) for k in range(LINE)])
+        )
+    grad_lines = jnp.concatenate(grad_lines, axis=0)
+    grad_rows = jnp.concatenate([grad_lines, flip(grad_lines, "c")], axis=0)
+
     half_shape = jax.ShapeDtypeStruct((tokens, cut), halves)
     out_own, out_other, lse = pl.pallas_call(
         functools.partial(attend_kernel, block),
         out_shape=(half_shape, half_shape, jax.ShapeDtypeStruct((2, length), floats)),
-        in_specs=[smem, smem] + whole_specs(3),
+        in_specs=[smem, smem] + whole_specs(2),
         out_specs=tuple(whole_specs(3)),
-        scratch_shapes=[pltpu.VMEM((length, cut), halves)] * 3
+        scratch_shapes=[pltpu.VMEM((1, length), jnp.int32)]
+        + [pltpu.VMEM((length, cut), halves)] * 3
         + [pltpu.VMEM((cut, length), halves), pltpu.VMEM((cut, length), floats)],
         name="attend",
-    )(place, first_block, begin_all[None, :], qkv_own, qkv_other)
-
-    def join_heads(own, other):
-        near = jnp.where(crossed == 0, own, other)
-        far = jnp.where(crossed == 0, other, own)
-        return jnp.concatenate([near, far], axis=-1)
-
-    attended = join_heads(out_own, flip(out_other, "x"))
+    )(place, lengths, qkv_own, qkv_other)
+
     half = tokens // 2
     send_shape = jax.ShapeDtypeStruct((half, model_width), halves)
     keep_shape = jax.ShapeDtypeStruct((half, model_width), floats)
-    own_shape = jax.ShapeDtypeStruct((QUARTER, model_width), floats)
     acc = pltpu.VMEM((CHUNK, model_width), floats)
 
     def spread(left, pieces):
         return pl.pallas_call(
             spread_kernel,
             out_shape=(send_shape, keep_shape),
-            in_specs=whole_specs(5),
+            in_specs=whole_specs(2),
             out_specs=tuple(whole_specs(2)),
             name="spread",
-        )(left, *pieces)
-
-    second_low, residual = remote_call(
+        )(left, pieces)
+
+    second_low, residual, attended = remote_call(
         middle_kernel,
         2,
-        (full_shape, own_shape),
-        [acc] + reduce_scratch(model_width) + gather_scratch(),
+        (full_shape, own_shape, jax.ShapeDtypeStruct((2, tokens, cut), halves)),
+        [pltpu.VMEM((half, model_width), halves), pltpu.VMEM((half, model_width), floats), acc]
+        + [dma((2,))] * 2
+        + reduce_scratch(model_width)
+        + gather_scratch(),
         "middle",
-    )(*spread(attended, pieces_out), input_wide, gain2[None, :], shift2[None, :])
+    )(out_own, out_other, full_out, input_wide, gains)
     step_rows = tokens // 2
     hidden, grad_gate_up = pl.pallas_call(
         feed_kernel,
@@ -1531,24 +1790,24 @@
             jax.ShapeDtypeStruct((tokens, 4 * wide), halves),
         ),
         grid=(tokens // step_rows,),
-        in_specs=[pl.BlockSpec((step_rows, model_width), lambda row: (row, 0))] * 2 + whole_specs(8),
+        in_specs=[pl.BlockSpec((step_rows, model_width), lambda row: (row, 0))] * 2 + whole_specs(2),
         out_specs=(
             pl.BlockSpec((step_rows, 2 * wide), lambda row: (row, 0)),
             pl.BlockSpec((step_rows, 4 * wide), lambda row: (row, 0)),
         ),
         name="feed",
-    )(second_low, grad_rows, *pieces_gate_up, *pieces_down)
+    )(second_low, grad_rows, full_gate_up, full_down)
     residual_low, grad_residual, sums2 = remote_call(
         middle_back_kernel,
         3,
         (full_shape, own_shape, jax.ShapeDtypeStruct((8, model_width), floats)),
         [acc] + reduce_scratch(model_width) + gather_scratch(),
         "middle_back",
-    )(*spread(grad_gate_up, pieces_gate_up), residual, own_rows(grad_y), gain2[None, :])
+    )(*spread(grad_gate_up, full_gate_up), residual, grad_own, gains[2:3])
     (second_low, grad_rows, hidden, grad_gate_up, out_left) = lax.optimization_barrier(
         (second_low, grad_rows, hidden, grad_gate_up, hidden, residual_low)
     )[:5]
-    out_send, out_keep = spread(out_left, pieces_down)
+    out_send, out_keep = spread(out_left, full_down)
     block_output = spread_output(residual + line_reduce(out_keep, out_send))
 
     def product(left_rows, right_rows):
@@ -1556,24 +1815,23 @@
             left_rows, right_rows, (((0,), (0,)), ((), ())), preferred_element_type=floats
         )
 
-    out_near, out_x, out_y, out_xy = pieces_out
-    full_out = jnp.concatenate(
-        [jnp.concatenate([out_near, out_y], axis=1), jnp.concatenate([out_x, out_xy], axis=1)], axis=0
+    joined_out = jnp.concatenate(
+        [jnp.concatenate([full_out[k, 0], full_out[k, 1]], axis=1) for k in range(2)], axis=0
     )
-    grad_attended = jnp.dot(residual_low, full_out, preferred_element_type=floats).astype(halves)
+    grad_attended = jnp.dot(residual_low, joined_out, preferred_element_type=floats).astype(halves)
     g_gate_up = narrow(product(second_low, grad_gate_up), at_z, "x")
     g_down = narrow(product(grad_rows, hidden), at_z, "y")
     grad_near, grad_far = grad_attended[:, :cut], grad_attended[:, cut:]
     grad_mine = jnp.where(crossed == 0, grad_near, grad_far)
     grad_their = flip(jnp.where(crossed == 0, grad_far, grad_near), "x")
 
-    qkv_shape = jax.ShapeDtypeStruct((3, tokens, cut), halves)
     back_own, back_other, bias_sums = pl.pallas_call(
         functools.partial(attend_back_kernel, block),
         out_shape=(qkv_shape, qkv_shape, jax.ShapeDtypeStruct((3, cut), floats)),
-        in_specs=[smem, smem] + whole_specs(11),
+        in_specs=[smem, smem] + whole_specs(9),
         out_specs=tuple(whole_specs(3)),
         scratch_shapes=[
+            pltpu.VMEM((1, length), jnp.int32),
             pltpu.VMEM((length, cut), halves),
             pltpu.VMEM((length, cut), halves),
             pltpu.VMEM((cut, length), halves),
@@ -1588,16 +1846,16 @@
         name="attend_back",
     )(
         place,
-        last_block,
-        begin_all[None, :],
+        lengths,
         qkv_own,
         qkv_other,
-        out_own,
-        out_other,
+        jnp.stack([out_own, out_other]),
         grad_mine,
         grad_their,
         lse,
-        *all_tables,
+        table_cos,
+        table_high,
+        table_low,
     )
     came_back = flip(back_other, "x")
     near = jnp.where(crossed == 0, back_own, came_back)
@@ -1623,10 +1881,12 @@
             dma((LINE - 1,)),
         ],
         "last",
-    )(*spread(grad_qkv, pieces_qkv), input_wide, grad_residual, gain1[None, :], early)
+    )(*spread(grad_qkv, full_qkv), input_wide, grad_residual, gains[0:1], early)
     sums = plain_features(sums[:4])
     g_qkv = narrow(product(first_low, grad_qkv), at_z, "y")
-    g_out = narrow(product(residual_low, attended), at_z, "y")
+    near = jnp.where(crossed == 0, attended[0], attended[1])
+    far = jnp.where(crossed == 0, attended[1], attended[0])
+    g_out = narrow(product(residual_low, jnp.concatenate([near, far], axis=1)), at_z, "y")
     bias_sums = bias_sums + flip(bias_sums, "y")
     bias_sums = jnp.where(crossed == 0, bias_sums, flip(bias_sums, "x"))
     bias_all = jnp.zeros((LINE, 3, cut), floats)

time: 863 us -> 883 us (1.023)
  waiting for transfers between devices: 205 us -> 60.7 us
  Pallas kernels: 380 us -> 497 us
  local copies, waits for them, and re-layouts: 76.8 us -> 154 us
  starting transfers between devices: 117 us -> 94.7 us
  other arithmetic: 52.3 us -> 36.3 us
    pallas_call x5, Pallas kernels: 278 us -> 401 us  [call(): pl.pallas_call(kernel, out_shape=shapes, in_specs=in_specs or whole_specs...]
    ppermute x34 -> x17, waiting for transfers between devices: 128 us -> 15.4 us  [flip(): return lax.ppermute(block, axis, FLIP)]
    dynamic_update_slice x21 -> x12, local copies, waits for them, and re-layouts: 7.94 us -> 70.4 us  [line_trade(): lax.dynamic_update_slice_in_dim(held, came, lax.rem(at_z + LINE - step, L...]
    ppermute x21 -> x12, waiting for transfers between devices: 68.2 us -> 13.1 us  [line_trade(): lax.ppermute(going, 'z', [(k, (k + step) % LINE) for k in range(LINE)])]
    ppermute x6 -> x3, waiting for transfers between devices: 0.02 us -> 25.2 us  [block_device(): lax.ppermute(grad_own, 'z', [(k, (k + LINE - step) % LINE) for k in range...]
    dynamic_update_slice x2 -> x4, local copies, waits for them, and re-layouts: 0.06 us -> 23.5 us  [line_trade(): held = lax.dynamic_update_slice_in_dim(held, mine, at_z, 0)]
    ppermute x34 -> x17, starting transfers between devices: 37.8 us -> 20.3 us  [flip(): return lax.ppermute(block, axis, FLIP)]
    unnamed x162 -> x100, local copies, waits for them, and re-layouts: 29.6 us -> 16.2 us
  transfers between devices with their start and end apart: 70 -> 41, of which waited for: 25 -> 9; matrix products, arithmetic and copies ran while one was open for 16% -> 22% of each run, Pallas kernels for 31% -> 28%
where the time goes in v3:
time: 883 us; the launch traced here: 872 us
  Pallas kernels  497 us (56%)
  local copies, waits for them, and re-layouts  154 us (17%)
  starting transfers between devices  94.7 us (11%)
  waiting for transfers between devices  60.7 us (7%)
  other arithmetic  36.3 us (4%)
  matrix products  27.8 us (3%)
    pallas_call x5, Pallas kernels, call(): pl.pallas_call(kernel, out_shape=shapes, in_specs=in_specs or whole_specs...  401 us
    dynamic_update_slice x12, local copies, waits for them, and re-layouts, line_trade(): lax.dynamic_update_slice_in_dim(held, came, lax.rem(at_z + LINE - step, L...  70.4 us
    ppermute x12, starting transfers between devices, line_trade(): lax.ppermute(going, 'z', [(k, (k + step) % LINE) for k in range(LINE)])  34.5 us
    pallas_call x3, Pallas kernels, spread(): pl.pallas_call(spread_kernel, out_shape=(send_shape, keep_shape), in_spec...  30.3 us
    ppermute x3, waiting for transfers between devices, block_device(): lax.ppermute(grad_own, 'z', [(k, (k + LINE - step) % LINE) for k in range...  25.2 us
    dot_general x4, matrix products, product(): lax.dot_general(left_rows, right_rows, (((0,), (0,)), ((), ())), preferre...  24.2 us
    pallas_call x1, Pallas kernels, block_device(): pl.pallas_call(functools.partial(attend_back_kernel, block), out_shape=(q...  24.2 us
    ppermute x3, starting transfers between devices, block_device(): lax.ppermute(grad_own, 'z', [(k, (k + LINE - step) % LINE) for k in range...  23.5 us
  transfers between devices with their start and end apart: 41, of which 9 were waited for; matrix products, arithmetic and copies ran while one was open for 22% of the time, Pallas kernels for 28%

profile of v3, /device:TPU:24, one launch (start us, length us, event | category | flops | bytes accessed | tf_op | source)
XLA Modules:
  0.0 872.2 jit_solution(12723029716748093965)
XLA Ops:
  0.7 4.4 fusion.40
  8.8 147.6 %open.1 = (bf16[1024,2048]{1,0:T(8,128)(2,1)}, f32[128,2048]{1,0:T(8,128)}, bf16[128,2048]{1,0:T(8,128)(2,1)}, f32[4,2048]{1,0:T(4,128)}, f32[2048,128]{1,0:T(8,...) custom-call(s32[2,6]{1,0:T(2,128)} %lengths_ref.1, ...), custom_call_target="tpu_custom_call" | custom-call | tf_op jit(solution)/shard_map/open/pallas_call | solution.py:1512
  156.4 20.2 %collective-permute-start.1 = (bf16[128,2048]{1,0:T(8,128)(2,1)}, bf16[128,2048]{1,0:T(8,128)(2,1)S(1)}, u32[]{:S(2)}, u32[]{:S(2)}) collective-permute-start(bf16[128,2048]{1,0:T(8,128)(2,1)} %get-tuple-element.65.grad_ref), channel_id=1, source_target_pairs={{0,24},{8,0},{16,8},{24,16},{1,25},{9,1},{17,9},{25,17},{2,26},{10... | collective-permute-start | bytes 1572872 | tf_op jit(solution)/shard_map/ppermute | solution.py:1744
  176.6 3.3 collective-permute-start.3
  179.9 2.1 collective-permute-start
  183.1 6.1 collective-permute-done.1
  189.2 11.3 %collective-permute-done.2 = bf16[128,2048]{1,0:T(8,128)(2,1)S(1)} collective-permute-done((bf16[128,2048]{1,0:T(8,128)(2,1)}, bf16[128,2048]{1,0:T(8,128)(2,1)S(1)}, u32[]{:S(2)}, u32[]{:S(2)}) %collective-permute-start.2) | collective-permute-done | bytes 524320 | tf_op jit(solution)/shard_map/ppermute | solution.py:1744
  200.5 7.8 collective-permute-done.3
  208.3 2.5 pad_maximum_fusion
  213.8 26.1 %project.1 = (bf16[3,1024,128]{2,1,0:T(8,128)(2,1)}, bf16[3,1024,128]{2,1,0:T(8,128)(2,1)}) custom-call(bf16[1024,2048]{1,0:T(8,128)(2,1)} %get-tuple-element.51.rows_ref, bf16[2,2,1024,384]{3,2,1,0:T(8,128)(2,1)} %get-tuple-element.52.weight_ref, f32[6,1,128]{2,1,0:T(1,128)} %broadcast_in_dim.24.bias_ref, f32[2048,128]{1,0:T(8,128)} %get-tuple-element.53.cos_ref, ...), custom_call_target="tpu_custom_call" | custom-call | tf_op jit(solution)/shard_map/project/pallas_call | solution.py:1512
  239.9 23.3 %attend.1 = (bf16[1024,128]{1,0:T(8,128)(2,1)}, bf16[1024,128]{1,0:T(8,128)(2,1)}, f32[2,2048]{1,0:T(2,128)}) custom-call(s32[3]{0:T(128)} %pad_add_fusion.place_ref, s32[6]{0:T(128)} %fusion.35.lengths_ref, bf16[3,1024,128]{2,1,0:T(8,128)(2,1)} %get-tuple-element.56.own_ref, bf16[3,1024,128]{2,1,0:T(8,128)(2,1)} %get-tuple-element.57.other_ref), custom_call_target="tpu_custom_call" | custom-call | tf_op jit(solution)/shard_map/attend/pallas_call | solution.py:1750
  263.2 89.0 %middle.1 = (bf16[1024,2048]{1,0:T(8,128)(2,1)}, f32[128,2048]{1,0:T(8,128)}, bf16[2,1024,128]{2,1,0:T(8,128)(2,1)}) custom-call(bf16[1024,128]{1,0:T(8,128)(2,1)} %get-tuple-element.58.own_ref, bf16[1024,128]{1,0:T(8,128)(2,1)} %get-tuple-element.59.going_ref, bf16[2,2,1024,128]{3,2,1,0:T(8,128)(2,1)} %get-tuple-element.60.weight_ref, ...), custom_call_target="tpu_custom_call" | custom-call | tf_op jit(solution)/shard_map/middle/pallas_call | solution.py:1512
  356.8 3.1 constant_dynamic-update-slice_fusion.grad_ref
  359.9 17.9 %feed.1 = (bf16[1024,768]{1,0:T(8,128)(2,1)}, bf16[1024,1536]{1,0:T(8,128)(2,1)}) custom-call(bf16[1024,2048]{1,0:T(8,128)(2,1)} %get-tuple-element.87.low_ref, bf16[1024,2048]{1,0:T(8,128)(2,1)} %constant_dynamic-update-slice_fusion.grad_ref, bf16[2,2,1024,768]{3,2,1,0:T(8,128)(2,1)} %get-tuple-element.66.up_weight.weight_ref, ...), custom_call_target="tpu_custom_call" | custom-call | tf_op jit(solution)/shard_map/feed/pallas_call | solution.py:1786
  377.8 12.4 %spread.3 = (bf16[512,2048]{1,0:T(8,128)(2,1)}, f32[512,2048]{1,0:T(8,128)}) custom-call(bf16[1024,1536]{1,0:T(8,128)(2,1)} %get-tuple-element.88.left_ref, bf16[2,2,1024,768]{3,2,1,0:T(8,128)(2,1)} %get-tuple-element.66.up_weight.weight_ref), custom_call_target="tpu_custom_call" | custom-call | tf_op jit(solution)/shard_map/spread/pallas_call | solution.py:1767
  390.3 73.2 %middle_back.1 = (bf16[1024,2048]{1,0:T(8,128)(2,1)}, f32[128,2048]{1,0:T(8,128)}, f32[8,2048]{1,0:T(8,128)}) custom-call(bf16[512,2048]{1,0:T(8,128)(2,1)} %get-tuple-element.70.send_ref, f32[512,2048]{1,0:T(8,128)} %get-tuple-element.71.keep_ref, f32[128,2048]{1,0:T(8,128)} %get-tuple-element.63.residual_ref, ...), custom_call_target="tpu_custom_call" | custom-call | tf_op jit(solution)/shard_map/middle_back/pallas_call | solution.py:1512
  463.5 3.6 convolution_convert_fusion
  471.6 2.4 collective-permute-start.26
  474.1 2.5 collective-permute-done.14.grad_other
  477.2 24.2 %attend_back.1 = (bf16[3,1024,128]{2,1,0:T(8,128)(2,1)}, bf16[3,1024,128]{2,1,0:T(8,128)(2,1)}, f32[3,128]{1,0:T(4,128)}) custom-call(s32[3]{0:T(128)} %pad_add_fusion.place_ref, s32[6]{0:T(128)} %fusion.35.lengths_ref, bf16[3,1024,128]{2,1,0:T(8,128)(2,1)} %get-tuple-element.56.own_ref, bf16[3,1024,128]{2,1,0:T(8,128)(2,1)} %get-tuple-element.57.other_ref, ...), custom_call_target="tpu_custom_call" | custom-call | tf_op jit(solution)/shard_map/attend_back/pallas_call | solution.py:1828
  503.3 11.4 %fusion.44 = f32[2048,1536]{1,0:T(8,128)} fusion(bf16[1024,2048]{1,0:T(8,128)(2,1)} %get-tuple-element.87.low_ref, bf16[1024,1536]{1,0:T(8,128)(2,1)S(1)} %copy-done.11), kind=kOutput, calls=%fused_computation.148 | convolution fusion | flops 6442450944 | bytes 19922944 | tf_op jit(solution)/shard_map/dot_general | solution.py:1814
  516.3 5.4 fusion.45
  521.8 2.8 collective-permute-start.23
  528.1 9.0 %spread.4 = (bf16[512,2048]{1,0:T(8,128)(2,1)}, f32[512,2048]{1,0:T(8,128)}) custom-call(bf16[1024,768]{1,0:T(8,128)(2,1)} %get-tuple-element.90.left_ref, bf16[2,2,1024,384]{3,2,1,0:T(8,128)(2,1)} %get-tuple-element.67.down_weight.weight_ref), custom_call_target="tpu_custom_call" | custom-call | tf_op jit(solution)/shard_map/spread/pallas_call | solution.py:1767
  537.1 4.8 slice.414
  541.9 3.3 slice.415
  546.2 3.3 collective-permute-start.28
  551.8 2.8 dynamic_update_slice.68
  556.5 2.8 dynamic_update_slice.69
  560.0 2.8 dynamic_update_slice.70
  562.9 2.8 dynamic_update_slice.71
  568.3 8.8 %spread.5 = (bf16[512,2048]{1,0:T(8,128)(2,1)}, f32[512,2048]{1,0:T(8,128)}) custom-call(bf16[1024,768]{1,0:T(8,128)(2,1)} %copy-done.12, bf16[2,2,1024,384]{3,2,1,0:T(8,128)(2,1)} %get-tuple-element.52.weight_ref), custom_call_target="tpu_custom_call" | custom-call | tf_op jit(solution)/shard_map/spread/pallas_call | solution.py:1767
  577.2 65.4 %last.1 = (bf16[2,256,2048]{2,1,0:T(8,128)(2,1)}, f32[8,2048]{1,0:T(8,128)}) custom-call(bf16[512,2048]{1,0:T(8,128)(2,1)} %get-tuple-element.79.send_ref, f32[512,2048]{1,0:T(8,128)} %get-tuple-element.80.keep_ref, f32[128,2048]{1,0:T(8,128)} %get-tuple-element.61.base_ref, f32[128,2048]{1,0:T(8,128)} %get-tuple-element.81.turned_ref, ...), custom_call_target="tpu_custom_call" | custom-call | tf_op jit(solution)/shard_map/last/pallas_call | solution.py:1512
  643.5 6.0 fusion.43
  652.7 1.9 slice_add_fusion.1
  656.3 2.5 convert_add_fusion
  659.0 2.2 collective-permute-start.6
  661.1 12.9 %collective-permute-done.37 = bf16[1024,384]{1,0:T(8,128)(2,1)S(1)} collective-permute-done((bf16[1024,384]{1,0:T(8,128)(2,1)S(1)}, bf16[1024,384]{1,0:T(8,128)(2,1)S(1)}, u32[]{:S(2)}, u32[]{:S(2)}) %collective-permute-start.37) | collective-permute-done | bytes 786464 | tf_op jit(solution)/shard_map/ppermute | solution.py:427
  676.1 5.2 collective-permute-done.38
  681.3 9.4 %collective-permute-start.40 = (bf16[1,256,384]{2,1,0:T(8,128)(2,1)S(1)}, bf16[1,256,384]{2,1,0:T(8,128)(2,1)}, u32[]{:S(2)}, u32[]{:S(2)}) collective-permute-start(bf16[1,256,384]{2,1,0:T(8,128)(2,1)S(1)} %get-tuple-element.126), channel_id=1, source_target_pairs={{0,24},{8,0},{16,8},{24,16},{1,25},{9,1},{17,9},{25,17},{2,26},{10... | collective-permute-start | bytes 589832 | tf_op jit(solution)/shard_map/ppermute | solution.py:1576
  693.7 5.1 dynamic_update_slice.76
  699.1 5.1 dynamic_update_slice.77
  706.1 5.1 dynamic_update_slice.78
  712.5 5.1 dynamic_update_slice.79
  719.0 1.9 collective-permute-start.7
  721.0 2.8 slice_add_fusion.3
  725.5 6.7 collective-permute-done.7
  734.0 6.2 collective-permute-start.8
  740.2 4.7 slice_add_fusion
  746.7 3.3 collective-permute-start.19
  750.0 4.9 collective-permute-start.20
  758.8 5.1 dynamic_update_slice.60
  765.1 5.1 dynamic_update_slice.61
  771.4 5.1 dynamic_update_slice.62
  776.8 5.1 dynamic_update_slice.63
  789.7 2.8 fusion
  793.5 8.3 collective-permute-start.33
  802.0 2.2 collective-permute-start.35
  806.9 10.5 %dynamic_update_slice.72 = bf16[4,256,768]{2,0,1:T(4,128)(2,1)S(1)} dynamic-update-slice(bf16[4,256,768]{2,0,1:T(4,128)(2,1)S(1)} %broadcast_in_dim.31, bf16[1,256,768]{2,0,1:T(2,128)(2,1)S(1)} %copy.71, s32[]{:T(128)S(6)} %select_n.214, s32[]{:T(128)} %constant.84.clone.1, s32[]{:T(128)} %constant.84.clone.1) | dynamic-update-slice | bytes 786436 | tf_op jit(solution)/shard_map/dynamic_update_slice | solution.py:1573
  819.0 10.5 %dynamic_update_slice.73 = bf16[4,256,768]{2,0,1:T(4,128)(2,1)S(1)} dynamic-update-slice(bf16[4,256,768]{2,0,1:T(4,128)(2,1)S(1)} %dynamic_update_slice.72, bf16[1,256,768]{2,0,1:T(2,128)(2,1)S(1)} %copy.72, s32[]{:T(128)S(6)} %select_n.216, s32[]{:T(128)} %constant.84.clone.1, s32[]{:T(128)} %constant.84.clone.1) | dynamic-update-slice | bytes 786436 | tf_op jit(solution)/shard_map/dynamic_update_slice | solution.py:1577
  829.6 7.8 collective-permute-done.34
  839.0 10.5 %dynamic_update_slice.74 = bf16[4,256,768]{2,0,1:T(4,128)(2,1)S(1)} dynamic-update-slice(bf16[4,256,768]{2,0,1:T(4,128)(2,1)S(1)} %dynamic_update_slice.73, bf16[1,256,768]{2,0,1:T(2,128)(2,1)S(1)} %copy.73, s32[]{:T(128)S(6)} %select_n.217, s32[]{:T(128)} %constant.84.clone.1, s32[]{:T(128)} %constant.84.clone.1) | dynamic-update-slice | bytes 786436 | tf_op jit(solution)/shard_map/dynamic_update_slice | solution.py:1577
  851.2 10.5 %dynamic_update_slice.75 = bf16[4,256,768]{2,0,1:T(4,128)(2,1)S(1)} dynamic-update-slice(bf16[4,256,768]{2,0,1:T(4,128)(2,1)S(1)} %dynamic_update_slice.74, bf16[1,256,768]{2,0,1:T(2,128)(2,1)S(1)} %copy.74, s32[]{:T(128)S(6)} %select_n.215, s32[]{:T(128)} %constant.84.clone.1, s32[]{:T(128)} %constant.84.clone.1) | dynamic-update-slice | bytes 786436 | tf_op jit(solution)/shard_map/dynamic_update_slice | solution.py:1577
  862.8 3.8 copy.79
  (253 shorter events, 83.7 us)
Async XLA Ops:
  0.6 179.3 %copy-start = (f32[3,512]{1,0:T(4,128)S(1)}, f32[3,512]{1,0:T(4,128)}, u32[]{:S(2)}) copy-start(f32[3,512]{1,0:T(4,128)} %param.17) | copy-start | bytes 18436
  8.8 173.2 %copy-start.35 = (s32[2,6]{1,0:T(2,128)S(1)}, s32[2,6]{1,0:T(2,128)}, u32[]{:S(2)}) copy-start(s32[2,6]{1,0:T(2,128)} %lengths_ref.1) | copy-start | bytes 148
  156.4 32.8 %collective-permute-start.1 = (bf16[128,2048]{1,0:T(8,128)(2,1)}, bf16[128,2048]{1,0:T(8,128)(2,1)S(1)}, u32[]{:S(2)}, u32[]{:S(2)}) collective-permute-start(bf16[128,2048]{1,0:T(8,128)(2,1)} %get-tuple-element.65.grad_ref), channel_id=1, source_target_pairs={{0,24},{8,0},{16,8},{24,16},{1,25},{9,1},{17,9},{25,17},{2,26},{10... | collective-permute-start | bytes 1572872 | tf_op jit(solution)/shard_map/ppermute | solution.py:1744
  176.5 23.9 %collective-permute-start.2 = (bf16[128,2048]{1,0:T(8,128)(2,1)}, bf16[128,2048]{1,0:T(8,128)(2,1)S(1)}, u32[]{:S(2)}, u32[]{:S(2)}) collective-permute-start(bf16[128,2048]{1,0:T(8,128)(2,1)} %get-tuple-element.65.grad_ref), channel_id=1, source_target_pairs={{0,16},{8,24},{16,0},{24,8},{1,17},{9,25},{17,1},{25,9},{2,18},{10... | collective-permute-start | bytes 1572872 | tf_op jit(solution)/shard_map/ppermute | solution.py:1744
  176.6 31.7 %collective-permute-start.3 = (bf16[128,2048]{1,0:T(8,128)(2,1)}, bf16[128,2048]{1,0:T(8,128)(2,1)S(1)}, u32[]{:S(2)}, u32[]{:S(2)}) collective-permute-start(bf16[128,2048]{1,0:T(8,128)(2,1)} %get-tuple-element.65.grad_ref), channel_id=1, source_target_pairs={{0,8},{8,16},{16,24},{24,0},{1,9},{9,17},{17,25},{25,1},{2,10},{10... | collective-permute-start | bytes 1572872 | tf_op jit(solution)/shard_map/ppermute | solution.py:1744
  179.9 33.3 %collective-permute-start = (f32[3,128]{1,0:T(4,128)S(1)}, f32[3,128]{1,0:T(4,128)S(1)}, u32[]{:S(2)}, u32[]{:S(2)}) collective-permute-start(f32[3,128]{1,0:T(4,128)S(1)} %constant_dynamic-slice_fusion.16), channel_id=1, source_target_pairs={{0,2},{2,0},{1,3},{3,1},{4,6},{6,4},{5,7},{7,5},{8,10},{10,8},{9,1... | collective-permute-start | bytes 4616 | tf_op jit(solution)/shard_map/ppermute | solution.py:427
  183.1 27.7 %copy-start.6 = (bf16[128,2048]{1,0:T(8,128)(2,1)S(1)}, bf16[128,2048]{1,0:T(8,128)(2,1)}, u32[]{:S(2)}) copy-start(bf16[128,2048]{1,0:T(8,128)(2,1)} %get-tuple-element.65.grad_ref) | copy-start | bytes 1572868
  183.1 28.6 %copy-start.9 = (bf16[2,2,1024,128]{3,2,1,0:T(8,128)(2,1)S(1)}, bf16[2,2,1024,128]{3,2,1,0:T(8,128)(2,1)}, u32[]{:S(2)}) copy-start(bf16[2,2,1024,128]{3,2,1,0:T(8,128)(2,1)} %get-tuple-element.60.weight_ref) | copy-start | bytes 3145732
  210.8 145.9 %collective-permute-start.4 = (bf16[512,2048]{1,0:T(8,128)(2,1)}, bf16[512,2048]{1,0:T(8,128)(2,1)}, u32[]{:S(2)}, u32[]{:S(2)}) collective-permute-start(bf16[512,2048]{1,0:T(8,128)(2,1)} %pad_maximum_fusion), channel_id=1, source_target_pairs={{0,1},{1,0},{2,3},{3,2},{4,5},{5,4},{6,7},{7,6},{8,9},{9,8},{10,11... | collective-permute-start | bytes 6291464 | tf_op jit(solution)/shard_map/ppermute | solution.py:427
  263.2 89.0 %copy-start.17 = (bf16[1024,128]{1,0:T(8,128)(2,1)S(1)}, bf16[1024,128]{1,0:T(8,128)(2,1)}, u32[]{:S(2)}) copy-start(bf16[1024,128]{1,0:T(8,128)(2,1)} %get-tuple-element.58.own_ref) | copy-start | bytes 786436
  263.2 89.0 %copy-start.18 = (bf16[1024,128]{1,0:T(8,128)(2,1)S(1)}, bf16[1024,128]{1,0:T(8,128)(2,1)}, u32[]{:S(2)}) copy-start(bf16[1024,128]{1,0:T(8,128)(2,1)} %get-tuple-element.59.going_ref) | copy-start | bytes 786436
  390.3 73.2 %copy-start.22 = (bf16[1024,128]{1,0:T(8,128)(2,1)S(1)}, bf16[1024,128]{1,0:T(8,128)(2,1)}, u32[]{:S(2)}) copy-start(bf16[1024,128]{1,0:T(8,128)(2,1)} %get-tuple-element.121) | copy-start | bytes 786436
  390.3 73.2 %copy-start.23 = (bf16[1024,128]{1,0:T(8,128)(2,1)S(1)}, bf16[1024,128]{1,0:T(8,128)(2,1)}, u32[]{:S(2)}) copy-start(bf16[1024,128]{1,0:T(8,128)(2,1)} %get-tuple-element.122) | copy-start | bytes 786436
  390.3 73.2 %copy-start.24 = (bf16[1024,128]{1,0:T(8,128)(2,1)S(1)}, bf16[1024,128]{1,0:T(8,128)(2,1)}, u32[]{:S(2)}) copy-start(bf16[1024,128]{1,0:T(8,128)(2,1)} %get-tuple-element.123) | copy-start | bytes 786436
  463.5 5.8 copy-start.36
  467.9 8.7 collective-permute-start.14
  471.6 52.9 %collective-permute-start.26 = (bf16[2048,128]{1,0:T(8,128)(2,1)}, bf16[2048,128]{1,0:T(8,128)(2,1)}, u32[]{:S(2)}, u32[]{:S(2)}) collective-permute-start(bf16[2048,128]{1,0:T(8,128)(2,1)} %slice.420), channel_id=1, source_target_pairs={{0,2},{2,0},{1,3},{3,1},{4,6},{6,4},{5,7},{7,5},{8,10},{10,8},{9,1... | collective-permute-start | bytes 1572872 | tf_op jit(solution)/shard_map/ppermute | solution.py:427
  477.2 26.1 %copy-start.11 = (bf16[1024,1536]{1,0:T(8,128)(2,1)S(1)}, bf16[1024,1536]{1,0:T(8,128)(2,1)}, u32[]{:S(2)}) copy-start(bf16[1024,1536]{1,0:T(8,128)(2,1)} %get-tuple-element.88.left_ref) | copy-start | bytes 9437188
  501.5 13.3 %copy-start.34 = (f32[3,128]{1,0:T(4,128)S(1)}, f32[3,128]{1,0:T(4,128)}, u32[]{:S(2)}) copy-start(f32[3,128]{1,0:T(4,128)} %get-tuple-element.85) | copy-start | bytes 4612
  501.5 14.9 %copy-start.5 = (bf16[1024,2048]{1,0:T(8,128)(2,1)S(1)}, bf16[1024,2048]{1,0:T(8,128)(2,1)}, u32[]{:S(2)}) copy-start(bf16[1024,2048]{1,0:T(8,128)(2,1)} %constant_dynamic-update-slice_fusion.grad_ref) | copy-start | bytes 12582916
  501.5 14.8 %copy-start.14 = (bf16[1024,768]{1,0:T(8,128)(2,1)S(1)}, bf16[1024,768]{1,0:T(8,128)(2,1)}, u32[]{:S(2)}) copy-start(bf16[1024,768]{1,0:T(8,128)(2,1)} %get-tuple-element.90.left_ref) | copy-start | bytes 4718596
  501.5 13.3 %collective-permute-start.21 = (f32[3,128]{1,0:T(4,128)}, f32[3,128]{1,0:T(4,128)S(1)}, u32[]{:S(2)}, u32[]{:S(2)}) collective-permute-start(f32[3,128]{1,0:T(4,128)} %get-tuple-element.85), channel_id=1, source_target_pairs={{0,2},{2,0},{1,3},{3,1},{4,6},{6,4},{5,7},{7,5},{8,10},{10,8},{9,1... | collective-permute-start | bytes 4616 | tf_op jit(solution)/shard_map/ppermute | solution.py:427
  514.8 7.0 copy-start.28
  514.8 9.8 %copy-start.16 = (f32[2048,256]{1,0:T(8,128)S(1)}, f32[2048,256]{1,0:T(8,128)}, u32[]{:S(2)}) copy-start(f32[2048,256]{1,0:T(8,128)} %copy-done.15) | copy-start | bytes 6291460
  514.8 7.0 collective-permute-start.22
  521.8 24.3 %collective-permute-start.23 = (f32[3,128]{1,0:T(4,128)S(1)}, f32[3,128]{1,0:T(4,128)S(1)}, u32[]{:S(2)}, u32[]{:S(2)}) collective-permute-start(f32[3,128]{1,0:T(4,128)S(1)} %get-tuple-element.103), channel_id=1, source_target_pairs={{0,8},{8,16},{16,24},{24,0},{1,9},{9,17},{17,25},{25,1},{2,10},{10... | collective-permute-start | bytes 4616 | tf_op jit(solution)/shard_map/ppermute | solution.py:1895
  525.8 20.4 %collective-permute-start.27 = (bf16[1024,128]{1,0:T(8,128)(2,1)S(1)}, bf16[1024,128]{1,0:T(8,128)(2,1)S(1)}, u32[]{:S(2)}, u32[]{:S(2)}) collective-permute-start(bf16[1024,128]{1,0:T(8,128)(2,1)S(1)} %slice.423), channel_id=1, source_target_pairs={{0,4},{4,0},{1,5},{5,1},{2,6},{6,2},{3,7},{7,3},{8,12},{12,8},{9,1... | collective-permute-start | bytes 786440 | tf_op jit(solution)/shard_map/ppermute | solution.py:427
  545.1 21.5 %collective-permute-start.15 = (bf16[3,1024,128]{2,1,0:T(8,128)(2,1)S(1)}, bf16[3,1024,128]{2,1,0:T(8,128)(2,1)S(1)}, u32[]{:S(2)}, u32[]{:S(2)}) collective-permute-start(bf16[3,1024,128]{2,1,0:T(8,128)(2,1)S(1)} %copy-done.37), channel_id=1, source_target_pairs={{0,4},{4,0},{1,5},{5,1},{2,6},{6,2},{3,7},{7,3},{8,12},{12,8},{9,1... | collective-permute-start | bytes 2359304 | tf_op jit(solution)/shard_map/ppermute | solution.py:427
  545.5 5.1 collective-permute-start.24
  545.5 5.4 collective-permute-start.25
  546.2 20.4 %copy-start.19 = (bf16[3,1024,128]{2,1,0:T(8,128)(2,1)S(1)}, bf16[3,1024,128]{2,1,0:T(8,128)(2,1)}, u32[]{:S(2)}) copy-start(bf16[3,1024,128]{2,1,0:T(8,128)(2,1)} %get-tuple-element.77) | copy-start | bytes 2359300
  546.2 8.3 collective-permute-start.28
  549.5 9.8 %collective-permute-start.29 = (bf16[1,256,128]{2,1,0:T(8,128)(2,1)S(1)}, bf16[1,256,128]{2,1,0:T(8,128)(2,1)S(1)}, u32[]{:S(2)}, u32[]{:S(2)}) collective-permute-start(bf16[1,256,128]{2,1,0:T(8,128)(2,1)S(1)} %get-tuple-element.142), channel_id=1, source_target_pairs={{0,16},{8,24},{16,0},{24,8},{1,17},{9,25},{17,1},{25,9},{2,18},{10... | collective-permute-start | bytes 196616 | tf_op jit(solution)/shard_map/ppermute | solution.py:1576
  550.7 12.2 %collective-permute-start.30 = (bf16[1,256,128]{2,1,0:T(8,128)(2,1)S(1)}, bf16[1,256,128]{2,1,0:T(8,128)(2,1)S(1)}, u32[]{:S(2)}, u32[]{:S(2)}) collective-permute-start(bf16[1,256,128]{2,1,0:T(8,128)(2,1)S(1)} %get-tuple-element.141), channel_id=1, source_target_pairs={{0,24},{8,0},{16,8},{24,16},{1,25},{9,1},{17,9},{25,17},{2,26},{10... | collective-permute-start | bytes 196616 | tf_op jit(solution)/shard_map/ppermute | solution.py:1576
  550.9 105.4 %collective-permute-start.5 = (bf16[512,2048]{1,0:T(8,128)(2,1)}, bf16[512,2048]{1,0:T(8,128)(2,1)}, u32[]{:S(2)}, u32[]{:S(2)}) collective-permute-start(bf16[512,2048]{1,0:T(8,128)(2,1)} %get-tuple-element.75), channel_id=1, source_target_pairs={{0,1},{1,0},{2,3},{3,2},{4,5},{5,4},{6,7},{7,6},{8,9},{9,8},{10,11... | collective-permute-start | bytes 6291464 | tf_op jit(solution)/shard_map/ppermute | solution.py:427
  554.6 185.6 %collective-permute-start.31 = (bf16[1024,1536]{1,0:T(8,128)(2,1)}, bf16[1024,1536]{1,0:T(8,128)(2,1)}, u32[]{:S(2)}, u32[]{:S(2)}) collective-permute-start(bf16[1024,1536]{1,0:T(8,128)(2,1)} %slice.414), channel_id=1, source_target_pairs={{0,4},{4,0},{1,5},{5,1},{2,6},{6,2},{3,7},{7,3},{8,12},{12,8},{9,1... | collective-permute-start | bytes 9437192 | tf_op jit(solution)/shard_map/ppermute | solution.py:427
  559.3 93.3 %collective-permute-start.36 = (bf16[2048,384]{1,0:T(8,128)(2,1)}, bf16[2048,384]{1,0:T(8,128)(2,1)}, u32[]{:S(2)}, u32[]{:S(2)}) collective-permute-start(bf16[2048,384]{1,0:T(8,128)(2,1)} %slice.415), channel_id=1, source_target_pairs={{0,2},{2,0},{1,3},{3,1},{4,6},{6,4},{5,7},{7,5},{8,10},{10,8},{9,1... | collective-permute-start | bytes 4718600 | tf_op jit(solution)/shard_map/ppermute | solution.py:427
  643.4 9.2 %slice-start = ((s8[6291456]{0:T(1024)(128)(4,1)}), s8[2097152]{0:T(1024)(128)(4,1)S(1)}, s32[]{:S(2)}) async-start(s8[6291456]{0:T(1024)(128)(4,1)} %bitcast.142), calls=%async_computation | async-start | bytes 4194304
  643.4 9.2 %slice-start.1 = ((s8[6291456]{0:T(1024)(128)(4,1)}), s8[4194304]{0:T(1024)(128)(4,1)S(1)}, s32[]{:S(2)}) async-start(s8[6291456]{0:T(1024)(128)(4,1)} %bitcast.142), calls=%async_computation.1 | async-start | bytes 8388608
  651.0 70.0 %collective-permute-start.16 = (bf16[2048,384]{1,0:T(8,128)(2,1)}, bf16[2048,384]{1,0:T(8,128)(2,1)}, u32[]{:S(2)}, u32[]{:S(2)}) collective-permute-start(bf16[2048,384]{1,0:T(8,128)(2,1)} %slice.417), channel_id=1, source_target_pairs={{0,2},{2,0},{1,3},{3,1},{4,6},{6,4},{5,7},{7,5},{8,10},{10,8},{9,1... | collective-permute-start | bytes 4718600 | tf_op jit(solution)/shard_map/ppermute | solution.py:427
  654.7 19.4 %collective-permute-start.37 = (bf16[1024,384]{1,0:T(8,128)(2,1)S(1)}, bf16[1024,384]{1,0:T(8,128)(2,1)S(1)}, u32[]{:S(2)}, u32[]{:S(2)}) collective-permute-start(bf16[1024,384]{1,0:T(8,128)(2,1)S(1)} %slice.418), channel_id=1, source_target_pairs={{0,4},{4,0},{1,5},{5,1},{2,6},{6,2},{3,7},{7,3},{8,12},{12,8},{9,1... | collective-permute-start | bytes 2359304 | tf_op jit(solution)/shard_map/ppermute | solution.py:427
  658.8 15.4 %copy-start.2 = (f32[512,2048]{1,0:T(8,128)}, f32[512,2048]{1,0:T(8,128)S(1)}, u32[]{:S(2)}) copy-start(f32[512,2048]{1,0:T(8,128)S(1)} %convert_add_fusion) | copy-start | bytes 12582916
  659.0 58.7 %collective-permute-start.6 = (bf16[128,2048]{1,0:T(8,128)(2,1)S(1)}, bf16[128,2048]{1,0:T(8,128)(2,1)S(1)}, u32[]{:S(2)}, u32[]{:S(2)}) collective-permute-start(bf16[128,2048]{1,0:T(8,128)(2,1)S(1)} %get-tuple-element.106), channel_id=1, source_target_pairs={{24,16},{25,17},{26,18},{27,19},{28,20},{29,21},{30,22},{31,23}} | collective-permute-start | bytes 1572872 | tf_op jit(solution)/shard_map/ppermute | solution.py:1561
  674.3 7.0 collective-permute-start.38
  675.4 28.8 %collective-permute-start.39 = (bf16[1,256,384]{2,1,0:T(8,128)(2,1)S(1)}, bf16[1,256,384]{2,1,0:T(8,128)(2,1)}, u32[]{:S(2)}, u32[]{:S(2)}) collective-permute-start(bf16[1,256,384]{2,1,0:T(8,128)(2,1)S(1)} %get-tuple-element.127), channel_id=1, source_target_pairs={{0,16},{8,24},{16,0},{24,8},{1,17},{9,25},{17,1},{25,9},{2,18},{10... | collective-permute-start | bytes 589832 | tf_op jit(solution)/shard_map/ppermute | solution.py:1576
  681.3 11.9 %copy-start.25 = (bf16[1,256,384]{2,1,0:T(8,128)(2,1)}, bf16[1,256,384]{2,1,0:T(8,128)(2,1)S(1)}, u32[]{:S(2)}) copy-start(bf16[1,256,384]{2,1,0:T(8,128)(2,1)S(1)} %collective-permute-done.38) | copy-start | bytes 589828
  681.3 29.9 %collective-permute-start.40 = (bf16[1,256,384]{2,1,0:T(8,128)(2,1)S(1)}, bf16[1,256,384]{2,1,0:T(8,128)(2,1)}, u32[]{:S(2)}, u32[]{:S(2)}) collective-permute-start(bf16[1,256,384]{2,1,0:T(8,128)(2,1)S(1)} %get-tuple-element.126), channel_id=1, source_target_pairs={{0,24},{8,0},{16,8},{24,16},{1,25},{9,1},{17,9},{25,17},{2,26},{10... | collective-permute-start | bytes 589832 | tf_op jit(solution)/shard_map/ppermute | solution.py:1576
  704.2 21.3 %collective-permute-start.9 = (bf16[128,2048]{1,0:T(8,128)(2,1)S(1)}, bf16[128,2048]{1,0:T(8,128)(2,1)S(1)}, u32[]{:S(2)}, u32[]{:S(2)}) collective-permute-start(bf16[128,2048]{1,0:T(8,128)(2,1)S(1)} %get-tuple-element.107), channel_id=1, source_target_pairs={{0,8},{1,9},{2,10},{3,11},{4,12},{5,13},{6,14},{7,15}} | collective-permute-start | bytes 1572872 | tf_op jit(solution)/shard_map/ppermute | solution.py:1564
  719.0 13.2 %collective-permute-start.7 = (bf16[128,2048]{1,0:T(8,128)(2,1)S(1)}, bf16[128,2048]{1,0:T(8,128)(2,1)S(1)}, u32[]{:S(2)}, u32[]{:S(2)}) collective-permute-start(bf16[128,2048]{1,0:T(8,128)(2,1)S(1)} %add_convert_fusion.3), channel_id=1, source_target_pairs={{16,8},{24,16},{17,9},{25,17},{18,10},{26,18},{19,11},{27,19},{20,... | collective-permute-start | bytes 1572872 | tf_op jit(solution)/shard_map/ppermute | solution.py:1561
  721.0 11.3 %copy-start.3 = (f32[512,2048]{1,0:T(8,128)S(1)}, f32[512,2048]{1,0:T(8,128)}, u32[]{:S(2)}) copy-start(f32[512,2048]{1,0:T(8,128)} %copy-done.2) | copy-start | bytes 12582916
  723.8 22.5 %collective-permute-start.17 = (bf16[1024,384]{1,0:T(8,128)(2,1)S(1)}, bf16[1024,384]{1,0:T(8,128)(2,1)S(1)}, u32[]{:S(2)}, u32[]{:S(2)}) collective-permute-start(bf16[1024,384]{1,0:T(8,128)(2,1)S(1)} %slice.419), channel_id=1, source_target_pairs={{0,4},{4,0},{1,5},{5,1},{2,6},{6,2},{3,7},{7,3},{8,12},{12,8},{9,1... | collective-permute-start | bytes 2359304 | tf_op jit(solution)/shard_map/ppermute | solution.py:427
  733.3 16.7 %collective-permute-start.10 = (bf16[128,2048]{1,0:T(8,128)(2,1)S(1)}, bf16[128,2048]{1,0:T(8,128)(2,1)S(1)}, u32[]{:S(2)}, u32[]{:S(2)}) collective-permute-start(bf16[128,2048]{1,0:T(8,128)(2,1)S(1)} %get-tuple-element.105), channel_id=1, source_target_pairs={{0,8},{8,16},{1,9},{9,17},{2,10},{10,18},{3,11},{11,19},{4,12},{12... | collective-permute-start | bytes 1572872 | tf_op jit(solution)/shard_map/ppermute | solution.py:1564
  734.0 51.5 %collective-permute-start.8 = (bf16[128,2048]{1,0:T(8,128)(2,1)}, bf16[128,2048]{1,0:T(8,128)(2,1)}, u32[]{:S(2)}, u32[]{:S(2)}) collective-permute-start(bf16[128,2048]{1,0:T(8,128)(2,1)} %get-tuple-element.104), channel_id=1, source_target_pairs={{8,0},{16,8},{24,16},{9,1},{17,9},{25,17},{10,2},{18,10},{26,18},{... | collective-permute-start | bytes 1572872 | tf_op jit(solution)/shard_map/ppermute | solution.py:1561
  744.9 13.7 %copy-start.4 = (f32[1024,1536]{1,0:T(8,128)}, f32[1024,1536]{1,0:T(8,128)S(1)}, u32[]{:S(2)}) copy-start(f32[1024,1536]{1,0:T(8,128)S(1)} %slice_add_fusion) | copy-start | bytes 18874372
  745.1 44.6 %collective-permute-start.32 = (bf16[1024,768]{1,0:T(8,128)(2,1)S(1)}, bf16[1024,768]{1,0:T(8,128)(2,1)}, u32[]{:S(2)}, u32[]{:S(2)}) collective-permute-start(bf16[1024,768]{1,0:T(8,128)(2,1)S(1)} %slice.416), channel_id=1, source_target_pairs={{0,2},{2,0},{1,3},{3,1},{4,6},{6,4},{5,7},{7,5},{8,10},{10,8},{9,1... | collective-permute-start | bytes 4718600 | tf_op jit(solution)/shard_map/ppermute | solution.py:427
  746.6 9.1 %collective-permute-start.18 = (bf16[1,256,384]{2,1,0:T(8,128)(2,1)S(1)}, bf16[1,256,384]{2,1,0:T(8,128)(2,1)S(1)}, u32[]{:S(2)}, u32[]{:S(2)}) collective-permute-start(bf16[1,256,384]{2,1,0:T(8,128)(2,1)S(1)} %get-tuple-element.135), channel_id=1, source_target_pairs={{0,8},{8,16},{16,24},{24,0},{1,9},{9,17},{17,25},{25,1},{2,10},{10... | collective-permute-start | bytes 589832 | tf_op jit(solution)/shard_map/ppermute | solution.py:1576
  746.7 23.5 %collective-permute-start.19 = (bf16[1,256,384]{2,1,0:T(8,128)(2,1)S(1)}, bf16[1,256,384]{2,1,0:T(8,128)(2,1)}, u32[]{:S(2)}, u32[]{:S(2)}) collective-permute-start(bf16[1,256,384]{2,1,0:T(8,128)(2,1)S(1)} %get-tuple-element.134), channel_id=1, source_target_pairs={{0,16},{8,24},{16,0},{24,8},{1,17},{9,25},{17,1},{25,9},{2,18},{10... | collective-permute-start | bytes 589832 | tf_op jit(solution)/shard_map/ppermute | solution.py:1576
  750.0 26.5 %collective-permute-start.20 = (bf16[1,256,384]{2,1,0:T(8,128)(2,1)S(1)}, bf16[1,256,384]{2,1,0:T(8,128)(2,1)S(1)}, u32[]{:S(2)}, u32[]{:S(2)}) collective-permute-start(bf16[1,256,384]{2,1,0:T(8,128)(2,1)S(1)} %get-tuple-element.133), channel_id=1, source_target_pairs={{0,24},{8,0},{16,8},{24,16},{1,25},{9,1},{17,9},{25,17},{2,26},{10... | collective-permute-start | bytes 589832 | tf_op jit(solution)/shard_map/ppermute | solution.py:1576
  755.8 29.7 %collective-permute-start.11 = (bf16[128,2048]{1,0:T(8,128)(2,1)}, bf16[128,2048]{1,0:T(8,128)(2,1)}, u32[]{:S(2)}, u32[]{:S(2)}) collective-permute-start(bf16[128,2048]{1,0:T(8,128)(2,1)} %add_convert_fusion), channel_id=1, source_target_pairs={{0,8},{8,16},{16,24},{1,9},{9,17},{17,25},{2,10},{10,18},{18,26},{... | collective-permute-start | bytes 1572872 | tf_op jit(solution)/shard_map/ppermute | solution.py:1564
  789.6 14.6 %collective-permute-start.12 = (bf16[128,2048]{1,0:T(8,128)(2,1)S(1)}, bf16[128,2048]{1,0:T(8,128)(2,1)S(1)}, u32[]{:S(2)}, u32[]{:S(2)}) collective-permute-start(bf16[128,2048]{1,0:T(8,128)(2,1)S(1)} %convert_element_type.163), channel_id=1, source_target_pairs={{0,1},{1,0},{2,3},{3,2},{4,5},{5,4},{6,7},{7,6},{8,9},{9,8},{10,11... | collective-permute-start | bytes 1572872 | tf_op jit(solution)/shard_map/ppermute | solution.py:427
  793.5 23.9 %collective-permute-start.33 = (bf16[1,256,768]{2,1,0:T(8,128)(2,1)}, bf16[1,256,768]{2,1,0:T(8,128)(2,1)}, u32[]{:S(2)}, u32[]{:S(2)}) collective-permute-start(bf16[1,256,768]{2,1,0:T(8,128)(2,1)} %get-tuple-element.114), channel_id=1, source_target_pairs={{0,8},{8,16},{16,24},{24,0},{1,9},{9,17},{17,25},{25,1},{2,10},{10... | collective-permute-start | bytes 1179656 | tf_op jit(solution)/shard_map/ppermute | solution.py:1576
  801.8 35.6 %collective-permute-start.34 = (bf16[1,256,768]{2,1,0:T(8,128)(2,1)}, bf16[1,256,768]{2,1,0:T(8,128)(2,1)}, u32[]{:S(2)}, u32[]{:S(2)}) collective-permute-start(bf16[1,256,768]{2,1,0:T(8,128)(2,1)} %get-tuple-element.113), channel_id=1, source_target_pairs={{0,16},{8,24},{16,0},{24,8},{1,17},{9,25},{17,1},{25,9},{2,18},{10... | collective-permute-start | bytes 1179656 | tf_op jit(solution)/shard_map/ppermute | solution.py:1576
  802.0 47.5 %collective-permute-start.35 = (bf16[1,256,768]{2,1,0:T(8,128)(2,1)}, bf16[1,256,768]{2,1,0:T(8,128)(2,1)}, u32[]{:S(2)}, u32[]{:S(2)}) collective-permute-start(bf16[1,256,768]{2,1,0:T(8,128)(2,1)} %get-tuple-element.112), channel_id=1, source_target_pairs={{0,24},{8,0},{16,8},{24,16},{1,25},{9,1},{17,9},{25,17},{2,26},{10... | collective-permute-start | bytes 1179656 | tf_op jit(solution)/shard_map/ppermute | solution.py:1576
  805.3 61.3 %collective-permute-start.13 = (bf16[256,2048]{1,0:T(8,128)(2,1)}, bf16[256,2048]{1,0:T(8,128)(2,1)}, u32[]{:S(2)}, u32[]{:S(2)}) collective-permute-start(bf16[256,2048]{1,0:T(8,128)(2,1)} %pad_maximum_fusion.2), channel_id=1, source_target_pairs={{0,2},{2,0},{1,3},{3,1},{4,6},{6,4},{5,7},{7,5},{8,10},{10,8},{9,1... | collective-permute-start | bytes 3145736 | tf_op jit(solution)/shard_map/ppermute | solution.py:427
  (17 other events, 48.4 us)
